TPU v7x, 256 devices: a whole 4x4x8 slice. The times are simulated.
256 devices in a mesh: seq: 32 (over z, x), tensor: 8 (over y, core).
Axes of the slice: x: 4, y: 4, z: 8, core: 2. Of those that a mesh axis runs over, the one named last changes fastest.
Arguments:
- hidden_in: bfloat16 [16, 5120], replicated, may hold values from -6 to 6
- united_down: bfloat16 [5120, 2112], P(None, 'tensor'), may hold values from -0.078125 to 0.078125
- q_gain: float32 [1536], replicated, may hold values from 0.1 to 1.9
- kv_gain: float32 [512], replicated, may hold values from 0.1 to 1.9
- q_up: bfloat16 [1536, 24576], P('seq', 'tensor'), may hold values from -0.15625 to 0.15625
- key_up: bfloat16 [512, 16384], P(None, 'tensor'), may hold values from -0.25 to 0.25
- value_up: bfloat16 [512, 16384], P(None, 'tensor'), may hold values from -0.0625 to 0.0625
- latent_block_store: bfloat16 [2048, 128, 512], P(('seq', 'tensor')), may hold values from -24 to 24
- rope_pool: bfloat16 [2048, 64, 128], P(('seq', 'tensor')), may hold values from -124 to 124
- lengths: int32 [16], replicated, may hold values from 8192 to 16384, as said below
- block_table: int32 [16, 128], P(None, 'seq'), may hold values from 0 to 2047, as said below
Outputs:
- attn_out: bfloat16 [16, 16384], P(None, 'tensor')
- new_entry: bfloat16 [16, 576], replicated
Inputs may be any that keep to these rules, and one draw needn't show every extreme that they name: `lengths`: every sequence holds 8192 to 16384 cached positions; one sequence holds exactly 16384 and another exactly 8192. block_table[b, j] is the pool slot of positions j * 128 to (j + 1) * 128 - 1 of sequence b. The columns j with j // 4 = s name exactly the 64 slots s * 16 * 4 to (s + 1) * 16 * 4 - 1, each once, in any order; blocks past a sequence's length also name such slots.
All inputs are finite; a program needn't handle non-finite values.
Results may differ from a plain program's by a relative error of at most 0.015.
The roundings to bfloat16 on the way count: a program that leaves them out, or rounds other values in their place, can miss the bound.
Values may be sent and summed in bfloat16 or wider, within the bound.
No kernel may reach another device: no remote copies, remote signals or barrier semaphores. Data moves between devices by JAX's collectives and lax.ppermute only.
A program may use at most 128 MiB of HBM per device.

v0:
```python
import jax
import jax.numpy as jnp
from jax import lax
from jax.experimental import pallas as pl
from jax.experimental.pallas import tpu as pltpu
from jax.sharding import Mesh
from jax.sharding import PartitionSpec as P


D = 5120
QR = 1536
LR = 512
ROT = 64
VD = 128
B = 16
BP = 128
QH = 192
SCALE = QH ** (-0.5)
FLOOR = -1e30
S = ("z", "x")
T = ("y", "c")
bf16 = jnp.bfloat16
f32 = jnp.float32
VM = pltpu.MemorySpace.VMEM
SM = pltpu.MemorySpace.SMEM
HB = pltpu.MemorySpace.HBM


def spec(space):
    return pl.BlockSpec(memory_space=space)


def exchange(pieces, axes):
    return lax.all_to_all(pieces, axes, split_axis=0, concat_axis=0, tiled=True)


UK = 5


def united_kernel(hid, wt, lat, rope, out, pack_a, pack_b, wbuf, cache, ropes, wsem, psem):
    step = D // UK
    copies = []
    for k in range(UK):
        cp = pltpu.make_async_copy(wt.at[:, pl.ds(k * step, step)], wbuf.at[k], wsem.at[k])
        cp.start()
        copies.append(cp)
    fetch_rope = pltpu.make_async_copy(rope, ropes, psem.at[0])
    fetch_rope.start()
    fetch_lat = pltpu.make_async_copy(lat, cache.at[:, pl.ds(0, BP), :], psem.at[1])
    fetch_lat.start()
    acc = jnp.zeros((B, out.shape[2]), f32)
    for k in range(UK):
        copies[k].wait()
        acc = acc + lax.dot_general(
            hid[:, k * step : (k + 1) * step],
            wbuf[k],
            (((1,), (1,)), ((), ())),
            preferred_element_type=f32,
        )
    fetch_rope.wait()
    for n in range(8):
        for g in range(4):
            cache[n, BP:, 128 * g : 128 * g + 128] = ropes[n, 16 * g : 16 * g + 16, :]
    fetch_lat.wait()
    stores = []
    for h, dst in enumerate((pack_a, pack_b)):
        st = pltpu.make_async_copy(cache.at[pl.ds(4 * h, 4)], dst, psem.at[2 + h])
        st.start()
        stores.append(st)
    val = acc.astype(bf16)
    for i in range(out.shape[0]):
        out[i] = val
    for st in stores:
        st.wait()


def united_call(hid, down, lat, rope):
    cols = down.shape[1]
    half = jax.ShapeDtypeStruct((4, BP + 16, LR), bf16)
    return pl.pallas_call(
        united_kernel,
        out_shape=(jax.ShapeDtypeStruct((8, B, cols), bf16), half, half),
        in_specs=[spec(VM), spec(HB), spec(HB), spec(HB)],
        out_specs=(spec(VM), spec(HB), spec(HB)),
        scratch_shapes=[
            pltpu.VMEM((UK, cols, D // UK), bf16),
            pltpu.VMEM((8, BP + 16, LR), bf16),
            pltpu.VMEM((8, ROT, BP), bf16),
            pltpu.SemaphoreType.DMA((UK,)),
            pltpu.SemaphoreType.DMA((4,)),
        ],
        name="united",
    )(hid, down.T, lat, rope)


def rotated(x, cs):
    lane = lax.broadcasted_iota(jnp.int32, x.shape, 1)
    swapped = jnp.where(lane < 32, pltpu.roll(x, 96, 1), pltpu.roll(x, 32, 1))
    return x * cs + swapped * pltpu.roll(cs, 64, 1)


def query_kernel(idx, parts, q_gain, kv_gain, cs, q_up, entry, wide, out, ql):
    s = idx[0]
    width = 264
    tiles = [None] * 17
    for i in range(8):
        piece = parts[i].astype(f32)
        piece = jnp.concatenate([piece, jnp.zeros((B, 384 - width), f32)], axis=1)
        if i:
            piece = pltpu.roll(piece, 8 * i, 1)
        for k in range(3):
            part = piece[:, 128 * k : 128 * k + 128]
            if 2 * i + k < 17:
                tiles[2 * i + k] = part if tiles[2 * i + k] is None else tiles[2 * i + k] + part
    u = jnp.concatenate(tiles, axis=1)
    uq = u[:, :QR]
    ul = u[:, QR : QR + LR]
    ur = u[:, QR + LR : QR + LR + 128]
    rq = lax.rsqrt(jnp.sum(uq * uq, axis=1, keepdims=True) / QR + 1.0)
    rl = lax.rsqrt(jnp.sum(ul * ul, axis=1, keepdims=True) / LR + 1.0)
    ql[:, :QR] = (uq * rq * q_gain[...]).astype(bf16).astype(f32)
    ql[:, QR:] = jnp.zeros((B, 128), f32)
    lat = (ul * rl * kv_gain[...]).astype(bf16)
    lane = lax.broadcasted_iota(jnp.int32, (B, 128), 1)
    rot = jnp.where(lane < ROT, rotated(ur, cs[...]), 0.0).astype(bf16)
    entry[:, :LR] = lat
    entry[:, LR:] = rot[:, :ROT]
    wide[:, :LR] = lat.astype(f32)
    wide[:, LR:] = rot.astype(f32)
    first = s * 48
    tile = first // 128
    own = ql[:, pl.ds(pl.multiple_of(tile * 128, 128), 256)]
    own = pltpu.roll(own, 256 - (first - tile * 128), 1)[:, :48].astype(bf16)
    q = jnp.dot(own, q_up[...], preferred_element_type=f32)
    for p in range(8):
        t0 = q[:, 384 * p : 384 * p + 128]
        t1 = q[:, 384 * p + 128 : 384 * p + 256]
        t2 = q[:, 384 * p + 256 : 384 * p + 384]
        hh, j = (2 * p) // 8, (2 * p) % 8
        t1r = pltpu.roll(t1, 64, 1)
        t2r = pltpu.roll(t2, 64, 1)
        out[:, hh, j, :] = t0
        out[:, hh, 8 + j, :] = t1
        out[:, hh, j + 1, :] = jnp.where(lane < 64, t1r, t2r)
        out[:, hh, 8 + j + 1, :] = t2r


def query_call(idx, parts, q_gain, kv_gain, cs, q_up):
    return pl.pallas_call(
        query_kernel,
        out_shape=(
            jax.ShapeDtypeStruct((B, LR + ROT), bf16),
            jax.ShapeDtypeStruct((B, LR + 128), f32),
            jax.ShapeDtypeStruct((B, 2, 16, 128), f32),
        ),
        in_specs=[spec(SM)] + [spec(VM)] * 5,
        out_specs=(spec(VM),) * 3,
        scratch_shapes=[pltpu.VMEM((B, QR + 128), f32)],
        name="query",
    )(idx, parts, q_gain, kv_gain, cs, q_up)


def absorb_kernel(idx, parts, cs, key_up, own, out, keys, sem):
    s = idx[0]
    b, hh = s // 2, s % 2
    cp = pltpu.make_async_copy(key_up.at[:, pl.ds(pl.multiple_of(hh * 1024, 128), 1024)], keys, sem)
    cp.start()
    q = parts[0]
    for i in range(1, 32):
        q = q + parts[i]
    nope = q[:8].astype(bf16)
    rot = rotated(q[8:], jnp.broadcast_to(cs[pl.ds(b, 1), :], (8, 128)))
    lane = lax.broadcasted_iota(jnp.int32, (8, 128), 1)
    row = lax.broadcasted_iota(jnp.int32, (8, 128), 0)
    rot = jnp.where(lane < ROT, rot * SCALE, 0.0).astype(bf16)
    zero = jnp.zeros((8, 128), bf16)
    spread = jnp.concatenate(
        [jnp.where(row == j, nope.astype(f32), 0.0).astype(bf16) for j in range(8)], axis=1
    )
    cp.wait()
    lat = lax.dot_general(spread, keys[...], (((1,), (1,)), ((), ())), preferred_element_type=f32)
    pack = jnp.concatenate([(lat * SCALE).astype(bf16), rot], axis=1)
    own[...] = pack
    for i in range(32):
        out[i] = pack


def absorb_call(idx, parts, cs, key_up):
    return pl.pallas_call(
        absorb_kernel,
        out_shape=(
            jax.ShapeDtypeStruct((8, LR + 128), bf16),
            jax.ShapeDtypeStruct((32, 8, LR + 128), bf16),
        ),
        in_specs=[spec(SM), spec(VM), spec(VM), spec(HB)],
        out_specs=(spec(VM),) * 2,
        scratch_shapes=[pltpu.VMEM((LR, 1024), bf16), pltpu.SemaphoreType.DMA],
        name="absorb",
    )(idx, parts, cs, key_up)


ORDER = [(dy, dc, h) for dy in (0, 3, 1, 2) for dc in (0, 1) for h in (0, 1)]


def attend_kernel(idx, table, lengths, q, *rest):
    bufs, out = rest[:16], rest[16]
    kv, s_s, p_s, st_s, inv, place, sem = rest[17:]
    s, y, c = idx[0], idx[1], idx[2]
    for i in range(16):
        pltpu.make_async_copy(bufs[i], kv.at[pl.ds(4 * i, 4)], sem.at[i // 4]).start()

    def fill(e, _):
        inv[table[e] - s * 64] = e
        return 0

    lax.fori_loop(0, 64, fill, 0, unroll=8)
    lane = lax.broadcasted_iota(jnp.int32, (B, BP), 1)

    def scores(g, _):
        here = kv.at[pl.ds(16 * g, 16)]
        pltpu.make_async_copy(here, here, sem.at[g]).wait()
        dy = jnp.where(g == 0, 0, jnp.where(g == 1, 3, jnp.where(g == 2, 1, 2)))
        ys = lax.rem(y + dy, 4)
        for dc in range(2):
            cs = c if dc == 0 else 1 - c
            first = (ys * 2 + cs) * 8
            for k in range(8):
                at = g * 16 + dc * 8 + k
                e = inv[first + k]
                place[e] = at
                qb = q[e // 4]
                keys = kv[at, :BP, :]
                rope = jnp.concatenate([kv[at, BP:, 128 * n : 128 * n + 128] for n in range(4)], axis=0)
                sc = lax.dot_general(qb[:, :LR], keys, (((1,), (1,)), ((), ())), preferred_element_type=f32)
                s_s[e] = sc + jnp.dot(qb[:, LR : LR + ROT], rope, preferred_element_type=f32)
        return 0

    lax.fori_loop(0, 4, scores, 0)

    def softmax(b, _):
        room = lengths[b] - s * (4 * BP)
        live = [lane < room - j * BP for j in range(4)]
        sc = [jnp.where(live[j], s_s[b * 4 + j], FLOOR) for j in range(4)]
        m = jnp.maximum(jnp.maximum(sc[0], sc[1]), jnp.maximum(sc[2], sc[3]))
        m = jnp.max(m, axis=1, keepdims=True)
        p = [jnp.where(live[j], jnp.exp(sc[j] - m), 0.0) for j in range(4)]
        l = jnp.sum((p[0] + p[1]) + (p[2] + p[3]), axis=1, keepdims=True)
        m1 = m.astype(bf16).astype(f32)
        m2 = (m - m1).astype(bf16).astype(f32)
        m3 = m - m1 - m2
        l1 = l.astype(bf16).astype(f32)
        l2 = (l - l1).astype(bf16).astype(f32)
        l3 = l - l1 - l2
        stats = jnp.zeros((B, 128), f32)
        for n, v in enumerate((m1, m2, m3, l1, l2, l3)):
            stats = jnp.where(lane == n, v, stats)
        st_s[b] = stats.astype(bf16)
        p_s[b] = jnp.concatenate(p, axis=1).astype(bf16)
        return 0

    lax.fori_loop(0, B, softmax, 0, unroll=4)

    def mixing(b, _):
        p = p_s[b]
        mix = jnp.zeros((B, LR), f32)
        for j in range(4):
            keys = kv[place[b * 4 + j], :BP, :]
            mix = mix + jnp.dot(p[:, 128 * j : 128 * j + 128], keys, preferred_element_type=f32)
        out[b] = jnp.concatenate([mix.astype(bf16), st_s[b]], axis=1)
        return 0

    lax.fori_loop(0, B, mixing, 0, unroll=4)


def attend_call(idx, table, lengths, q, bufs):
    return pl.pallas_call(
        attend_kernel,
        out_shape=jax.ShapeDtypeStruct((B, 16, LR + 128), bf16),
        in_specs=[spec(SM)] * 3 + [spec(VM)] + [spec(HB)] * 16,
        out_specs=spec(VM),
        scratch_shapes=[
            pltpu.VMEM((64, BP + 16, LR), bf16),
            pltpu.VMEM((64, B, BP), f32),
            pltpu.VMEM((B, B, 4 * BP), bf16),
            pltpu.VMEM((B, B, 128), bf16),
            pltpu.SMEM((64,), jnp.int32),
            pltpu.SMEM((64,), jnp.int32),
            pltpu.SemaphoreType.DMA((4,)),
        ],
        name="attend",
    )(idx, table, lengths, q, *bufs)


def value_kernel(idx, parts, own, wide, value_up, out, vals, sem):
    s = idx[0]
    b, hh = s // 2, s % 2
    cp = pltpu.make_async_copy(value_up.at[:, pl.ds(pl.multiple_of(hh * 1024, 128), 1024)], vals, sem)
    cp.start()
    entry = wide[pl.ds(b, 1), :]
    own_score = jnp.sum(own[...].astype(f32) * entry, axis=1, keepdims=True)
    tops, tots = [], []
    for i in range(32):
        st = parts[i, :, LR:].astype(f32)
        tops.append(st[:, 0:1] + st[:, 1:2] + st[:, 2:3])
        tots.append(st[:, 3:4] + st[:, 4:5] + st[:, 5:6])
    top = own_score
    for i in range(32):
        top = jnp.maximum(top, tops[i])
    own_w = jnp.exp(own_score - top)
    total = own_w
    mix = own_w.astype(bf16).astype(f32) * entry[:, :LR]
    for i in range(32):
        w = jnp.exp(tops[i] - top)
        total = total + w * tots[i]
        mix = mix + w * parts[i, :, :LR].astype(f32)
    att = (mix / total).astype(bf16)
    cp.wait()
    full = jnp.dot(att, vals[...], preferred_element_type=f32)
    row = lax.broadcasted_iota(jnp.int32, (8, 128), 0)
    res = jnp.zeros((8, 128), f32)
    for j in range(8):
        res = jnp.where(row == j, full[:, 128 * j : 128 * j + 128], res)
    res = res.astype(bf16)
    for i in range(32):
        out[i] = res


def value_call(idx, parts, own, wide, value_up):
    return pl.pallas_call(
        value_kernel,
        out_shape=jax.ShapeDtypeStruct((32, 8, VD), bf16),
        in_specs=[spec(SM), spec(VM), spec(VM), spec(VM), spec(HB)],
        out_specs=spec(VM),
        scratch_shapes=[pltpu.VMEM((LR, 1024), bf16), pltpu.SemaphoreType.DMA],
        name="value",
    )(idx, parts, own, wide, value_up)


UP = [(i, (i + 1) % 4) for i in range(4)]
DOWN = [(i, (i + 3) % 4) for i in range(4)]
SWAP = [(0, 1), (1, 0)]


def body(hidden_in, united_down, q_gain, kv_gain, q_up, key_up, value_up, store, rope_pool, lengths, table):
    s = lax.axis_index(S)
    idx = jnp.stack([s, lax.axis_index("y"), lax.axis_index("c")]).astype(jnp.int32)
    cols, half_a, half_b = united_call(hidden_in, united_down, store, rope_pool)
    freq = 10000.0 ** (-2.0 * jnp.arange(32, dtype=f32) / ROT)
    angles = lengths.astype(f32)[:, None] * freq
    cos, sin = jnp.cos(angles), jnp.sin(angles)
    cs = jnp.concatenate([cos, cos, -sin, sin], axis=1)
    parts = exchange(cols, T)
    up_a = lax.ppermute(half_a, "y", UP)
    down_b = lax.ppermute(half_b, "y", DOWN)
    up_b = lax.ppermute(half_b, "y", UP)
    down_a = lax.ppermute(half_a, "y", DOWN)
    far_a = lax.ppermute(up_a, "y", UP)
    far_b = lax.ppermute(down_b, "y", DOWN)
    near = {0: (half_a, half_b), 3: (up_a, up_b), 1: (down_a, down_b), 2: (far_a, far_b)}
    bufs = []
    for dy, dc, h in ORDER:
        bufs.append(near[dy][h] if dc == 0 else lax.ppermute(near[dy][h], "c", SWAP))
    entry, wide, q_part = query_call(idx, parts, q_gain[None], kv_gain[None], cs, q_up)
    q_sum = exchange(q_part.reshape(32, 16, 128), S)
    own, q_copies = absorb_call(idx, q_sum, cs, key_up)
    q_all = exchange(q_copies, S)
    q_all = q_all.reshape(B, 16, LR + 128)
    mixed = attend_call(idx, table.reshape(-1), lengths, q_all, bufs)
    spans = exchange(mixed.reshape(32, 8, LR + 128), S)
    res = value_call(idx, spans, own, wide, value_up)
    res = exchange(res, S)
    return res.reshape(B, 16 * VD), entry


def solution(mesh):
    split = Mesh(mesh.devices.reshape(8, 4, 4, 2), ("z", "x", "y", "c"))
    return jax.shard_map(
        body,
        mesh=split,
        in_specs=(
            P(),
            P(None, T),
            P(),
            P(),
            P(S, T),
            P(None, T),
            P(None, T),
            P(S + T, None, None),
            P(S + T, None, None),
            P(),
            P(None, S),
        ),
        out_specs=(P(None, T), P()),
        check_vma=False,
    )
```

profile of v0, /device:TPU:2, one launch (start us, length us, event | category | flops | bytes accessed | tf_op | source)
XLA Modules:
  0.0 131.6 jit_solution(11353792290621014368)
XLA Ops:
  0.6 0.0 copy-start.9
  0.6 0.0 copy-start.7
  0.7 5.4 %united.1 = (bf16[8,16,264]{2,1,0:T(8,128)(2,1)}, bf16[4,144,512]{2,1,0:T(8,128)(2,1)}, bf16[4,144,512]{2,1,0:T(8,128)(2,1)}) custom-call(bf16[16,5120]{1,0:T(8,128)(2,1)} %hid.1, bf16[264,5120]{1,0:T(8,128)(2,1)} %bitcast.8, bf16[8,128,512]{2,1,0:T(8,128)(2,1)} %lat.1, bf16[8,64,128]{2,1,0:T(8,128)(2,1)} %rope.1), custom_call_target="tpu_custom_call" | custom-call | tf_op jit(solution)/shard_map/united/pallas_call | solution.py:80
  6.0 3.1 %collective-permute-start.6 = (bf16[4,144,512]{2,1,0:T(8,128)(2,1)}, bf16[4,144,512]{2,1,0:T(8,128)(2,1)S(1)}, u32[]{:S(2)}, u32[]{:S(2)}) collective-permute-start(bf16[4,144,512]{2,1,0:T(8,128)(2,1)} %get-tuple-element.13.rest_0_), channel_id=1, source_target_pairs={{0,6},{2,0},{4,2},{6,4},{1,7},{3,1},{5,3},{7,5},{8,14},{10,8},{12,... | collective-permute-start | bytes 1769480 | tf_op jit(solution)/shard_map/ppermute | solution.py:356
  9.1 0.0 collective-permute-start.2
  9.1 0.0 collective-permute-start
  9.1 3.2 %collective-permute-start.7 = (bf16[4,144,512]{2,1,0:T(8,128)(2,1)}, bf16[4,144,512]{2,1,0:T(8,128)(2,1)S(1)}, u32[]{:S(2)}, u32[]{:S(2)}) collective-permute-start(bf16[4,144,512]{2,1,0:T(8,128)(2,1)} %get-tuple-element.14.rest_1_), channel_id=1, source_target_pairs={{0,6},{2,0},{4,2},{6,4},{1,7},{3,1},{5,3},{7,5},{8,14},{10,8},{12,... | collective-permute-start | bytes 1769480 | tf_op jit(solution)/shard_map/ppermute | solution.py:354
  12.3 0.0 collective-permute-start.3
  12.3 0.0 copy-start.8
  12.4 4.6 %all-to-all-start = ((bf16[8,16,264]{2,1,0:T(8,128)(2,1)}), bf16[8,16,264]{2,1,0:T(8,128)(2,1)S(1)}, u32[]{:S(2)}, u32[]{:S(2)}) async-start(bf16[8,16,264]{2,1,0:T(8,128)(2,1)} %get-tuple-element.10), calls=%async_computation | async-start | bytes 196608 | tf_op jit(solution)/shard_map/all_to_all | solution.py:34
  17.0 0.0 copy-done.9
  17.0 0.1 multiply_cosine_fusion
  17.2 0.7 pad_maximum_fusion.cs
  17.8 5.3 %collective-permute-done.6.rest_8_ = bf16[4,144,512]{2,1,0:T(8,128)(2,1)S(1)} collective-permute-done((bf16[4,144,512]{2,1,0:T(8,128)(2,1)}, bf16[4,144,512]{2,1,0:T(8,128)(2,1)S(1)}, u32[]{:S(2)}, u32[]{:S(2)}) %collective-permute-start.6) | collective-permute-done | bytes 589856 | tf_op jit(solution)/shard_map/ppermute | solution.py:356
  23.1 0.0 copy-start.1
  23.1 0.0 collective-permute-start.1
  23.1 3.6 %collective-permute-done.2.rest_4_ = bf16[4,144,512]{2,1,0:T(8,128)(2,1)S(1)} collective-permute-done((bf16[4,144,512]{2,1,0:T(8,128)(2,1)}, bf16[4,144,512]{2,1,0:T(8,128)(2,1)S(1)}, u32[]{:S(2)}, u32[]{:S(2)}) %collective-permute-start.2) | collective-permute-done | bytes 589856 | tf_op jit(solution)/shard_map/ppermute | solution.py:353
  26.7 0.0 copy-start.2
  26.7 0.0 collective-permute-start.8
  26.7 0.0 collective-permute-done.rest_2_
  26.7 0.0 copy-start.3
  26.8 0.1 collective-permute-start.10
  26.8 8.6 %collective-permute-done.7.rest_9_ = bf16[4,144,512]{2,1,0:T(8,128)(2,1)S(1)} collective-permute-done((bf16[4,144,512]{2,1,0:T(8,128)(2,1)}, bf16[4,144,512]{2,1,0:T(8,128)(2,1)S(1)}, u32[]{:S(2)}, u32[]{:S(2)}) %collective-permute-start.7) | collective-permute-done | bytes 589856 | tf_op jit(solution)/shard_map/ppermute | solution.py:354
  35.5 3.6 %collective-permute-start.11 = (bf16[4,144,512]{2,1,0:T(8,128)(2,1)S(1)}, bf16[4,144,512]{2,1,0:T(8,128)(2,1)}, u32[]{:S(2)}, u32[]{:S(2)}) collective-permute-start(bf16[4,144,512]{2,1,0:T(8,128)(2,1)S(1)} %collective-permute-done.7.rest_9_), channel_id=1, source_target_pairs={{0,6},{2,0},{4,2},{6,4},{1,7},{3,1},{5,3},{7,5},{8,14},{10,8},{12,... | collective-permute-start | bytes 1769480 | tf_op jit(solution)/shard_map/ppermute | solution.py:358
  39.0 0.6 pad_add_fusion.idx
  39.6 0.0 copy-done.7
  39.6 0.6 broadcast_in_dim.8.q_gain
  40.2 0.2 all-to-all-done.parts
  40.4 0.6 copy-done.6
  41.1 2.3 %query.1 = (bf16[16,576]{1,0:T(8,128)(2,1)}, f32[16,640]{1,0:T(8,128)}, f32[16,2,16,128]{3,2,1,0:T(8,128)}) custom-call(s32[3]{0:T(128)} %pad_add_fusion.idx, bf16[8,16,264]{2,1,0:T(8,128)(2,1)} %copy-done.6, f32[1,1536]{1,0:T(1,128)} %broadcast_in_dim.8.q_gain, f32[1,512]{1,0:T(1,128)} %bitcast.12, f32[16,128]{1,0:T(8,128)} %pad_maximum_fusion.cs, ...), custom_call_target="tpu_custom_call" | custom-call | tf_op jit(solution)/shard_map/query/pallas_call | solution.py:149
  43.4 22.7 %all_to_all.25.parts = f32[32,16,128]{2,1,0:T(8,128)} all-to-all(f32[32,16,128]{2,1,0:T(8,128)} %bitcast.11), channel_id=1, replica_groups=mesh['z'=8,'x'=4,'y'=4,'c'=2] {'z','x'}, dimensions={0} | all-to-all | bytes 524288 | tf_op jit(solution)/shard_map/all_to_all | solution.py:34
  66.1 3.3 %absorb.1 = (bf16[8,640]{1,0:T(8,128)(2,1)}, bf16[32,8,640]{2,1,0:T(8,128)(2,1)}) custom-call(s32[3]{0:T(128)} %pad_add_fusion.idx, f32[32,16,128]{2,1,0:T(8,128)} %all_to_all.25.parts, f32[16,128]{1,0:T(8,128)} %pad_maximum_fusion.cs, bf16[512,2048]{1,0:T(8,128)(2,1)} %key_up.1), custom_call_target="tpu_custom_call" | custom-call | tf_op jit(solution)/shard_map/absorb/pallas_call | solution.py:189
  69.4 5.6 %all-to-all-start.2 = ((bf16[32,8,640]{2,1,0:T(8,128)(2,1)}), bf16[32,8,640]{2,1,0:T(8,128)(2,1)S(1)}, u32[]{:S(2)}, u32[]{:S(2)}) async-start(bf16[32,8,640]{2,1,0:T(8,128)(2,1)} %get-tuple-element.12), calls=%async_computation.2 | async-start | bytes 655360 | tf_op jit(solution)/shard_map/all_to_all | solution.py:34
  75.0 0.0 collective-permute-done.3.rest_5_
  75.0 0.0 copy-start.5
  75.0 0.1 collective-permute-start.4
  75.1 0.0 collective-permute-done.1.rest_3_
  75.1 0.5 collective-permute-start.9
  75.6 0.0 collective-permute-done.8.rest_10_
  75.6 0.1 collective-permute-start.5
  75.7 0.0 collective-permute-done.10.rest_12_
  75.7 0.4 collective-permute-start.12
  76.1 0.0 collective-permute-done.11.rest_13_
  76.1 0.1 collective-permute-start.13
  76.2 0.0 copy-done.8
  76.2 0.1 copy.14
  76.3 0.6 reshape.25.table
  76.9 0.3 collective-permute-done.4.rest_6_
  77.2 0.8 collective-permute-done.9.rest_11_
  78.1 0.8 collective-permute-done.5.rest_7_
  78.9 7.8 %all-to-all-done.2 = bf16[32,8,640]{2,1,0:T(8,128)(2,1)S(1)} async-done(((bf16[32,8,640]{2,1,0:T(8,128)(2,1)}), bf16[32,8,640]{2,1,0:T(8,128)(2,1)S(1)}, u32[]{:S(2)}, u32[]{:S(2)}) %all-to-all-start.2) | async-done | bytes 327712 | tf_op jit(solution)/shard_map/all_to_all | solution.py:34
  86.8 0.0 collective-permute-done.12.rest_14_
  86.8 0.0 collective-permute-done.13.rest_15_
  86.8 0.0 copy-done.1
  86.8 0.0 copy-done.2
  86.8 0.0 copy-done.3
  86.8 0.0 copy-done.4
  86.8 0.0 copy-done.5
  86.8 0.7 copy-done
  87.5 8.8 %attend.1 = bf16[16,16,640]{2,1,0:T(8,128)(2,1)} custom-call(s32[3]{0:T(128)} %pad_add_fusion.idx, s32[64]{0:T(128)} %reshape.25.table, s32[16]{0:T(128)} %lengths.1, bf16[16,16,640]{2,1,0:T(8,128)(2,1)} %bitcast.9, bf16[4,144,512]{2,1,0:T(8,128)(2,1)} %get-tuple-element.13.rest_0_, bf16[4,144,512]{2,1,0:T(8,128)(2,1)} %get-tuple-element.14.rest_1_, ...), custom_call_target="tpu_custom_call" | custom-call | tf_op jit(solution)/shard_map/attend/pallas_call | solution.py:276
  96.3 17.2 %all_to_all.26.parts = bf16[32,8,640]{2,1,0:T(8,128)(2,1)} all-to-all(bf16[32,8,640]{2,1,0:T(8,128)(2,1)} %bitcast.10), channel_id=1, replica_groups=mesh['z'=8,'x'=4,'y'=4,'c'=2] {'z','x'}, dimensions={0} | all-to-all | bytes 655360 | tf_op jit(solution)/shard_map/all_to_all | solution.py:34
  113.5 3.1 %value.1 = bf16[32,8,128]{2,1,0:T(8,128)(2,1)} custom-call(s32[3]{0:T(128)} %pad_add_fusion.idx, bf16[32,8,640]{2,1,0:T(8,128)(2,1)} %all_to_all.26.parts, bf16[8,640]{1,0:T(8,128)(2,1)} %get-tuple-element.15.own, f32[16,640]{1,0:T(8,128)} %get-tuple-element.16.wide, bf16[512,2048]{1,0:T(8,128)(2,1)} %value_up.1), custom_call_target="tpu_custom_call" | custom-call | tf_op jit(solution)/shard_map/value/pallas_call | solution.py:329
  116.6 14.3 %all_to_all.27 = bf16[32,8,128]{2,1,0:T(8,128)(2,1)S(1)} all-to-all(bf16[32,8,128]{2,1,0:T(8,128)(2,1)} %value.1), channel_id=1, replica_groups=mesh['z'=8,'x'=4,'y'=4,'c'=2] {'z','x'}, dimensions={0} | all-to-all | bytes 131072 | tf_op jit(solution)/shard_map/all_to_all | solution.py:34
  130.9 0.7 reshape.29
  (5 shorter events, 0.0 us)
Async XLA Ops:
  0.6 16.4 %copy-start.9 = (s32[16]{0:T(128)S(1)}, s32[16]{0:T(128)}, u32[]{:S(2)}) copy-start(s32[16]{0:T(128)} %lengths.1) | copy-start | bytes 196
  0.6 38.9 %copy-start.7 = (f32[1536]{0:T(1024)S(1)}, f32[1536]{0:T(1024)}, u32[]{:S(2)}) copy-start(f32[1536]{0:T(1024)} %param.13) | copy-start | bytes 18436
  6.0 17.1 %collective-permute-start.6 = (bf16[4,144,512]{2,1,0:T(8,128)(2,1)}, bf16[4,144,512]{2,1,0:T(8,128)(2,1)S(1)}, u32[]{:S(2)}, u32[]{:S(2)}) collective-permute-start(bf16[4,144,512]{2,1,0:T(8,128)(2,1)} %get-tuple-element.13.rest_0_), channel_id=1, source_target_pairs={{0,6},{2,0},{4,2},{6,4},{1,7},{3,1},{5,3},{7,5},{8,14},{10,8},{12,... | collective-permute-start | bytes 1769480 | tf_op jit(solution)/shard_map/ppermute | solution.py:356
  9.1 17.6 %collective-permute-start.2 = (bf16[4,144,512]{2,1,0:T(8,128)(2,1)}, bf16[4,144,512]{2,1,0:T(8,128)(2,1)S(1)}, u32[]{:S(2)}, u32[]{:S(2)}) collective-permute-start(bf16[4,144,512]{2,1,0:T(8,128)(2,1)} %get-tuple-element.13.rest_0_), channel_id=1, source_target_pairs={{0,2},{2,4},{4,6},{6,0},{1,3},{3,5},{5,7},{7,1},{8,10},{10,12},{12... | collective-permute-start | bytes 1769480 | tf_op jit(solution)/shard_map/ppermute | solution.py:353
  9.1 17.6 %collective-permute-start = (bf16[4,144,512]{2,1,0:T(8,128)(2,1)}, bf16[4,144,512]{2,1,0:T(8,128)(2,1)S(1)}, u32[]{:S(2)}, u32[]{:S(2)}) collective-permute-start(bf16[4,144,512]{2,1,0:T(8,128)(2,1)} %get-tuple-element.13.rest_0_), channel_id=1, source_target_pairs={{0,1},{1,0},{2,3},{3,2},{4,5},{5,4},{6,7},{7,6},{8,9},{9,8},{10,11... | collective-permute-start | bytes 1769480 | tf_op jit(solution)/shard_map/ppermute | solution.py:362
  9.1 26.4 %collective-permute-start.7 = (bf16[4,144,512]{2,1,0:T(8,128)(2,1)}, bf16[4,144,512]{2,1,0:T(8,128)(2,1)S(1)}, u32[]{:S(2)}, u32[]{:S(2)}) collective-permute-start(bf16[4,144,512]{2,1,0:T(8,128)(2,1)} %get-tuple-element.14.rest_1_), channel_id=1, source_target_pairs={{0,6},{2,0},{4,2},{6,4},{1,7},{3,1},{5,3},{7,5},{8,14},{10,8},{12,... | collective-permute-start | bytes 1769480 | tf_op jit(solution)/shard_map/ppermute | solution.py:354
  12.3 62.7 %collective-permute-start.3 = (bf16[4,144,512]{2,1,0:T(8,128)(2,1)}, bf16[4,144,512]{2,1,0:T(8,128)(2,1)S(1)}, u32[]{:S(2)}, u32[]{:S(2)}) collective-permute-start(bf16[4,144,512]{2,1,0:T(8,128)(2,1)} %get-tuple-element.14.rest_1_), channel_id=1, source_target_pairs={{0,2},{2,4},{4,6},{6,0},{1,3},{3,5},{5,7},{7,1},{8,10},{10,12},{12... | collective-permute-start | bytes 1769480 | tf_op jit(solution)/shard_map/ppermute | solution.py:355
  12.3 63.9 %copy-start.8 = (s32[16,4]{0,1:T(4,128)S(1)}, s32[16,4]{0,1:T(4,128)}, u32[]{:S(2)}) copy-start(s32[16,4]{0,1:T(4,128)} %param.21) | copy-start | bytes 772
  12.4 28.1 %all-to-all-start = ((bf16[8,16,264]{2,1,0:T(8,128)(2,1)}), bf16[8,16,264]{2,1,0:T(8,128)(2,1)S(1)}, u32[]{:S(2)}, u32[]{:S(2)}) async-start(bf16[8,16,264]{2,1,0:T(8,128)(2,1)} %get-tuple-element.10), calls=%async_computation | async-start | bytes 196608 | tf_op jit(solution)/shard_map/all_to_all | solution.py:34
  23.1 63.6 %copy-start.1 = (bf16[4,144,512]{2,1,0:T(8,128)(2,1)}, bf16[4,144,512]{2,1,0:T(8,128)(2,1)S(1)}, u32[]{:S(2)}) copy-start(bf16[4,144,512]{2,1,0:T(8,128)(2,1)S(1)} %collective-permute-done.6.rest_8_) | copy-start | bytes 1769476
  23.1 52.0 %collective-permute-start.1 = (bf16[4,144,512]{2,1,0:T(8,128)(2,1)}, bf16[4,144,512]{2,1,0:T(8,128)(2,1)}, u32[]{:S(2)}, u32[]{:S(2)}) collective-permute-start(bf16[4,144,512]{2,1,0:T(8,128)(2,1)} %get-tuple-element.14.rest_1_), channel_id=1, source_target_pairs={{0,1},{1,0},{2,3},{3,2},{4,5},{5,4},{6,7},{7,6},{8,9},{9,8},{10,11... | collective-permute-start | bytes 1769480 | tf_op jit(solution)/shard_map/ppermute | solution.py:362
  26.7 60.1 %copy-start.2 = (bf16[4,144,512]{2,1,0:T(8,128)(2,1)}, bf16[4,144,512]{2,1,0:T(8,128)(2,1)S(1)}, u32[]{:S(2)}) copy-start(bf16[4,144,512]{2,1,0:T(8,128)(2,1)S(1)} %collective-permute-done.2.rest_4_) | copy-start | bytes 1769476
  26.7 48.9 %collective-permute-start.8 = (bf16[4,144,512]{2,1,0:T(8,128)(2,1)S(1)}, bf16[4,144,512]{2,1,0:T(8,128)(2,1)}, u32[]{:S(2)}, u32[]{:S(2)}) collective-permute-start(bf16[4,144,512]{2,1,0:T(8,128)(2,1)S(1)} %collective-permute-done.6.rest_8_), channel_id=1, source_target_pairs={{0,1},{1,0},{2,3},{3,2},{4,5},{5,4},{6,7},{7,6},{8,9},{9,8},{10,11... | collective-permute-start | bytes 1769480 | tf_op jit(solution)/shard_map/ppermute | solution.py:362
  26.7 60.1 %copy-start.3 = (bf16[4,144,512]{2,1,0:T(8,128)(2,1)}, bf16[4,144,512]{2,1,0:T(8,128)(2,1)S(1)}, u32[]{:S(2)}) copy-start(bf16[4,144,512]{2,1,0:T(8,128)(2,1)S(1)} %collective-permute-done.rest_2_) | copy-start | bytes 1769476
  26.8 49.0 %collective-permute-start.10 = (bf16[4,144,512]{2,1,0:T(8,128)(2,1)S(1)}, bf16[4,144,512]{2,1,0:T(8,128)(2,1)}, u32[]{:S(2)}, u32[]{:S(2)}) collective-permute-start(bf16[4,144,512]{2,1,0:T(8,128)(2,1)S(1)} %collective-permute-done.2.rest_4_), channel_id=1, source_target_pairs={{0,2},{2,4},{4,6},{6,0},{1,3},{3,5},{5,7},{7,1},{8,10},{10,12},{12... | collective-permute-start | bytes 1769480 | tf_op jit(solution)/shard_map/ppermute | solution.py:357
  35.5 51.3 %copy-start.4 = (bf16[4,144,512]{2,1,0:T(8,128)(2,1)}, bf16[4,144,512]{2,1,0:T(8,128)(2,1)S(1)}, u32[]{:S(2)}) copy-start(bf16[4,144,512]{2,1,0:T(8,128)(2,1)S(1)} %collective-permute-done.7.rest_9_) | copy-start | bytes 1769476
  35.5 40.7 %collective-permute-start.11 = (bf16[4,144,512]{2,1,0:T(8,128)(2,1)S(1)}, bf16[4,144,512]{2,1,0:T(8,128)(2,1)}, u32[]{:S(2)}, u32[]{:S(2)}) collective-permute-start(bf16[4,144,512]{2,1,0:T(8,128)(2,1)S(1)} %collective-permute-done.7.rest_9_), channel_id=1, source_target_pairs={{0,6},{2,0},{4,2},{6,4},{1,7},{3,1},{5,3},{7,5},{8,14},{10,8},{12,... | collective-permute-start | bytes 1769480 | tf_op jit(solution)/shard_map/ppermute | solution.py:358
  40.4 0.6 copy-start.6
  69.4 17.3 %all-to-all-start.2 = ((bf16[32,8,640]{2,1,0:T(8,128)(2,1)}), bf16[32,8,640]{2,1,0:T(8,128)(2,1)S(1)}, u32[]{:S(2)}, u32[]{:S(2)}) async-start(bf16[32,8,640]{2,1,0:T(8,128)(2,1)} %get-tuple-element.12), calls=%async_computation.2 | async-start | bytes 655360 | tf_op jit(solution)/shard_map/all_to_all | solution.py:34
  75.0 11.8 %copy-start.5 = (bf16[4,144,512]{2,1,0:T(8,128)(2,1)}, bf16[4,144,512]{2,1,0:T(8,128)(2,1)S(1)}, u32[]{:S(2)}) copy-start(bf16[4,144,512]{2,1,0:T(8,128)(2,1)S(1)} %collective-permute-done.3.rest_5_) | copy-start | bytes 1769476
  75.0 2.2 %collective-permute-start.4 = (bf16[4,144,512]{2,1,0:T(8,128)(2,1)S(1)}, bf16[4,144,512]{2,1,0:T(8,128)(2,1)}, u32[]{:S(2)}, u32[]{:S(2)}) collective-permute-start(bf16[4,144,512]{2,1,0:T(8,128)(2,1)S(1)} %collective-permute-done.2.rest_4_), channel_id=1, source_target_pairs={{0,1},{1,0},{2,3},{3,2},{4,5},{5,4},{6,7},{7,6},{8,9},{9,8},{10,11... | collective-permute-start | bytes 1769480 | tf_op jit(solution)/shard_map/ppermute | solution.py:362
  75.1 3.0 %collective-permute-start.9 = (bf16[4,144,512]{2,1,0:T(8,128)(2,1)S(1)}, bf16[4,144,512]{2,1,0:T(8,128)(2,1)}, u32[]{:S(2)}, u32[]{:S(2)}) collective-permute-start(bf16[4,144,512]{2,1,0:T(8,128)(2,1)S(1)} %collective-permute-done.7.rest_9_), channel_id=1, source_target_pairs={{0,1},{1,0},{2,3},{3,2},{4,5},{5,4},{6,7},{7,6},{8,9},{9,8},{10,11... | collective-permute-start | bytes 1769480 | tf_op jit(solution)/shard_map/ppermute | solution.py:362
  75.6 3.3 %collective-permute-start.5 = (bf16[4,144,512]{2,1,0:T(8,128)(2,1)S(1)}, bf16[4,144,512]{2,1,0:T(8,128)(2,1)}, u32[]{:S(2)}, u32[]{:S(2)}) collective-permute-start(bf16[4,144,512]{2,1,0:T(8,128)(2,1)S(1)} %collective-permute-done.3.rest_5_), channel_id=1, source_target_pairs={{0,1},{1,0},{2,3},{3,2},{4,5},{5,4},{6,7},{7,6},{8,9},{9,8},{10,11... | collective-permute-start | bytes 1769480 | tf_op jit(solution)/shard_map/ppermute | solution.py:362
  75.7 11.0 %collective-permute-start.12 = (bf16[4,144,512]{2,1,0:T(8,128)(2,1)}, bf16[4,144,512]{2,1,0:T(8,128)(2,1)}, u32[]{:S(2)}, u32[]{:S(2)}) collective-permute-start(bf16[4,144,512]{2,1,0:T(8,128)(2,1)} %collective-permute-done.10.rest_12_), channel_id=1, source_target_pairs={{0,1},{1,0},{2,3},{3,2},{4,5},{5,4},{6,7},{7,6},{8,9},{9,8},{10,11... | collective-permute-start | bytes 1769480 | tf_op jit(solution)/shard_map/ppermute | solution.py:362
  76.1 10.6 %collective-permute-start.13 = (bf16[4,144,512]{2,1,0:T(8,128)(2,1)}, bf16[4,144,512]{2,1,0:T(8,128)(2,1)}, u32[]{:S(2)}, u32[]{:S(2)}) collective-permute-start(bf16[4,144,512]{2,1,0:T(8,128)(2,1)} %collective-permute-done.11.rest_13_), channel_id=1, source_target_pairs={{0,1},{1,0},{2,3},{3,2},{4,5},{5,4},{6,7},{7,6},{8,9},{9,8},{10,11... | collective-permute-start | bytes 1769480 | tf_op jit(solution)/shard_map/ppermute | solution.py:362
  86.8 0.7 copy-start
where the time goes:
time: 132 us
  blocking collectives  54.2 us (41%)
  waiting for transfers between devices  27.6 us (21%)
  Pallas kernels  22.9 us (17%)
  starting transfers between devices  21.4 us (16%)
  local copies, waits for them, and re-layouts  3.27 us (2%)
  other arithmetic  1.36 us (1%)
    all_to_all x3, blocking collectives, exchange(): return lax.all_to_all(pieces, axes, split_axis=0, concat_axis=0, tiled=True)  54.2 us
    all_to_all x2, starting transfers between devices, exchange(): return lax.all_to_all(pieces, axes, split_axis=0, concat_axis=0, tiled=True)  10.2 us
    pallas_call x1, Pallas kernels, attend_call(): pl.pallas_call(attend_kernel, out_shape=jax.ShapeDtypeStruct((B, 16, LR +...  8.76 us
    ppermute x1, waiting for transfers between devices, body(): down_b = lax.ppermute(half_b, 'y', DOWN)  8.63 us
    all_to_all x2, waiting for transfers between devices, exchange(): return lax.all_to_all(pieces, axes, split_axis=0, concat_axis=0, tiled=True)  8.07 us
    pallas_call x1, Pallas kernels, united_call(): pl.pallas_call(united_kernel, out_shape=(jax.ShapeDtypeStruct((8, B, cols...  5.35 us
    ppermute x1, waiting for transfers between devices, body(): down_a = lax.ppermute(half_a, 'y', DOWN)  5.31 us
    ppermute x1, waiting for transfers between devices, body(): up_a = lax.ppermute(half_a, 'y', UP)  3.58 us
  transfers between devices with their start and end apart: 16, of which 8 were waited for; matrix products, arithmetic and copies ran while one was open for 2% of the time, Pallas kernels for 4%

commit v1 on v0

v1 whole, which is shorter than its diff:
```python
import functools

import jax
import jax.numpy as jnp
from jax import lax
from jax.experimental import pallas as pl
from jax.experimental.pallas import tpu as pltpu
from jax.sharding import Mesh
from jax.sharding import PartitionSpec as P


D = 5120
QR = 1536
LR = 512
ROT = 64
VD = 128
B = 16
BP = 128
QH = 192
SCALE = QH ** (-0.5)
FLOOR = -1e30
S = ("z", "x")
T = ("y", "c")
bf16 = jnp.bfloat16
f32 = jnp.float32
VM = pltpu.MemorySpace.VMEM
SM = pltpu.MemorySpace.SMEM
HB = pltpu.MemorySpace.HBM


def spec(space):
    return pl.BlockSpec(memory_space=space)


def exchange(pieces, axes):
    return lax.all_to_all(pieces, axes, split_axis=0, concat_axis=0, tiled=True)


UK = 5


def united_kernel(hid, wt, out, wbuf, wsem):
    step = D // UK
    copies = []
    for k in range(UK):
        cp = pltpu.make_async_copy(wt.at[:, pl.ds(k * step, step)], wbuf.at[k], wsem.at[k])
        cp.start()
        copies.append(cp)
    acc = jnp.zeros(out.shape, f32)
    for k in range(UK):
        copies[k].wait()
        acc = acc + lax.dot_general(
            hid[:, k * step : (k + 1) * step],
            wbuf[k],
            (((1,), (1,)), ((), ())),
            preferred_element_type=f32,
        )
    out[...] = acc.astype(bf16)


def united_call(hid, down):
    cols = down.shape[1]
    return pl.pallas_call(
        united_kernel,
        out_shape=jax.ShapeDtypeStruct((B, cols), bf16),
        in_specs=[spec(VM), spec(HB)],
        out_specs=spec(VM),
        scratch_shapes=[pltpu.VMEM((UK, cols, D // UK), bf16), pltpu.SemaphoreType.DMA((UK,))],
        name="united",
    )(hid, down.T)


def tiles_kernel(q_up, out):
    for k in range(32):
        j = k % 24
        out[k] = q_up[:, 128 * j : 128 * j + 128]


def tiles_call(q_up):
    return pl.pallas_call(
        tiles_kernel,
        out_shape=jax.ShapeDtypeStruct((32, 48, 128), bf16),
        in_specs=[spec(VM)],
        out_specs=spec(VM),
        name="tiles",
    )(q_up)


def pack_kernel(lat, rope, pack_a, pack_b, cache, ropes, sem):
    fetch_rope = pltpu.make_async_copy(rope, ropes, sem.at[0])
    fetch_rope.start()
    fetch = []
    for h in range(2):
        cp = pltpu.make_async_copy(lat.at[pl.ds(4 * h, 4)], cache.at[pl.ds(4 * h, 4), pl.ds(0, BP), :], sem.at[1 + h])
        cp.start()
        fetch.append(cp)
    fetch_rope.wait()
    for n in range(8):
        for g in range(4):
            cache[n, BP:, 128 * g : 128 * g + 128] = ropes[n, 16 * g : 16 * g + 16, :]
    stores = []
    for h, dst in enumerate((pack_a, pack_b)):
        fetch[h].wait()
        st = pltpu.make_async_copy(cache.at[pl.ds(4 * h, 4)], dst, sem.at[3 + h])
        st.start()
        stores.append(st)
    for st in stores:
        st.wait()


def pack_call(lat, rope):
    half = jax.ShapeDtypeStruct((4, BP + 16, LR), bf16)
    return pl.pallas_call(
        pack_kernel,
        out_shape=(half, half),
        in_specs=[spec(HB), spec(HB)],
        out_specs=(spec(HB), spec(HB)),
        scratch_shapes=[
            pltpu.VMEM((8, BP + 16, LR), bf16),
            pltpu.VMEM((8, ROT, BP), bf16),
            pltpu.SemaphoreType.DMA((5,)),
        ],
        name="pack",
    )(lat, rope)


def swapped(x):
    lane = lax.broadcasted_iota(jnp.int32, x.shape, 1)
    return jnp.where(lane % ROT < ROT // 2, pltpu.roll(x, 96, 1), pltpu.roll(x, 32, 1))


def query_kernel(idx, *refs):
    pieces, (q_gain, kv_gain, cos, sin, weights, entry, wide, out, parts) = refs[:8], refs[8:]
    s, y, c = idx[0], idx[1], idx[2]
    width = 264
    for i in range(8):
        cp = c if i % 2 == 0 else 1 - c
        parts[lax.rem(y + i // 2, 4) * 2 + cp] = pieces[i][...].astype(f32)
    tiles = [None] * 17
    for i in range(8):
        piece = parts[i]
        piece = jnp.concatenate([piece, jnp.zeros((B, 384 - width), f32)], axis=1)
        if i:
            piece = pltpu.roll(piece, 8 * i, 1)
        for k in range(3):
            part = piece[:, 128 * k : 128 * k + 128]
            if 2 * i + k < 17:
                tiles[2 * i + k] = part if tiles[2 * i + k] is None else tiles[2 * i + k] + part
    u = jnp.concatenate(tiles, axis=1)
    uq = u[:, :QR]
    ul = u[:, QR : QR + LR]
    ur = u[:, QR + LR : QR + LR + 128]
    rq = lax.rsqrt(jnp.sum(uq * uq, axis=1, keepdims=True) / QR + 1.0)
    rl = lax.rsqrt(jnp.sum(ul * ul, axis=1, keepdims=True) / LR + 1.0)
    ql = (uq * rq * q_gain[...]).astype(bf16)
    q = jnp.dot(ql, weights[...].reshape(QR, 128), preferred_element_type=f32)
    lane = lax.broadcasted_iota(jnp.int32, (B, 128), 1)
    kind = lax.rem(s, 3)
    in_rope = ((lane < ROT) & (kind == 1)) | ((lane >= ROT) & (kind == 2))
    res = jnp.where(in_rope, (q * cos[...] + swapped(q) * sin[...]) * SCALE, q).astype(bf16)
    for i in range(32):
        out[i] = res
    lat = (ul * rl * kv_gain[...]).astype(bf16)
    rot = jnp.where(lane < ROT, ur * cos[...] + swapped(ur) * sin[...], 0.0).astype(bf16)
    entry[:, :LR] = lat
    entry[:, LR:] = rot[:, :ROT]
    wide[:, :LR] = lat.astype(f32)
    wide[:, LR:] = rot.astype(f32)


def query_call(idx, parts, q_gain, kv_gain, cos, sin, weights):
    return pl.pallas_call(
        query_kernel,
        out_shape=(
            jax.ShapeDtypeStruct((B, LR + ROT), bf16),
            jax.ShapeDtypeStruct((B, LR + 128), f32),
            jax.ShapeDtypeStruct((32, B, 128), bf16),
        ),
        in_specs=[spec(SM)] + [spec(VM)] * 13,
        out_specs=(spec(VM),) * 3,
        scratch_shapes=[pltpu.VMEM((8, B, 264), f32)],
        name="query",
    )(idx, *parts, q_gain, kv_gain, cos, sin, weights)


ORDER = [(dy, dc, h) for dy in (0, 3, 1, 2) for dc in (0, 1) for h in (0, 1)]


def attend_kernel(idx, table, lengths, q, wide, key_up, *rest):
    bufs, out = rest[:16], rest[16]
    keys_v, kv, q_s, s_s, p_s, o_s, own_s, inv, place, ksem, sem = rest[17:]
    s, y, c = idx[0], idx[1], idx[2]
    load_keys = pltpu.make_async_copy(key_up, keys_v, ksem)
    load_keys.start()
    for i in range(16):
        pltpu.make_async_copy(bufs[i], kv.at[pl.ds(4 * i, 4)], sem.at[i // 4]).start()

    def fill(e, _):
        inv[table[e] - s * 64] = e
        return 0

    lax.fori_loop(0, 64, fill, 0, unroll=8)
    lane = lax.broadcasted_iota(jnp.int32, (B, BP), 1)
    load_keys.wait()
    for p in range(8):
        t0 = q[3 * p].astype(f32)
        t1 = pltpu.roll(q[3 * p + 1].astype(f32), 64, 1)
        t2 = pltpu.roll(q[3 * p + 2].astype(f32), 64, 1)
        r0 = q[3 * p + 1].astype(f32)
        nopes = (t0, jnp.where(lane < ROT, t1, t2))
        ropes = (jnp.where(lane < ROT, r0, 0.0), jnp.where(lane < ROT, t2, 0.0))
        for j in range(2):
            h = 2 * p + j
            lat = lax.dot_general(
                nopes[j].astype(bf16),
                keys_v[:, 128 * h : 128 * h + 128],
                (((1,), (1,)), ((), ())),
                preferred_element_type=f32,
            )
            q_s[:, h, :LR] = (lat * SCALE).astype(bf16).astype(f32)
            q_s[:, h, LR:] = ropes[j]

    def scores(g, _):
        here = kv.at[pl.ds(16 * g, 16)]
        pltpu.make_async_copy(here, here, sem.at[g]).wait()
        dy = jnp.where(g == 0, 0, jnp.where(g == 1, 3, jnp.where(g == 2, 1, 2)))
        ys = lax.rem(y + dy, 4)
        for dc in range(2):
            cs = c if dc == 0 else 1 - c
            first = (ys * 2 + cs) * 8
            for k in range(8):
                at = g * 16 + dc * 8 + k
                e = inv[first + k]
                place[e] = at
                qb = q_s[e // 4].astype(bf16)
                keys = kv[at, :BP, :]
                rope = jnp.concatenate([kv[at, BP:, 128 * n : 128 * n + 128] for n in range(4)], axis=0)
                sc = lax.dot_general(qb[:, :LR], keys, (((1,), (1,)), ((), ())), preferred_element_type=f32)
                s_s[e] = sc + jnp.dot(qb[:, LR : LR + ROT], rope, preferred_element_type=f32)
        return 0

    lax.fori_loop(0, 4, scores, 0)

    def softmax(bh, r):
        b = bh * 8 + r
        room = lengths[b] - s * (4 * BP)
        new = jnp.sum(q_s[b] * wide[pl.ds(b, 1), :], axis=1, keepdims=True)
        mine = jnp.full((B, 1), s, jnp.int32) == 0
        live = [lane < room - j * BP for j in range(4)]
        sc = [jnp.where(live[j], s_s[b * 4 + j], FLOOR) for j in range(4)]
        m = jnp.maximum(jnp.maximum(sc[0], sc[1]), jnp.maximum(sc[2], sc[3]))
        m = jnp.maximum(jnp.max(m, axis=1, keepdims=True), jnp.where(mine, new, FLOOR))
        p = [jnp.where(live[j], jnp.exp(sc[j] - m), 0.0) for j in range(4)]
        new = jnp.where(mine, jnp.exp(new - m), 0.0)
        l = jnp.sum((p[0] + p[1]) + (p[2] + p[3]), axis=1, keepdims=True) + new
        m1 = m.astype(bf16).astype(f32)
        m2 = (m - m1).astype(bf16).astype(f32)
        m3 = m - m1 - m2
        l1 = l.astype(bf16).astype(f32)
        l2 = (l - l1).astype(bf16).astype(f32)
        l3 = l - l1 - l2
        stats = jnp.zeros((B, 128), f32)
        for n, v in enumerate((m1, m2, m3, l1, l2, l3)):
            stats = jnp.where(lane == n, v, stats)
        o_s[pl.ds(bh * 16, 16), r, LR:] = stats
        own_s[b] = new.astype(bf16).astype(f32) * wide[pl.ds(b, 1), :LR]
        p_s[b] = jnp.concatenate(p, axis=1).astype(bf16)

    def mixing(bh, r):
        b = bh * 8 + r
        p = p_s[b]
        mix = own_s[b]
        for j in range(4):
            keys = kv[place[b * 4 + j], :BP, :]
            mix = mix + jnp.dot(p[:, 128 * j : 128 * j + 128], keys, preferred_element_type=f32)
        o_s[pl.ds(bh * 16, 16), r, :LR] = mix

    def halves(step):
        def both(bh, _):
            for r in range(8):
                step(bh, r)
            return 0

        lax.fori_loop(0, 2, both, 0)

    halves(softmax)
    halves(mixing)

    def pour(i, _):
        out[i] = o_s[i].astype(bf16)
        return 0

    lax.fori_loop(0, 32, pour, 0, unroll=8)


def attend_call(idx, table, lengths, q, wide, key_up, bufs):
    return pl.pallas_call(
        attend_kernel,
        out_shape=jax.ShapeDtypeStruct((32, 8, LR + 128), bf16),
        in_specs=[spec(SM)] * 3 + [spec(VM)] * 2 + [spec(HB)] * 17,
        out_specs=spec(VM),
        scratch_shapes=[
            pltpu.VMEM((LR, 2048), bf16),
            pltpu.VMEM((64, BP + 16, LR), bf16),
            pltpu.VMEM((B, B, LR + 128), f32),
            pltpu.VMEM((64, B, BP), f32),
            pltpu.VMEM((B, B, 4 * BP), bf16),
            pltpu.VMEM((32, 8, LR + 128), f32),
            pltpu.VMEM((B, B, LR), f32),
            pltpu.SMEM((64,), jnp.int32),
            pltpu.SMEM((64,), jnp.int32),
            pltpu.SemaphoreType.DMA,
            pltpu.SemaphoreType.DMA((4,)),
        ],
        name="attend",
    )(idx, table, lengths, q, wide, key_up, *bufs)


def value_kernel(idx, parts, value_up, out, vals, sem):
    h = lax.rem(idx[0], 16)
    cp = pltpu.make_async_copy(value_up.at[:, pl.ds(pl.multiple_of(h * VD, VD), VD)], vals, sem)
    cp.start()
    tops, tots = [], []
    for i in range(32):
        st = parts[i, :, LR:].astype(f32)
        tops.append(st[:, 0:1] + st[:, 1:2] + st[:, 2:3])
        tots.append(st[:, 3:4] + st[:, 4:5] + st[:, 5:6])
    top = functools.reduce(jnp.maximum, tops)
    total = jnp.zeros((8, 1), f32)
    mix = jnp.zeros((8, LR), f32)
    for i in range(32):
        w = jnp.exp(tops[i] - top)
        total = total + w * tots[i]
        mix = mix + w * parts[i, :, :LR].astype(f32)
    att = (mix / total).astype(bf16)
    cp.wait()
    res = jnp.dot(att, vals[...], preferred_element_type=f32).astype(bf16)
    for i in range(32):
        out[i] = res


def value_call(idx, parts, value_up):
    return pl.pallas_call(
        value_kernel,
        out_shape=jax.ShapeDtypeStruct((32, 8, VD), bf16),
        in_specs=[spec(SM), spec(VM), spec(HB)],
        out_specs=spec(VM),
        scratch_shapes=[pltpu.VMEM((LR, VD), bf16), pltpu.SemaphoreType.DMA],
        name="value",
    )(idx, parts, value_up)


UP = [(i, (i + 1) % 4) for i in range(4)]
DOWN = [(i, (i + 3) % 4) for i in range(4)]
SWAP = [(0, 1), (1, 0)]


def shift(value, axis, pairs):
    return lax.ppermute(value, axis, pairs)


def body(hidden_in, united_down, q_gain, kv_gain, q_up, key_up, value_up, store, rope_pool, lengths, table):
    s = lax.axis_index(S)
    idx = jnp.stack([s, lax.axis_index("y"), lax.axis_index("c")]).astype(jnp.int32)
    lane = jnp.arange(128)
    freq = 10000.0 ** (-2.0 * (lane % 32).astype(f32) / ROT)
    angles = lengths.astype(f32)[:, None] * freq
    cos, sin = jnp.cos(angles), jnp.sin(angles)
    sin = jnp.where(lane % ROT < ROT // 2, -sin, sin)
    half_a, half_b = pack_call(store, rope_pool)
    up_a = shift(half_a, "y", UP)
    down_b = shift(half_b, "y", DOWN)
    q_tile = exchange(tiles_call(q_up), S)
    cols = united_call(hidden_in, united_down)
    spread = [cols] + [shift(cols, "y", [((i + d) % 4, i) for i in range(4)]) for d in (1, 2, 3)]
    parts = []
    for d in range(4):
        parts += [spread[d], shift(spread[d], "c", SWAP)]
    up_b = shift(half_b, "y", UP)
    down_a = shift(half_a, "y", DOWN)
    far_a = shift(up_a, "y", UP)
    far_b = shift(down_b, "y", DOWN)
    near = {0: (half_a, half_b), 3: (up_a, up_b), 1: (down_a, down_b), 2: (far_a, far_b)}
    bufs = []
    for dy, dc, h in ORDER:
        bufs.append(near[dy][h] if dc == 0 else shift(near[dy][h], "c", SWAP))
    entry, wide, q_copies = query_call(idx, parts, q_gain[None], kv_gain[None], cos, sin, q_tile)
    q_all = exchange(q_copies, S)
    mixed = attend_call(idx, table.reshape(-1), lengths, q_all, wide, key_up, bufs)
    spans = exchange(mixed, S)
    res = value_call(idx, spans, value_up)
    res = exchange(res, S)
    res = res.reshape(2, 16, 8, VD).transpose(0, 2, 1, 3).reshape(B, 16 * VD)
    return res, entry


def solution(mesh):
    split = Mesh(mesh.devices.reshape(8, 4, 4, 2), ("z", "x", "y", "c"))
    return jax.shard_map(
        body,
        mesh=split,
        in_specs=(
            P(),
            P(None, T),
            P(),
            P(),
            P(S, T),
            P(None, T),
            P(None, T),
            P(S + T, None, None),
            P(S + T, None, None),
            P(),
            P(None, S),
        ),
        out_specs=(P(None, T), P()),
        check_vma=False,
    )
```

time: 132 us -> 144 us (1.091)
  the two profiles are of different devices: /device:TPU:2 before, /device:TPU:8 now
where the time goes in v1:
time: 144 us; the launch traced here: 143 us
  waiting for transfers between devices  49.7 us (35%)
  blocking collectives  31.7 us (22%)
  starting transfers between devices  31.3 us (22%)
  Pallas kernels  25 us (17%)
  local copies, waits for them, and re-layouts  3.45 us (2%)
    ppermute x21, waiting for transfers between devices, shift(): return lax.ppermute(value, axis, pairs)  37.9 us
    all_to_all x2, blocking collectives, exchange(): return lax.all_to_all(pieces, axes, split_axis=0, concat_axis=0, tiled=True)  31.7 us
    all_to_all x2, starting transfers between devices, exchange(): return lax.all_to_all(pieces, axes, split_axis=0, concat_axis=0, tiled=True)  20.8 us
    all_to_all x2, waiting for transfers between devices, exchange(): return lax.all_to_all(pieces, axes, split_axis=0, concat_axis=0, tiled=True)  11.8 us
    pallas_call x1, Pallas kernels, attend_call(): pl.pallas_call(attend_kernel, out_shape=jax.ShapeDtypeStruct((32, 8, LR +...  11.7 us
    ppermute x21, starting transfers between devices, shift(): return lax.ppermute(value, axis, pairs)  10.5 us
    pallas_call x1, Pallas kernels, united_call(): pl.pallas_call(united_kernel, out_shape=jax.ShapeDtypeStruct((B, cols), b...  4.26 us
  transfers between devices with their start and end apart: 23, of which 10 were waited for; matrix products, arithmetic and copies ran while one was open for 2% of the time, Pallas kernels for 6%

profile of v1, /device:TPU:8, one launch (start us, length us, event | category | flops | bytes accessed | tf_op | source)
XLA Modules:
  0.0 143.5 jit_solution(4164888968850820928)
XLA Ops:
  0.6 2.2 %pack.1 = (bf16[4,144,512]{2,1,0:T(8,128)(2,1)}, bf16[4,144,512]{2,1,0:T(8,128)(2,1)}) custom-call(bf16[8,128,512]{2,1,0:T(8,128)(2,1)} %lat.1, bf16[8,64,128]{2,1,0:T(8,128)(2,1)} %rope.1), custom_call_target="tpu_custom_call" | custom-call | tf_op jit(solution)/shard_map/pack/pallas_call | solution.py:113
  2.8 2.2 %collective-permute-start.13 = (bf16[4,144,512]{2,1,0:T(8,128)(2,1)}, bf16[4,144,512]{2,1,0:T(8,128)(2,1)S(1)}, u32[]{:S(2)}, u32[]{:S(2)}) collective-permute-start(bf16[4,144,512]{2,1,0:T(8,128)(2,1)} %get-tuple-element.9.rest_0_), channel_id=1, source_target_pairs={{0,6},{2,0},{4,2},{6,4},{1,7},{3,1},{5,3},{7,5},{8,14},{10,8},{12,... | collective-permute-start | bytes 1769480 | tf_op jit(solution)/shard_map/ppermute | solution.py:359
  5.1 0.0 collective-permute-start.9
  5.1 0.0 collective-permute-start.7
  5.1 2.0 %collective-permute-start.14 = (bf16[4,144,512]{2,1,0:T(8,128)(2,1)}, bf16[4,144,512]{2,1,0:T(8,128)(2,1)S(1)}, u32[]{:S(2)}, u32[]{:S(2)}) collective-permute-start(bf16[4,144,512]{2,1,0:T(8,128)(2,1)} %get-tuple-element.10.rest_1_), channel_id=1, source_target_pairs={{0,6},{2,0},{4,2},{6,4},{1,7},{3,1},{5,3},{7,5},{8,14},{10,8},{12,... | collective-permute-start | bytes 1769480 | tf_op jit(solution)/shard_map/ppermute | solution.py:359
  7.1 4.3 %united.1.refs_0_ = bf16[16,264]{1,0:T(8,128)(2,1)} custom-call(bf16[16,5120]{1,0:T(8,128)(2,1)} %hid.1, bf16[264,5120]{1,0:T(8,128)(2,1)} %bitcast.10), custom_call_target="tpu_custom_call" | custom-call | tf_op jit(solution)/shard_map/united/pallas_call | solution.py:63
  11.4 0.1 collective-permute-start.5
  11.5 8.5 %collective-permute-done.5.refs_6_ = bf16[16,264]{1,0:T(8,128)(2,1)S(1)} collective-permute-done((bf16[16,264]{1,0:T(8,128)(2,1)}, bf16[16,264]{1,0:T(8,128)(2,1)S(1)}, u32[]{:S(2)}, u32[]{:S(2)}) %collective-permute-start.5) | collective-permute-done | bytes 8480 | tf_op jit(solution)/shard_map/ppermute | solution.py:359
  19.9 1.3 collective-permute-start.3
  21.2 11.0 %collective-permute-done.3.refs_4_ = bf16[16,264]{1,0:T(8,128)(2,1)S(1)} collective-permute-done((bf16[16,264]{1,0:T(8,128)(2,1)}, bf16[16,264]{1,0:T(8,128)(2,1)S(1)}, u32[]{:S(2)}, u32[]{:S(2)}) %collective-permute-start.3) | collective-permute-done | bytes 8480 | tf_op jit(solution)/shard_map/ppermute | solution.py:359
  32.2 0.0 collective-permute-start.1
  32.3 3.9 %collective-permute-done.1.refs_2_ = bf16[16,264]{1,0:T(8,128)(2,1)S(1)} collective-permute-done((bf16[16,264]{1,0:T(8,128)(2,1)}, bf16[16,264]{1,0:T(8,128)(2,1)S(1)}, u32[]{:S(2)}, u32[]{:S(2)}) %collective-permute-start.1) | collective-permute-done | bytes 8480 | tf_op jit(solution)/shard_map/ppermute | solution.py:359
  36.2 0.0 collective-permute-start
  36.2 1.4 collective-permute-done.refs_1_
  37.5 0.2 collective-permute-start.6
  37.7 1.0 collective-permute-done.6.refs_7_
  38.7 0.2 collective-permute-start.4
  38.9 1.0 collective-permute-done.4.refs_5_
  39.9 0.2 collective-permute-start.2
  40.1 1.0 collective-permute-done.2.refs_3_
  41.1 0.0 copy-done.1
  41.1 0.0 collective-permute-start.10
  41.1 0.0 collective-permute-done.13.rest_8_
  41.1 0.3 collective-permute-start.8
  41.4 0.0 collective-permute-done.9.rest_4_
  41.4 0.3 collective-permute-start.15
  41.7 0.0 collective-permute-done.7.rest_2_
  41.7 2.4 %collective-permute-start.17 = (bf16[4,144,512]{2,1,0:T(8,128)(2,1)S(1)}, bf16[4,144,512]{2,1,0:T(8,128)(2,1)}, u32[]{:S(2)}, u32[]{:S(2)}) collective-permute-start(bf16[4,144,512]{2,1,0:T(8,128)(2,1)S(1)} %collective-permute-done.9.rest_4_), channel_id=1, source_target_pairs={{0,2},{2,4},{4,6},{6,0},{1,3},{3,5},{5,7},{7,1},{8,10},{10,12},{12... | collective-permute-start | bytes 1769480 | tf_op jit(solution)/shard_map/ppermute | solution.py:359
  44.1 0.0 collective-permute-done.14.rest_9_
  44.2 0.0 collective-permute-start.18
  44.2 2.0 %tiles.1 = bf16[32,48,128]{2,1,0:T(8,128)(2,1)} custom-call(bf16[48,3072]{1,0:T(8,128)(2,1)} %q_up.1), custom_call_target="tpu_custom_call" | custom-call | tf_op jit(solution)/shard_map/tiles/pallas_call | solution.py:80
  46.1 11.5 %all-to-all-start = ((bf16[32,48,128]{2,1,0:T(8,128)(2,1)}), bf16[32,48,128]{2,1,0:T(8,128)(2,1)S(1)}, u32[]{:S(2)}, u32[]{:S(2)}) async-start(bf16[32,48,128]{2,1,0:T(8,128)(2,1)} %tiles.1), calls=%async_computation | async-start | bytes 786432 | tf_op jit(solution)/shard_map/all_to_all | solution.py:36
  57.7 0.6 broadcast_in_dim.12.refs_8_
  58.3 0.0 collective-permute-done.10.rest_5_
  58.3 0.3 collective-permute-start.11
  58.6 0.0 collective-permute-done.8.rest_3_
  58.6 0.5 collective-permute-start.16
  59.1 0.0 collective-permute-done.15.rest_10_
  59.1 0.1 collective-permute-start.12
  59.2 10.1 %collective-permute-done.17.rest_12_ = bf16[4,144,512]{2,1,0:T(8,128)(2,1)} collective-permute-done((bf16[4,144,512]{2,1,0:T(8,128)(2,1)S(1)}, bf16[4,144,512]{2,1,0:T(8,128)(2,1)}, u32[]{:S(2)}, u32[]{:S(2)}) %collective-permute-start.17) | collective-permute-done | bytes 589856 | tf_op jit(solution)/shard_map/ppermute | solution.py:359
  69.2 0.0 collective-permute-start.19
  69.2 0.0 collective-permute-done.18.rest_13_
  69.2 0.5 collective-permute-start.20
  69.8 0.6 pad_add_fusion.idx
  70.3 0.7 negate_select_fusion
  71.0 1.9 %all-to-all-done.refs_12_ = bf16[32,48,128]{2,1,0:T(8,128)(2,1)S(1)} async-done(((bf16[32,48,128]{2,1,0:T(8,128)(2,1)}), bf16[32,48,128]{2,1,0:T(8,128)(2,1)S(1)}, u32[]{:S(2)}, u32[]{:S(2)}) %all-to-all-start) | async-done | bytes 393248 | tf_op jit(solution)/shard_map/all_to_all | solution.py:36
  73.0 0.7 copy-done
  73.7 2.3 %query.1 = (bf16[16,576]{1,0:T(8,128)(2,1)}, f32[16,640]{1,0:T(8,128)}, bf16[32,16,128]{2,1,0:T(8,128)(2,1)}) custom-call(s32[3]{0:T(128)} %pad_add_fusion.idx, bf16[16,264]{1,0:T(8,128)(2,1)} %united.1.refs_0_, bf16[16,264]{1,0:T(8,128)(2,1)} %copy-done.11, bf16[16,264]{1,0:T(8,128)(2,1)} %copy-done.10, bf16[16,264]{1,0:T(8,128)(2,1)} %copy-done.14, ...), custom_call_target="tpu_custom_call" | custom-call | tf_op jit(solution)/shard_map/query/pallas_call | solution.py:172
  75.9 9.3 %all-to-all-start.1 = ((bf16[32,16,128]{2,1,0:T(8,128)(2,1)}), bf16[32,16,128]{2,1,0:T(8,128)(2,1)S(1)}, u32[]{:S(2)}, u32[]{:S(2)}) async-start(bf16[32,16,128]{2,1,0:T(8,128)(2,1)} %get-tuple-element.7), calls=%async_computation.1 | async-start | bytes 262144 | tf_op jit(solution)/shard_map/all_to_all | solution.py:36
  85.2 0.1 copy.14
  85.3 0.6 reshape.26.table
  85.9 9.9 %all-to-all-done.1.q = bf16[32,16,128]{2,1,0:T(8,128)(2,1)S(1)} async-done(((bf16[32,16,128]{2,1,0:T(8,128)(2,1)}), bf16[32,16,128]{2,1,0:T(8,128)(2,1)S(1)}, u32[]{:S(2)}, u32[]{:S(2)}) %all-to-all-start.1) | async-done | bytes 131104 | tf_op jit(solution)/shard_map/all_to_all | solution.py:36
  95.9 0.0 collective-permute-done.11.rest_6_
  95.9 0.0 collective-permute-done.16.rest_11_
  95.9 0.0 collective-permute-done.12.rest_7_
  95.9 0.0 collective-permute-done.19.rest_14_
  95.9 0.0 collective-permute-done.20.rest_15_
  96.0 0.6 copy-done.7
  96.5 0.2 copy-done.6
  96.7 11.7 %attend.1 = bf16[32,8,640]{2,1,0:T(8,128)(2,1)} custom-call(s32[3]{0:T(128)} %pad_add_fusion.idx, s32[64]{0:T(128)} %reshape.26.table, s32[16]{0:T(128)} %lengths.1, bf16[32,16,128]{2,1,0:T(8,128)(2,1)} %copy-done.7, f32[16,640]{1,0:T(8,128)} %get-tuple-element.8.wide, bf16[512,2048]{1,0:T(8,128)(2,1)} %key_up.1, ...), custom_call_target="tpu_custom_call" | custom-call | tf_op jit(solution)/shard_map/attend/pallas_call | solution.py:297
  108.4 17.8 %all_to_all.20.parts = bf16[32,8,640]{2,1,0:T(8,128)(2,1)} all-to-all(bf16[32,8,640]{2,1,0:T(8,128)(2,1)} %attend.1), channel_id=1, replica_groups=mesh['z'=8,'x'=4,'y'=4,'c'=2] {'z','x'}, dimensions={0} | all-to-all | bytes 655360 | tf_op jit(solution)/shard_map/all_to_all | solution.py:36
  126.3 2.7 %value.1 = bf16[32,8,128]{2,1,0:T(8,128)(2,1)} custom-call(s32[3]{0:T(128)} %pad_add_fusion.idx, bf16[32,8,640]{2,1,0:T(8,128)(2,1)} %all_to_all.20.parts, bf16[512,2048]{1,0:T(8,128)(2,1)} %value_up.1), custom_call_target="tpu_custom_call" | custom-call | tf_op jit(solution)/shard_map/value/pallas_call | solution.py:343
  128.9 13.9 %all_to_all.21 = bf16[32,8,128]{2,1,0:T(8,128)(2,1)S(1)} all-to-all(bf16[32,8,128]{2,1,0:T(8,128)(2,1)} %value.1), channel_id=1, replica_groups=mesh['z'=8,'x'=4,'y'=4,'c'=2] {'z','x'}, dimensions={0} | all-to-all | bytes 131072 | tf_op jit(solution)/shard_map/all_to_all | solution.py:36
  142.8 0.6 copy.16
  (35 shorter events, 0.1 us)
Async XLA Ops:
  2.8 38.3 %copy-start.1 = (bf16[4,144,512]{2,1,0:T(8,128)(2,1)S(1)}, bf16[4,144,512]{2,1,0:T(8,128)(2,1)}, u32[]{:S(2)}) copy-start(bf16[4,144,512]{2,1,0:T(8,128)(2,1)} %get-tuple-element.10.rest_1_) | copy-start | bytes 1769476
  2.8 38.3 %collective-permute-start.13 = (bf16[4,144,512]{2,1,0:T(8,128)(2,1)}, bf16[4,144,512]{2,1,0:T(8,128)(2,1)S(1)}, u32[]{:S(2)}, u32[]{:S(2)}) collective-permute-start(bf16[4,144,512]{2,1,0:T(8,128)(2,1)} %get-tuple-element.9.rest_0_), channel_id=1, source_target_pairs={{0,6},{2,0},{4,2},{6,4},{1,7},{3,1},{5,3},{7,5},{8,14},{10,8},{12,... | collective-permute-start | bytes 1769480 | tf_op jit(solution)/shard_map/ppermute | solution.py:359
  5.1 36.3 %collective-permute-start.9 = (bf16[4,144,512]{2,1,0:T(8,128)(2,1)}, bf16[4,144,512]{2,1,0:T(8,128)(2,1)S(1)}, u32[]{:S(2)}, u32[]{:S(2)}) collective-permute-start(bf16[4,144,512]{2,1,0:T(8,128)(2,1)} %get-tuple-element.9.rest_0_), channel_id=1, source_target_pairs={{0,2},{2,4},{4,6},{6,0},{1,3},{3,5},{5,7},{7,1},{8,10},{10,12},{12... | collective-permute-start | bytes 1769480 | tf_op jit(solution)/shard_map/ppermute | solution.py:359
  5.1 36.6 %collective-permute-start.7 = (bf16[4,144,512]{2,1,0:T(8,128)(2,1)}, bf16[4,144,512]{2,1,0:T(8,128)(2,1)S(1)}, u32[]{:S(2)}, u32[]{:S(2)}) collective-permute-start(bf16[4,144,512]{2,1,0:T(8,128)(2,1)} %get-tuple-element.9.rest_0_), channel_id=1, source_target_pairs={{0,1},{1,0},{2,3},{3,2},{4,5},{5,4},{6,7},{7,6},{8,9},{9,8},{10,11... | collective-permute-start | bytes 1769480 | tf_op jit(solution)/shard_map/ppermute | solution.py:359
  5.1 39.1 %collective-permute-start.14 = (bf16[4,144,512]{2,1,0:T(8,128)(2,1)}, bf16[4,144,512]{2,1,0:T(8,128)(2,1)S(1)}, u32[]{:S(2)}, u32[]{:S(2)}) collective-permute-start(bf16[4,144,512]{2,1,0:T(8,128)(2,1)} %get-tuple-element.10.rest_1_), channel_id=1, source_target_pairs={{0,6},{2,0},{4,2},{6,4},{1,7},{3,1},{5,3},{7,5},{8,14},{10,8},{12,... | collective-permute-start | bytes 1769480 | tf_op jit(solution)/shard_map/ppermute | solution.py:359
  7.1 50.5 %copy-start.17 = (s32[16]{0:T(128)S(1)}, s32[16]{0:T(128)}, u32[]{:S(2)}) copy-start(s32[16]{0:T(128)} %lengths.1) | copy-start | bytes 196
  7.1 50.5 %copy-start.15 = (f32[1536]{0:T(1024)S(1)}, f32[1536]{0:T(1024)}, u32[]{:S(2)}) copy-start(f32[1536]{0:T(1024)} %param.13) | copy-start | bytes 18436
  7.1 78.1 %copy-start.16 = (s32[16,4]{0,1:T(4,128)S(1)}, s32[16,4]{0,1:T(4,128)}, u32[]{:S(2)}) copy-start(s32[16,4]{0,1:T(4,128)} %param.21) | copy-start | bytes 772
  11.4 8.5 %collective-permute-start.5 = (bf16[16,264]{1,0:T(8,128)(2,1)}, bf16[16,264]{1,0:T(8,128)(2,1)S(1)}, u32[]{:S(2)}, u32[]{:S(2)}) collective-permute-start(bf16[16,264]{1,0:T(8,128)(2,1)} %united.1.refs_0_), channel_id=1, source_target_pairs={{6,0},{0,2},{2,4},{4,6},{7,1},{1,3},{3,5},{5,7},{14,8},{8,10},{10,... | collective-permute-start | bytes 25352 | tf_op jit(solution)/shard_map/ppermute | solution.py:359
  19.9 53.0 %copy-start.8 = (bf16[16,264]{1,0:T(8,128)(2,1)}, bf16[16,264]{1,0:T(8,128)(2,1)S(1)}, u32[]{:S(2)}) copy-start(bf16[16,264]{1,0:T(8,128)(2,1)S(1)} %collective-permute-done.5.refs_6_) | copy-start | bytes 25348
  19.9 12.3 %collective-permute-start.3 = (bf16[16,264]{1,0:T(8,128)(2,1)}, bf16[16,264]{1,0:T(8,128)(2,1)S(1)}, u32[]{:S(2)}, u32[]{:S(2)}) collective-permute-start(bf16[16,264]{1,0:T(8,128)(2,1)} %united.1.refs_0_), channel_id=1, source_target_pairs={{4,0},{6,2},{0,4},{2,6},{5,1},{7,3},{1,5},{3,7},{12,8},{14,10},{8,... | collective-permute-start | bytes 25352 | tf_op jit(solution)/shard_map/ppermute | solution.py:359
  32.2 40.7 %copy-start.9 = (bf16[16,264]{1,0:T(8,128)(2,1)}, bf16[16,264]{1,0:T(8,128)(2,1)S(1)}, u32[]{:S(2)}) copy-start(bf16[16,264]{1,0:T(8,128)(2,1)S(1)} %collective-permute-done.3.refs_4_) | copy-start | bytes 25348
  32.2 3.9 %collective-permute-start.1 = (bf16[16,264]{1,0:T(8,128)(2,1)}, bf16[16,264]{1,0:T(8,128)(2,1)S(1)}, u32[]{:S(2)}, u32[]{:S(2)}) collective-permute-start(bf16[16,264]{1,0:T(8,128)(2,1)} %united.1.refs_0_), channel_id=1, source_target_pairs={{2,0},{4,2},{6,4},{0,6},{3,1},{5,3},{7,5},{1,7},{10,8},{12,10},{14... | collective-permute-start | bytes 25352 | tf_op jit(solution)/shard_map/ppermute | solution.py:359
  36.2 36.8 %copy-start.10 = (bf16[16,264]{1,0:T(8,128)(2,1)}, bf16[16,264]{1,0:T(8,128)(2,1)S(1)}, u32[]{:S(2)}) copy-start(bf16[16,264]{1,0:T(8,128)(2,1)S(1)} %collective-permute-done.1.refs_2_) | copy-start | bytes 25348
  36.2 1.4 collective-permute-start
  37.5 35.4 %copy-start.11 = (bf16[16,264]{1,0:T(8,128)(2,1)}, bf16[16,264]{1,0:T(8,128)(2,1)S(1)}, u32[]{:S(2)}) copy-start(bf16[16,264]{1,0:T(8,128)(2,1)S(1)} %collective-permute-done.refs_1_) | copy-start | bytes 25348
  37.5 1.2 collective-permute-start.6
  38.7 34.2 %copy-start.12 = (bf16[16,264]{1,0:T(8,128)(2,1)}, bf16[16,264]{1,0:T(8,128)(2,1)S(1)}, u32[]{:S(2)}) copy-start(bf16[16,264]{1,0:T(8,128)(2,1)S(1)} %collective-permute-done.6.refs_7_) | copy-start | bytes 25348
  38.7 1.2 collective-permute-start.4
  39.9 33.0 %copy-start.13 = (bf16[16,264]{1,0:T(8,128)(2,1)}, bf16[16,264]{1,0:T(8,128)(2,1)S(1)}, u32[]{:S(2)}) copy-start(bf16[16,264]{1,0:T(8,128)(2,1)S(1)} %collective-permute-done.4.refs_5_) | copy-start | bytes 25348
  39.9 1.2 collective-permute-start.2
  41.1 31.9 %copy-start.14 = (bf16[16,264]{1,0:T(8,128)(2,1)}, bf16[16,264]{1,0:T(8,128)(2,1)S(1)}, u32[]{:S(2)}) copy-start(bf16[16,264]{1,0:T(8,128)(2,1)S(1)} %collective-permute-done.2.refs_3_) | copy-start | bytes 25348
  41.1 17.2 %collective-permute-start.10 = (bf16[4,144,512]{2,1,0:T(8,128)(2,1)S(1)}, bf16[4,144,512]{2,1,0:T(8,128)(2,1)}, u32[]{:S(2)}, u32[]{:S(2)}) collective-permute-start(bf16[4,144,512]{2,1,0:T(8,128)(2,1)S(1)} %copy-done.1), channel_id=1, source_target_pairs={{0,2},{2,4},{4,6},{6,0},{1,3},{3,5},{5,7},{7,1},{8,10},{10,12},{12... | collective-permute-start | bytes 1769480 | tf_op jit(solution)/shard_map/ppermute | solution.py:359
  41.1 54.8 %copy-start.2 = (bf16[4,144,512]{2,1,0:T(8,128)(2,1)}, bf16[4,144,512]{2,1,0:T(8,128)(2,1)S(1)}, u32[]{:S(2)}) copy-start(bf16[4,144,512]{2,1,0:T(8,128)(2,1)S(1)} %collective-permute-done.13.rest_8_) | copy-start | bytes 1769476
  41.1 17.5 %collective-permute-start.8 = (bf16[4,144,512]{2,1,0:T(8,128)(2,1)S(1)}, bf16[4,144,512]{2,1,0:T(8,128)(2,1)}, u32[]{:S(2)}, u32[]{:S(2)}) collective-permute-start(bf16[4,144,512]{2,1,0:T(8,128)(2,1)S(1)} %copy-done.1), channel_id=1, source_target_pairs={{0,1},{1,0},{2,3},{3,2},{4,5},{5,4},{6,7},{7,6},{8,9},{9,8},{10,11... | collective-permute-start | bytes 1769480 | tf_op jit(solution)/shard_map/ppermute | solution.py:359
  41.4 54.6 %copy-start.3 = (bf16[4,144,512]{2,1,0:T(8,128)(2,1)}, bf16[4,144,512]{2,1,0:T(8,128)(2,1)S(1)}, u32[]{:S(2)}) copy-start(bf16[4,144,512]{2,1,0:T(8,128)(2,1)S(1)} %collective-permute-done.9.rest_4_) | copy-start | bytes 1769476
  41.4 17.7 %collective-permute-start.15 = (bf16[4,144,512]{2,1,0:T(8,128)(2,1)S(1)}, bf16[4,144,512]{2,1,0:T(8,128)(2,1)}, u32[]{:S(2)}, u32[]{:S(2)}) collective-permute-start(bf16[4,144,512]{2,1,0:T(8,128)(2,1)S(1)} %collective-permute-done.13.rest_8_), channel_id=1, source_target_pairs={{0,1},{1,0},{2,3},{3,2},{4,5},{5,4},{6,7},{7,6},{8,9},{9,8},{10,11... | collective-permute-start | bytes 1769480 | tf_op jit(solution)/shard_map/ppermute | solution.py:359
  41.7 54.2 %copy-start.4 = (bf16[4,144,512]{2,1,0:T(8,128)(2,1)}, bf16[4,144,512]{2,1,0:T(8,128)(2,1)S(1)}, u32[]{:S(2)}) copy-start(bf16[4,144,512]{2,1,0:T(8,128)(2,1)S(1)} %collective-permute-done.7.rest_2_) | copy-start | bytes 1769476
  41.7 27.5 %collective-permute-start.17 = (bf16[4,144,512]{2,1,0:T(8,128)(2,1)S(1)}, bf16[4,144,512]{2,1,0:T(8,128)(2,1)}, u32[]{:S(2)}, u32[]{:S(2)}) collective-permute-start(bf16[4,144,512]{2,1,0:T(8,128)(2,1)S(1)} %collective-permute-done.9.rest_4_), channel_id=1, source_target_pairs={{0,2},{2,4},{4,6},{6,0},{1,3},{3,5},{5,7},{7,1},{8,10},{10,12},{12... | collective-permute-start | bytes 1769480 | tf_op jit(solution)/shard_map/ppermute | solution.py:359
  44.1 51.8 %copy-start.5 = (bf16[4,144,512]{2,1,0:T(8,128)(2,1)}, bf16[4,144,512]{2,1,0:T(8,128)(2,1)S(1)}, u32[]{:S(2)}) copy-start(bf16[4,144,512]{2,1,0:T(8,128)(2,1)S(1)} %collective-permute-done.14.rest_9_) | copy-start | bytes 1769476
  44.2 25.1 %collective-permute-start.18 = (bf16[4,144,512]{2,1,0:T(8,128)(2,1)S(1)}, bf16[4,144,512]{2,1,0:T(8,128)(2,1)}, u32[]{:S(2)}, u32[]{:S(2)}) collective-permute-start(bf16[4,144,512]{2,1,0:T(8,128)(2,1)S(1)} %collective-permute-done.14.rest_9_), channel_id=1, source_target_pairs={{0,6},{2,0},{4,2},{6,4},{1,7},{3,1},{5,3},{7,5},{8,14},{10,8},{12,... | collective-permute-start | bytes 1769480 | tf_op jit(solution)/shard_map/ppermute | solution.py:359
  46.1 26.8 %all-to-all-start = ((bf16[32,48,128]{2,1,0:T(8,128)(2,1)}), bf16[32,48,128]{2,1,0:T(8,128)(2,1)S(1)}, u32[]{:S(2)}, u32[]{:S(2)}) async-start(bf16[32,48,128]{2,1,0:T(8,128)(2,1)} %tiles.1), calls=%async_computation | async-start | bytes 786432 | tf_op jit(solution)/shard_map/all_to_all | solution.py:36
  58.3 37.6 %collective-permute-start.11 = (bf16[4,144,512]{2,1,0:T(8,128)(2,1)S(1)}, bf16[4,144,512]{2,1,0:T(8,128)(2,1)}, u32[]{:S(2)}, u32[]{:S(2)}) collective-permute-start(bf16[4,144,512]{2,1,0:T(8,128)(2,1)S(1)} %collective-permute-done.9.rest_4_), channel_id=1, source_target_pairs={{0,1},{1,0},{2,3},{3,2},{4,5},{5,4},{6,7},{7,6},{8,9},{9,8},{10,11... | collective-permute-start | bytes 1769480 | tf_op jit(solution)/shard_map/ppermute | solution.py:359
  58.6 37.3 %collective-permute-start.16 = (bf16[4,144,512]{2,1,0:T(8,128)(2,1)S(1)}, bf16[4,144,512]{2,1,0:T(8,128)(2,1)S(1)}, u32[]{:S(2)}, u32[]{:S(2)}) collective-permute-start(bf16[4,144,512]{2,1,0:T(8,128)(2,1)S(1)} %collective-permute-done.14.rest_9_), channel_id=1, source_target_pairs={{0,1},{1,0},{2,3},{3,2},{4,5},{5,4},{6,7},{7,6},{8,9},{9,8},{10,11... | collective-permute-start | bytes 1769480 | tf_op jit(solution)/shard_map/ppermute | solution.py:359
  59.1 36.8 %collective-permute-start.12 = (bf16[4,144,512]{2,1,0:T(8,128)(2,1)}, bf16[4,144,512]{2,1,0:T(8,128)(2,1)}, u32[]{:S(2)}, u32[]{:S(2)}) collective-permute-start(bf16[4,144,512]{2,1,0:T(8,128)(2,1)} %collective-permute-done.10.rest_5_), channel_id=1, source_target_pairs={{0,1},{1,0},{2,3},{3,2},{4,5},{5,4},{6,7},{7,6},{8,9},{9,8},{10,11... | collective-permute-start | bytes 1769480 | tf_op jit(solution)/shard_map/ppermute | solution.py:359
  69.2 26.7 %collective-permute-start.19 = (bf16[4,144,512]{2,1,0:T(8,128)(2,1)}, bf16[4,144,512]{2,1,0:T(8,128)(2,1)}, u32[]{:S(2)}, u32[]{:S(2)}) collective-permute-start(bf16[4,144,512]{2,1,0:T(8,128)(2,1)} %collective-permute-done.17.rest_12_), channel_id=1, source_target_pairs={{0,1},{1,0},{2,3},{3,2},{4,5},{5,4},{6,7},{7,6},{8,9},{9,8},{10,11... | collective-permute-start | bytes 1769480 | tf_op jit(solution)/shard_map/ppermute | solution.py:359
  69.2 26.7 %collective-permute-start.20 = (bf16[4,144,512]{2,1,0:T(8,128)(2,1)}, bf16[4,144,512]{2,1,0:T(8,128)(2,1)}, u32[]{:S(2)}, u32[]{:S(2)}) collective-permute-start(bf16[4,144,512]{2,1,0:T(8,128)(2,1)} %collective-permute-done.18.rest_13_), channel_id=1, source_target_pairs={{0,1},{1,0},{2,3},{3,2},{4,5},{5,4},{6,7},{7,6},{8,9},{9,8},{10,11... | collective-permute-start | bytes 1769480 | tf_op jit(solution)/shard_map/ppermute | solution.py:359
  72.9 0.7 copy-start
  75.9 20.0 %all-to-all-start.1 = ((bf16[32,16,128]{2,1,0:T(8,128)(2,1)}), bf16[32,16,128]{2,1,0:T(8,128)(2,1)S(1)}, u32[]{:S(2)}, u32[]{:S(2)}) async-start(bf16[32,16,128]{2,1,0:T(8,128)(2,1)} %get-tuple-element.7), calls=%async_computation.1 | async-start | bytes 262144 | tf_op jit(solution)/shard_map/all_to_all | solution.py:36
  95.9 0.7 copy-start.7
  95.9 0.9 copy-start.6

commit v2 on v1

--- a/solution.py
+++ b/solution.py
@@ -32,6 +32,10 @@
     return pl.BlockSpec(memory_space=space)
 
 
+def here(*values):
+    return tuple(pltpu.with_memory_space_constraint(v, VM) for v in values)
+
+
 def exchange(pieces, axes):
     return lax.all_to_all(pieces, axes, split_axis=0, concat_axis=0, tiled=True)
 
@@ -62,31 +66,17 @@
     cols = down.shape[1]
     return pl.pallas_call(
         united_kernel,
-        out_shape=jax.ShapeDtypeStruct((B, cols), bf16),
+        out_shape=pltpu.VMEM((B, cols), bf16),
         in_specs=[spec(VM), spec(HB)],
         out_specs=spec(VM),
         scratch_shapes=[pltpu.VMEM((UK, cols, D // UK), bf16), pltpu.SemaphoreType.DMA((UK,))],
         name="united",
-    )(hid, down.T)
-
-
-def tiles_kernel(q_up, out):
-    for k in range(32):
-        j = k % 24
-        out[k] = q_up[:, 128 * j : 128 * j + 128]
-
-
-def tiles_call(q_up):
-    return pl.pallas_call(
-        tiles_kernel,
-        out_shape=jax.ShapeDtypeStruct((32, 48, 128), bf16),
-        in_specs=[spec(VM)],
-        out_specs=spec(VM),
-        name="tiles",
-    )(q_up)
-
-
-def pack_kernel(lat, rope, pack_a, pack_b, cache, ropes, sem):
+    )(*here(hid), down.T)
+
+
+def pack_kernel(lat, rope, q_up, pack_a, pack_b, out, cache, ropes, wide_q, sem):
+    fetch_q = pltpu.make_async_copy(q_up, wide_q, sem.at[5])
+    fetch_q.start()
     fetch_rope = pltpu.make_async_copy(rope, ropes, sem.at[0])
     fetch_rope.start()
     fetch = []
@@ -94,6 +84,10 @@
         cp = pltpu.make_async_copy(lat.at[pl.ds(4 * h, 4)], cache.at[pl.ds(4 * h, 4), pl.ds(0, BP), :], sem.at[1 + h])
         cp.start()
         fetch.append(cp)
+    fetch_q.wait()
+    for k in range(32):
+        j = k % 24
+        out[k] = wide_q[:, 128 * j : 128 * j + 128]
     fetch_rope.wait()
     for n in range(8):
         for g in range(4):
@@ -108,20 +102,25 @@
         st.wait()
 
 
-def pack_call(lat, rope):
+def pack_call(lat, rope, q_up):
     half = jax.ShapeDtypeStruct((4, BP + 16, LR), bf16)
     return pl.pallas_call(
         pack_kernel,
-        out_shape=(half, half),
-        in_specs=[spec(HB), spec(HB)],
-        out_specs=(spec(HB), spec(HB)),
+        out_shape=(half, half, pltpu.VMEM((32, 48, 128), bf16)),
+        in_specs=[spec(HB)] * 3,
+        out_specs=(spec(HB), spec(HB), spec(VM)),
         scratch_shapes=[
             pltpu.VMEM((8, BP + 16, LR), bf16),
             pltpu.VMEM((8, ROT, BP), bf16),
-            pltpu.SemaphoreType.DMA((5,)),
+            pltpu.VMEM((48, 3072), bf16),
+            pltpu.SemaphoreType.DMA((6,)),
         ],
         name="pack",
-    )(lat, rope)
+    )(lat, rope, q_up)
+
+
+def place_of():
+    return lax.axis_index("z") * 4 + lax.axis_index("x"), lax.axis_index("y"), lax.axis_index("c")
 
 
 def swapped(x):
@@ -129,9 +128,9 @@
     return jnp.where(lane % ROT < ROT // 2, pltpu.roll(x, 96, 1), pltpu.roll(x, 32, 1))
 
 
-def query_kernel(idx, *refs):
-    pieces, (q_gain, kv_gain, cos, sin, weights, entry, wide, out, parts) = refs[:8], refs[8:]
-    s, y, c = idx[0], idx[1], idx[2]
+def query_kernel(*refs):
+    pieces, (q_gain, kv_gain, cos, sin_part, weights, entry, wide, out, parts) = refs[:8], refs[8:]
+    s, y, c = place_of()
     width = 264
     for i in range(8):
         cp = c if i % 2 == 0 else 1 - c
@@ -152,56 +151,71 @@
     ur = u[:, QR + LR : QR + LR + 128]
     rq = lax.rsqrt(jnp.sum(uq * uq, axis=1, keepdims=True) / QR + 1.0)
     rl = lax.rsqrt(jnp.sum(ul * ul, axis=1, keepdims=True) / LR + 1.0)
-    ql = (uq * rq * q_gain[...]).astype(bf16)
+    ql = (uq * rq * q_gain[...].reshape(1, QR)).astype(bf16)
     q = jnp.dot(ql, weights[...].reshape(QR, 128), preferred_element_type=f32)
     lane = lax.broadcasted_iota(jnp.int32, (B, 128), 1)
+    sin = jnp.where(lane % ROT < ROT // 2, -sin_part[...], sin_part[...])
     kind = lax.rem(s, 3)
     in_rope = ((lane < ROT) & (kind == 1)) | ((lane >= ROT) & (kind == 2))
-    res = jnp.where(in_rope, (q * cos[...] + swapped(q) * sin[...]) * SCALE, q).astype(bf16)
+    res = jnp.where(in_rope, (q * cos[...] + swapped(q) * sin) * SCALE, q).astype(bf16)
     for i in range(32):
         out[i] = res
-    lat = (ul * rl * kv_gain[...]).astype(bf16)
-    rot = jnp.where(lane < ROT, ur * cos[...] + swapped(ur) * sin[...], 0.0).astype(bf16)
+    lat = (ul * rl * kv_gain[...].reshape(1, LR)).astype(bf16)
+    rot = jnp.where(lane < ROT, ur * cos[...] + swapped(ur) * sin, 0.0).astype(bf16)
     entry[:, :LR] = lat
     entry[:, LR:] = rot[:, :ROT]
     wide[:, :LR] = lat.astype(f32)
     wide[:, LR:] = rot.astype(f32)
 
 
-def query_call(idx, parts, q_gain, kv_gain, cos, sin, weights):
+def query_call(parts, q_gain, kv_gain, cos, sin, weights):
     return pl.pallas_call(
         query_kernel,
         out_shape=(
             jax.ShapeDtypeStruct((B, LR + ROT), bf16),
-            jax.ShapeDtypeStruct((B, LR + 128), f32),
-            jax.ShapeDtypeStruct((32, B, 128), bf16),
+            pltpu.VMEM((B, LR + 128), f32),
+            pltpu.VMEM((32, B, 128), bf16),
         ),
-        in_specs=[spec(SM)] + [spec(VM)] * 13,
+        in_specs=[spec(VM)] * 13,
         out_specs=(spec(VM),) * 3,
         scratch_shapes=[pltpu.VMEM((8, B, 264), f32)],
         name="query",
-    )(idx, *parts, q_gain, kv_gain, cos, sin, weights)
+    )(*here(*parts, q_gain, kv_gain, cos, sin, weights))
+
+
+def keys_kernel(src, dst, sem):
+    cp = pltpu.make_async_copy(src, dst, sem)
+    cp.start()
+    cp.wait()
+
+
+def keys_call(key_up):
+    return pl.pallas_call(
+        keys_kernel,
+        out_shape=pltpu.VMEM(key_up.shape, bf16),
+        in_specs=[spec(HB)],
+        out_specs=spec(VM),
+        scratch_shapes=[pltpu.SemaphoreType.DMA],
+        name="keys",
+    )(key_up)
 
 
 ORDER = [(dy, dc, h) for dy in (0, 3, 1, 2) for dc in (0, 1) for h in (0, 1)]
 
 
-def attend_kernel(idx, table, lengths, q, wide, key_up, *rest):
+def attend_kernel(table, lengths, q, wide, keys_v, *rest):
     bufs, out = rest[:16], rest[16]
-    keys_v, kv, q_s, s_s, p_s, o_s, own_s, inv, place, ksem, sem = rest[17:]
-    s, y, c = idx[0], idx[1], idx[2]
-    load_keys = pltpu.make_async_copy(key_up, keys_v, ksem)
-    load_keys.start()
+    kv, q_s, s_s, p_s, o_s, own_s, inv, place, sem = rest[17:]
+    s, y, c = place_of()
     for i in range(16):
         pltpu.make_async_copy(bufs[i], kv.at[pl.ds(4 * i, 4)], sem.at[i // 4]).start()
 
     def fill(e, _):
-        inv[table[e] - s * 64] = e
+        inv[table[e // 4, e % 4] - s * 64] = e
         return 0
 
     lax.fori_loop(0, 64, fill, 0, unroll=8)
     lane = lax.broadcasted_iota(jnp.int32, (B, BP), 1)
-    load_keys.wait()
     for p in range(8):
         t0 = q[3 * p].astype(f32)
         t1 = pltpu.roll(q[3 * p + 1].astype(f32), 64, 1)
@@ -293,14 +307,13 @@
     lax.fori_loop(0, 32, pour, 0, unroll=8)
 
 
-def attend_call(idx, table, lengths, q, wide, key_up, bufs):
+def attend_call(table, lengths, q, wide, key_up, bufs):
     return pl.pallas_call(
         attend_kernel,
-        out_shape=jax.ShapeDtypeStruct((32, 8, LR + 128), bf16),
-        in_specs=[spec(SM)] * 3 + [spec(VM)] * 2 + [spec(HB)] * 17,
+        out_shape=pltpu.VMEM((32, 8, LR + 128), bf16),
+        in_specs=[spec(SM)] * 2 + [spec(VM)] * 3 + [spec(HB)] * 16,
         out_specs=spec(VM),
         scratch_shapes=[
-            pltpu.VMEM((LR, 2048), bf16),
             pltpu.VMEM((64, BP + 16, LR), bf16),
             pltpu.VMEM((B, B, LR + 128), f32),
             pltpu.VMEM((64, B, BP), f32),
@@ -309,15 +322,14 @@
             pltpu.VMEM((B, B, LR), f32),
             pltpu.SMEM((64,), jnp.int32),
             pltpu.SMEM((64,), jnp.int32),
-            pltpu.SemaphoreType.DMA,
             pltpu.SemaphoreType.DMA((4,)),
         ],
         name="attend",
-    )(idx, table, lengths, q, wide, key_up, *bufs)
-
-
-def value_kernel(idx, parts, value_up, out, vals, sem):
-    h = lax.rem(idx[0], 16)
+    )(table, lengths, *here(q, wide, key_up), *bufs)
+
+
+def value_kernel(parts, value_up, out, vals, sem):
+    h = lax.rem(place_of()[0], 16)
     cp = pltpu.make_async_copy(value_up.at[:, pl.ds(pl.multiple_of(h * VD, VD), VD)], vals, sem)
     cp.start()
     tops, tots = [], []
@@ -339,15 +351,15 @@
         out[i] = res
 
 
-def value_call(idx, parts, value_up):
+def value_call(parts, value_up):
     return pl.pallas_call(
         value_kernel,
-        out_shape=jax.ShapeDtypeStruct((32, 8, VD), bf16),
-        in_specs=[spec(SM), spec(VM), spec(HB)],
+        out_shape=pltpu.VMEM((32, 8, VD), bf16),
+        in_specs=[spec(VM), spec(HB)],
         out_specs=spec(VM),
         scratch_shapes=[pltpu.VMEM((LR, VD), bf16), pltpu.SemaphoreType.DMA],
         name="value",
-    )(idx, parts, value_up)
+    )(*here(parts), value_up)
 
 
 UP = [(i, (i + 1) % 4) for i in range(4)]
@@ -360,17 +372,14 @@
 
 
 def body(hidden_in, united_down, q_gain, kv_gain, q_up, key_up, value_up, store, rope_pool, lengths, table):
-    s = lax.axis_index(S)
-    idx = jnp.stack([s, lax.axis_index("y"), lax.axis_index("c")]).astype(jnp.int32)
     lane = jnp.arange(128)
     freq = 10000.0 ** (-2.0 * (lane % 32).astype(f32) / ROT)
     angles = lengths.astype(f32)[:, None] * freq
     cos, sin = jnp.cos(angles), jnp.sin(angles)
-    sin = jnp.where(lane % ROT < ROT // 2, -sin, sin)
-    half_a, half_b = pack_call(store, rope_pool)
+    half_a, half_b, tiles = pack_call(store, rope_pool, q_up)
     up_a = shift(half_a, "y", UP)
     down_b = shift(half_b, "y", DOWN)
-    q_tile = exchange(tiles_call(q_up), S)
+    q_tile = exchange(tiles, S)
     cols = united_call(hidden_in, united_down)
     spread = [cols] + [shift(cols, "y", [((i + d) % 4, i) for i in range(4)]) for d in (1, 2, 3)]
     parts = []
@@ -384,11 +393,11 @@
     bufs = []
     for dy, dc, h in ORDER:
         bufs.append(near[dy][h] if dc == 0 else shift(near[dy][h], "c", SWAP))
-    entry, wide, q_copies = query_call(idx, parts, q_gain[None], kv_gain[None], cos, sin, q_tile)
+    entry, wide, q_copies = query_call(parts, q_gain, kv_gain, cos, sin, q_tile)
     q_all = exchange(q_copies, S)
-    mixed = attend_call(idx, table.reshape(-1), lengths, q_all, wide, key_up, bufs)
+    mixed = attend_call(table, lengths, q_all, wide, keys_call(key_up), bufs)
     spans = exchange(mixed, S)
-    res = value_call(idx, spans, value_up)
+    res = value_call(spans, value_up)
     res = exchange(res, S)
     res = res.reshape(2, 16, 8, VD).transpose(0, 2, 1, 3).reshape(B, 16 * VD)
     return res, entry

time: 144 us -> 134 us (0.931)
  Pallas kernels: 25 us -> 17.2 us
    pallas_call x5, Pallas kernels: 22.8 us -> 16 us  [the longest x1 7.47 us: attend_call(): pl.pallas_call(attend_kernel, out_shape=pltpu.VMEM((32, 8, LR + 128), bf1...]
    ppermute x21, waiting for transfers between devices: 37.9 us -> 40.9 us  [shift(): return lax.ppermute(value, axis, pairs)]
    all_to_all x2, waiting for transfers between devices: 11.8 us -> 9.39 us  [exchange(): return lax.all_to_all(pieces, axes, split_axis=0, concat_axis=0, tiled=True)]
    all_to_all x2, blocking collectives: 31.7 us -> 30.3 us  [exchange(): return lax.all_to_all(pieces, axes, split_axis=0, concat_axis=0, tiled=True)]
    unnamed x38 -> x22, local copies, waits for them, and re-layouts: 2.24 us -> 3.03 us
  transfers between devices with their start and end apart: 23 -> 23, of which waited for: 10 -> 11; matrix products, arithmetic and copies ran while one was open for 2% -> 1% of each run, Pallas kernels for 6% -> 4%
where the time goes in v2:
time: 134 us
  waiting for transfers between devices  50.3 us (38%)
  starting transfers between devices  32 us (24%)
  blocking collectives  30.3 us (23%)
  Pallas kernels  17.2 us (13%)
  local copies, waits for them, and re-layouts  3.03 us (2%)
    ppermute x21, waiting for transfers between devices, shift(): return lax.ppermute(value, axis, pairs)  40.9 us
    all_to_all x2, blocking collectives, exchange(): return lax.all_to_all(pieces, axes, split_axis=0, concat_axis=0, tiled=True)  30.3 us
    all_to_all x2, starting transfers between devices, exchange(): return lax.all_to_all(pieces, axes, split_axis=0, concat_axis=0, tiled=True)  21.7 us
    ppermute x21, starting transfers between devices, shift(): return lax.ppermute(value, axis, pairs)  10.3 us
    all_to_all x2, waiting for transfers between devices, exchange(): return lax.all_to_all(pieces, axes, split_axis=0, concat_axis=0, tiled=True)  9.39 us
    pallas_call x1, Pallas kernels, attend_call(): pl.pallas_call(attend_kernel, out_shape=pltpu.VMEM((32, 8, LR + 128), bf1...  7.47 us
    pallas_call x1, Pallas kernels, pack_call(): pl.pallas_call(pack_kernel, out_shape=(half, half, pltpu.VMEM((32, 48, 12...  3.03 us
    unnamed x22, local copies, waits for them, and re-layouts  3.03 us
  transfers between devices with their start and end apart: 23, of which 11 were waited for; matrix products, arithmetic and copies ran while one was open for 1% of the time, Pallas kernels for 4%

profile of v2, /device:TPU:8, one launch (start us, length us, event | category | flops | bytes accessed | tf_op | source)
XLA Modules:
  0.0 133.7 jit_solution(16598043952812055537)
XLA Ops:
  0.6 0.0 copy-start.1
  0.6 3.0 %pack.1 = (bf16[4,144,512]{2,1,0:T(8,128)(2,1)}, bf16[4,144,512]{2,1,0:T(8,128)(2,1)}, bf16[32,48,128]{2,1,0:T(8,128)(2,1)}) custom-call(bf16[8,128,512]{2,1,0:T(8,128)(2,1)} %lat.1, bf16[8,64,128]{2,1,0:T(8,128)(2,1)} %rope.1, bf16[48,3072]{1,0:T(8,128)(2,1)} %q_up.1), custom_call_target="tpu_custom_call" | custom-call | tf_op jit(solution)/shard_map/pack/pallas_call | solution.py:107
  3.7 0.0 copy-start.9
  3.7 0.0 copy-start.2
  3.7 2.2 %collective-permute-start.13 = (bf16[4,144,512]{2,1,0:T(8,128)(2,1)}, bf16[4,144,512]{2,1,0:T(8,128)(2,1)S(1)}, u32[]{:S(2)}, u32[]{:S(2)}) collective-permute-start(bf16[4,144,512]{2,1,0:T(8,128)(2,1)} %get-tuple-element.11.rest_0_), channel_id=1, source_target_pairs={{0,6},{2,0},{4,2},{6,4},{1,7},{3,1},{5,3},{7,5},{8,14},{10,8},{12,... | collective-permute-start | bytes 1769480 | tf_op jit(solution)/shard_map/ppermute | solution.py:371
  5.9 0.0 collective-permute-start.9
  5.9 0.0 collective-permute-start.7
  5.9 2.0 %collective-permute-start.14 = (bf16[4,144,512]{2,1,0:T(8,128)(2,1)}, bf16[4,144,512]{2,1,0:T(8,128)(2,1)}, u32[]{:S(2)}, u32[]{:S(2)}) collective-permute-start(bf16[4,144,512]{2,1,0:T(8,128)(2,1)} %get-tuple-element.12.rest_1_), channel_id=1, source_target_pairs={{0,6},{2,0},{4,2},{6,4},{1,7},{3,1},{5,3},{7,5},{8,14},{10,8},{12,... | collective-permute-start | bytes 1769480 | tf_op jit(solution)/shard_map/ppermute | solution.py:371
  8.0 0.9 copy-done
  8.9 2.8 %united.1.refs_0_ = bf16[16,264]{1,0:T(8,128)(2,1)S(1)} custom-call(bf16[16,5120]{1,0:T(8,128)(2,1)S(1)} %copy-done, bf16[264,5120]{1,0:T(8,128)(2,1)} %bitcast.6), custom_call_target="tpu_custom_call" | custom-call | tf_op jit(solution)/shard_map/united/pallas_call | solution.py:67
  11.7 0.1 collective-permute-start.5
  11.8 9.0 %collective-permute-done.5.refs_6_ = bf16[16,264]{1,0:T(8,128)(2,1)S(1)} collective-permute-done((bf16[16,264]{1,0:T(8,128)(2,1)S(1)}, bf16[16,264]{1,0:T(8,128)(2,1)S(1)}, u32[]{:S(2)}, u32[]{:S(2)}) %collective-permute-start.5) | collective-permute-done | bytes 8480 | tf_op jit(solution)/shard_map/ppermute | solution.py:371
  20.8 1.3 collective-permute-start.3
  22.1 11.0 %collective-permute-done.3.refs_4_ = bf16[16,264]{1,0:T(8,128)(2,1)S(1)} collective-permute-done((bf16[16,264]{1,0:T(8,128)(2,1)S(1)}, bf16[16,264]{1,0:T(8,128)(2,1)S(1)}, u32[]{:S(2)}, u32[]{:S(2)}) %collective-permute-start.3) | collective-permute-done | bytes 8480 | tf_op jit(solution)/shard_map/ppermute | solution.py:371
  33.1 0.0 collective-permute-start.1
  33.1 3.7 %collective-permute-done.1.refs_2_ = bf16[16,264]{1,0:T(8,128)(2,1)S(1)} collective-permute-done((bf16[16,264]{1,0:T(8,128)(2,1)S(1)}, bf16[16,264]{1,0:T(8,128)(2,1)S(1)}, u32[]{:S(2)}, u32[]{:S(2)}) %collective-permute-start.1) | collective-permute-done | bytes 8480 | tf_op jit(solution)/shard_map/ppermute | solution.py:371
  36.8 0.0 collective-permute-start
  36.8 1.2 collective-permute-done.refs_1_
  38.0 0.2 collective-permute-start.6
  38.1 1.0 collective-permute-done.6.refs_7_
  39.2 0.2 collective-permute-start.4
  39.3 1.0 collective-permute-done.4.refs_5_
  40.3 0.2 collective-permute-start.2
  40.5 1.0 collective-permute-done.2.refs_3_
  41.5 0.0 collective-permute-start.10
  41.5 0.0 collective-permute-done.13.rest_8_
  41.5 0.3 collective-permute-start.8
  41.8 0.0 collective-permute-done.9.rest_4_
  41.8 0.3 collective-permute-start.15
  42.1 0.0 collective-permute-done.7.rest_2_
  42.1 2.4 %collective-permute-start.17 = (bf16[4,144,512]{2,1,0:T(8,128)(2,1)}, bf16[4,144,512]{2,1,0:T(8,128)(2,1)}, u32[]{:S(2)}, u32[]{:S(2)}) collective-permute-start(bf16[4,144,512]{2,1,0:T(8,128)(2,1)} %collective-permute-done.9.rest_4_), channel_id=1, source_target_pairs={{0,2},{2,4},{4,6},{6,0},{1,3},{3,5},{5,7},{7,1},{8,10},{10,12},{12... | collective-permute-start | bytes 1769480 | tf_op jit(solution)/shard_map/ppermute | solution.py:371
  44.6 0.0 collective-permute-done.14.rest_9_
  44.6 0.0 collective-permute-start.18
  44.6 11.5 %all-to-all-start = ((bf16[32,48,128]{2,1,0:T(8,128)(2,1)}), bf16[32,48,128]{2,1,0:T(8,128)(2,1)S(1)}, u32[]{:S(2)}, u32[]{:S(2)}) async-start(bf16[32,48,128]{2,1,0:T(8,128)(2,1)} %get-tuple-element.8), calls=%async_computation | async-start | bytes 786432 | tf_op jit(solution)/shard_map/all_to_all | solution.py:40
  56.1 1.7 %collective-permute-done.10.rest_5_ = bf16[4,144,512]{2,1,0:T(8,128)(2,1)} collective-permute-done((bf16[4,144,512]{2,1,0:T(8,128)(2,1)S(1)}, bf16[4,144,512]{2,1,0:T(8,128)(2,1)}, u32[]{:S(2)}, u32[]{:S(2)}) %collective-permute-start.10) | collective-permute-done | bytes 589856 | tf_op jit(solution)/shard_map/ppermute | solution.py:371
  57.8 0.0 collective-permute-start.11
  57.8 0.0 collective-permute-done.8.rest_3_
  57.8 0.5 collective-permute-start.16
  58.3 0.0 collective-permute-done.15.rest_10_
  58.4 0.1 collective-permute-start.12
  58.4 11.2 %collective-permute-done.17.rest_12_ = bf16[4,144,512]{2,1,0:T(8,128)(2,1)} collective-permute-done((bf16[4,144,512]{2,1,0:T(8,128)(2,1)}, bf16[4,144,512]{2,1,0:T(8,128)(2,1)}, u32[]{:S(2)}, u32[]{:S(2)}) %collective-permute-start.17) | collective-permute-done | bytes 589856 | tf_op jit(solution)/shard_map/ppermute | solution.py:371
  69.7 0.0 collective-permute-start.19
  69.7 0.0 collective-permute-done.18.rest_13_
  69.7 0.5 collective-permute-start.20
  70.2 0.1 multiply_sine_fusion
  70.3 1.0 all-to-all-done.refs_12_
  71.4 0.0 copy-done.6
  71.4 0.0 copy-done.2
  71.4 1.1 query.1
  72.5 10.2 %all-to-all-start.1 = ((bf16[32,16,128]{2,1,0:T(8,128)(2,1)}), bf16[32,16,128]{2,1,0:T(8,128)(2,1)S(1)}, u32[]{:S(2)}, u32[]{:S(2)}) async-start(bf16[32,16,128]{2,1,0:T(8,128)(2,1)} %get-tuple-element.9), calls=%async_computation.1 | async-start | bytes 262144 | tf_op jit(solution)/shard_map/all_to_all | solution.py:40
  82.7 0.7 copy.13.table
  83.4 1.6 %keys.1.keys_v = bf16[512,2048]{1,0:T(8,128)(2,1)S(1)} custom-call(bf16[512,2048]{1,0:T(8,128)(2,1)} %src.1), custom_call_target="tpu_custom_call" | custom-call | tf_op jit(solution)/shard_map/keys/pallas_call | solution.py:193
  85.0 8.3 %all-to-all-done.1.q = bf16[32,16,128]{2,1,0:T(8,128)(2,1)S(1)} async-done(((bf16[32,16,128]{2,1,0:T(8,128)(2,1)}), bf16[32,16,128]{2,1,0:T(8,128)(2,1)S(1)}, u32[]{:S(2)}, u32[]{:S(2)}) %all-to-all-start.1) | async-done | bytes 131104 | tf_op jit(solution)/shard_map/all_to_all | solution.py:40
  93.3 0.0 collective-permute-done.11.rest_6_
  93.3 0.0 collective-permute-done.16.rest_11_
  93.3 0.0 collective-permute-done.12.rest_7_
  93.3 0.0 collective-permute-done.19.rest_14_
  93.4 0.0 collective-permute-done.20.rest_15_
  93.4 0.8 copy-done.7
  94.1 7.5 %attend.1 = bf16[32,8,640]{2,1,0:T(8,128)(2,1)S(1)} custom-call(s32[16,4]{1,0:T(8,128)} %copy.13.table, s32[16]{0:T(128)} %lengths.1, bf16[32,16,128]{2,1,0:T(8,128)(2,1)S(1)} %all-to-all-done.1.q, f32[16,640]{1,0:T(8,128)S(1)} %get-tuple-element.10.wide, bf16[512,2048]{1,0:T(8,128)(2,1)S(1)} %keys.1.keys_v, bf16[4,144,512]{2,1,0:T(8,128)(2,1)} %get-tuple-element.11.rest_0_, ...), custom_call_target="tpu_custom_call" | custom-call | tf_op jit(solution)/shard_map/attend/pallas_call | solution.py:311
  101.6 16.6 %all_to_all.20.parts = bf16[32,8,640]{2,1,0:T(8,128)(2,1)S(1)} all-to-all(bf16[32,8,640]{2,1,0:T(8,128)(2,1)S(1)} %attend.1), channel_id=1, replica_groups=mesh['z'=8,'x'=4,'y'=4,'c'=2] {'z','x'}, dimensions={0} | all-to-all | bytes 655360 | tf_op jit(solution)/shard_map/all_to_all | solution.py:40
  118.2 1.2 value.1
  119.4 13.7 %all_to_all.21 = bf16[32,8,128]{2,1,0:T(8,128)(2,1)S(1)} all-to-all(bf16[32,8,128]{2,1,0:T(8,128)(2,1)S(1)} %value.1), channel_id=1, replica_groups=mesh['z'=8,'x'=4,'y'=4,'c'=2] {'z','x'}, dimensions={0} | all-to-all | bytes 131072 | tf_op jit(solution)/shard_map/all_to_all | solution.py:40
  133.1 0.6 copy.15
  (15 shorter events, 0.0 us)
Async XLA Ops:
  0.6 70.7 %copy-start.1 = (f32[1536]{0:T(1024)S(1)}, f32[1536]{0:T(1024)}, u32[]{:S(2)}) copy-start(f32[1536]{0:T(1024)} %refs_8_.1) | copy-start | bytes 18436
  3.7 52.4 %copy-start.9 = (s32[16]{0:T(128)S(1)}, s32[16]{0:T(128)}, u32[]{:S(2)}) copy-start(s32[16]{0:T(128)} %lengths.1) | copy-start | bytes 196
  3.7 67.7 %copy-start.2 = (f32[512]{0:T(512)S(1)}, f32[512]{0:T(512)}, u32[]{:S(2)}) copy-start(f32[512]{0:T(512)} %refs_9_.1) | copy-start | bytes 6148
  3.7 37.8 %collective-permute-start.13 = (bf16[4,144,512]{2,1,0:T(8,128)(2,1)}, bf16[4,144,512]{2,1,0:T(8,128)(2,1)S(1)}, u32[]{:S(2)}, u32[]{:S(2)}) collective-permute-start(bf16[4,144,512]{2,1,0:T(8,128)(2,1)} %get-tuple-element.11.rest_0_), channel_id=1, source_target_pairs={{0,6},{2,0},{4,2},{6,4},{1,7},{3,1},{5,3},{7,5},{8,14},{10,8},{12,... | collective-permute-start | bytes 1769480 | tf_op jit(solution)/shard_map/ppermute | solution.py:371
  5.9 35.9 %collective-permute-start.9 = (bf16[4,144,512]{2,1,0:T(8,128)(2,1)}, bf16[4,144,512]{2,1,0:T(8,128)(2,1)}, u32[]{:S(2)}, u32[]{:S(2)}) collective-permute-start(bf16[4,144,512]{2,1,0:T(8,128)(2,1)} %get-tuple-element.11.rest_0_), channel_id=1, source_target_pairs={{0,2},{2,4},{4,6},{6,0},{1,3},{3,5},{5,7},{7,1},{8,10},{10,12},{12... | collective-permute-start | bytes 1769480 | tf_op jit(solution)/shard_map/ppermute | solution.py:371
  5.9 36.2 %collective-permute-start.7 = (bf16[4,144,512]{2,1,0:T(8,128)(2,1)}, bf16[4,144,512]{2,1,0:T(8,128)(2,1)S(1)}, u32[]{:S(2)}, u32[]{:S(2)}) collective-permute-start(bf16[4,144,512]{2,1,0:T(8,128)(2,1)} %get-tuple-element.11.rest_0_), channel_id=1, source_target_pairs={{0,1},{1,0},{2,3},{3,2},{4,5},{5,4},{6,7},{7,6},{8,9},{9,8},{10,11... | collective-permute-start | bytes 1769480 | tf_op jit(solution)/shard_map/ppermute | solution.py:371
  5.9 38.6 %collective-permute-start.14 = (bf16[4,144,512]{2,1,0:T(8,128)(2,1)}, bf16[4,144,512]{2,1,0:T(8,128)(2,1)}, u32[]{:S(2)}, u32[]{:S(2)}) collective-permute-start(bf16[4,144,512]{2,1,0:T(8,128)(2,1)} %get-tuple-element.12.rest_1_), channel_id=1, source_target_pairs={{0,6},{2,0},{4,2},{6,4},{1,7},{3,1},{5,3},{7,5},{8,14},{10,8},{12,... | collective-permute-start | bytes 1769480 | tf_op jit(solution)/shard_map/ppermute | solution.py:371
  8.0 0.9 copy-start
  8.9 32.6 %copy-start.3 = (bf16[4,144,512]{2,1,0:T(8,128)(2,1)S(1)}, bf16[4,144,512]{2,1,0:T(8,128)(2,1)}, u32[]{:S(2)}) copy-start(bf16[4,144,512]{2,1,0:T(8,128)(2,1)} %get-tuple-element.12.rest_1_) | copy-start | bytes 1769476
  8.9 73.8 %copy-start.8 = (s32[16,4]{0,1:T(4,128)S(1)}, s32[16,4]{0,1:T(4,128)}, u32[]{:S(2)}) copy-start(s32[16,4]{0,1:T(4,128)} %param.21) | copy-start | bytes 772
  11.7 9.1 %collective-permute-start.5 = (bf16[16,264]{1,0:T(8,128)(2,1)S(1)}, bf16[16,264]{1,0:T(8,128)(2,1)S(1)}, u32[]{:S(2)}, u32[]{:S(2)}) collective-permute-start(bf16[16,264]{1,0:T(8,128)(2,1)S(1)} %united.1.refs_0_), channel_id=1, source_target_pairs={{6,0},{0,2},{2,4},{4,6},{7,1},{1,3},{3,5},{5,7},{14,8},{8,10},{10,... | collective-permute-start | bytes 25352 | tf_op jit(solution)/shard_map/ppermute | solution.py:371
  20.8 12.3 %collective-permute-start.3 = (bf16[16,264]{1,0:T(8,128)(2,1)S(1)}, bf16[16,264]{1,0:T(8,128)(2,1)S(1)}, u32[]{:S(2)}, u32[]{:S(2)}) collective-permute-start(bf16[16,264]{1,0:T(8,128)(2,1)S(1)} %united.1.refs_0_), channel_id=1, source_target_pairs={{4,0},{6,2},{0,4},{2,6},{5,1},{7,3},{1,5},{3,7},{12,8},{14,10},{8,... | collective-permute-start | bytes 25352 | tf_op jit(solution)/shard_map/ppermute | solution.py:371
  33.1 3.7 %collective-permute-start.1 = (bf16[16,264]{1,0:T(8,128)(2,1)S(1)}, bf16[16,264]{1,0:T(8,128)(2,1)S(1)}, u32[]{:S(2)}, u32[]{:S(2)}) collective-permute-start(bf16[16,264]{1,0:T(8,128)(2,1)S(1)} %united.1.refs_0_), channel_id=1, source_target_pairs={{2,0},{4,2},{6,4},{0,6},{3,1},{5,3},{7,5},{1,7},{10,8},{12,10},{14... | collective-permute-start | bytes 25352 | tf_op jit(solution)/shard_map/ppermute | solution.py:371
  36.8 1.2 collective-permute-start
  38.0 1.2 collective-permute-start.6
  39.2 1.2 collective-permute-start.4
  40.3 1.2 collective-permute-start.2
  41.5 16.3 %collective-permute-start.10 = (bf16[4,144,512]{2,1,0:T(8,128)(2,1)S(1)}, bf16[4,144,512]{2,1,0:T(8,128)(2,1)}, u32[]{:S(2)}, u32[]{:S(2)}) collective-permute-start(bf16[4,144,512]{2,1,0:T(8,128)(2,1)S(1)} %copy-done.3), channel_id=1, source_target_pairs={{0,2},{2,4},{4,6},{6,0},{1,3},{3,5},{5,7},{7,1},{8,10},{10,12},{12... | collective-permute-start | bytes 1769480 | tf_op jit(solution)/shard_map/ppermute | solution.py:371
  41.5 41.1 %copy-start.4 = (bf16[4,144,512]{2,1,0:T(8,128)(2,1)}, bf16[4,144,512]{2,1,0:T(8,128)(2,1)S(1)}, u32[]{:S(2)}) copy-start(bf16[4,144,512]{2,1,0:T(8,128)(2,1)S(1)} %collective-permute-done.13.rest_8_) | copy-start | bytes 1769476
  41.5 16.3 %collective-permute-start.8 = (bf16[4,144,512]{2,1,0:T(8,128)(2,1)S(1)}, bf16[4,144,512]{2,1,0:T(8,128)(2,1)S(1)}, u32[]{:S(2)}, u32[]{:S(2)}) collective-permute-start(bf16[4,144,512]{2,1,0:T(8,128)(2,1)S(1)} %copy-done.3), channel_id=1, source_target_pairs={{0,1},{1,0},{2,3},{3,2},{4,5},{5,4},{6,7},{7,6},{8,9},{9,8},{10,11... | collective-permute-start | bytes 1769480 | tf_op jit(solution)/shard_map/ppermute | solution.py:371
  41.8 16.6 %collective-permute-start.15 = (bf16[4,144,512]{2,1,0:T(8,128)(2,1)S(1)}, bf16[4,144,512]{2,1,0:T(8,128)(2,1)}, u32[]{:S(2)}, u32[]{:S(2)}) collective-permute-start(bf16[4,144,512]{2,1,0:T(8,128)(2,1)S(1)} %collective-permute-done.13.rest_8_), channel_id=1, source_target_pairs={{0,1},{1,0},{2,3},{3,2},{4,5},{5,4},{6,7},{7,6},{8,9},{9,8},{10,11... | collective-permute-start | bytes 1769480 | tf_op jit(solution)/shard_map/ppermute | solution.py:371
  42.1 2.4 %copy-start.5 = (bf16[4,144,512]{2,1,0:T(8,128)(2,1)}, bf16[4,144,512]{2,1,0:T(8,128)(2,1)S(1)}, u32[]{:S(2)}) copy-start(bf16[4,144,512]{2,1,0:T(8,128)(2,1)S(1)} %collective-permute-done.7.rest_2_) | copy-start | bytes 1769476
  42.1 27.5 %collective-permute-start.17 = (bf16[4,144,512]{2,1,0:T(8,128)(2,1)}, bf16[4,144,512]{2,1,0:T(8,128)(2,1)}, u32[]{:S(2)}, u32[]{:S(2)}) collective-permute-start(bf16[4,144,512]{2,1,0:T(8,128)(2,1)} %collective-permute-done.9.rest_4_), channel_id=1, source_target_pairs={{0,2},{2,4},{4,6},{6,0},{1,3},{3,5},{5,7},{7,1},{8,10},{10,12},{12... | collective-permute-start | bytes 1769480 | tf_op jit(solution)/shard_map/ppermute | solution.py:371
  44.6 25.1 %collective-permute-start.18 = (bf16[4,144,512]{2,1,0:T(8,128)(2,1)}, bf16[4,144,512]{2,1,0:T(8,128)(2,1)}, u32[]{:S(2)}, u32[]{:S(2)}) collective-permute-start(bf16[4,144,512]{2,1,0:T(8,128)(2,1)} %collective-permute-done.14.rest_9_), channel_id=1, source_target_pairs={{0,6},{2,0},{4,2},{6,4},{1,7},{3,1},{5,3},{7,5},{8,14},{10,8},{12,... | collective-permute-start | bytes 1769480 | tf_op jit(solution)/shard_map/ppermute | solution.py:371
  44.6 26.8 %all-to-all-start = ((bf16[32,48,128]{2,1,0:T(8,128)(2,1)}), bf16[32,48,128]{2,1,0:T(8,128)(2,1)S(1)}, u32[]{:S(2)}, u32[]{:S(2)}) async-start(bf16[32,48,128]{2,1,0:T(8,128)(2,1)} %get-tuple-element.8), calls=%async_computation | async-start | bytes 786432 | tf_op jit(solution)/shard_map/all_to_all | solution.py:40
  57.8 35.5 %collective-permute-start.11 = (bf16[4,144,512]{2,1,0:T(8,128)(2,1)}, bf16[4,144,512]{2,1,0:T(8,128)(2,1)}, u32[]{:S(2)}, u32[]{:S(2)}) collective-permute-start(bf16[4,144,512]{2,1,0:T(8,128)(2,1)} %collective-permute-done.9.rest_4_), channel_id=1, source_target_pairs={{0,1},{1,0},{2,3},{3,2},{4,5},{5,4},{6,7},{7,6},{8,9},{9,8},{10,11... | collective-permute-start | bytes 1769480 | tf_op jit(solution)/shard_map/ppermute | solution.py:371
  57.8 13.5 %copy-start.6 = (bf16[4,144,512]{2,1,0:T(8,128)(2,1)}, bf16[4,144,512]{2,1,0:T(8,128)(2,1)S(1)}, u32[]{:S(2)}) copy-start(bf16[4,144,512]{2,1,0:T(8,128)(2,1)S(1)} %collective-permute-done.8.rest_3_) | copy-start | bytes 1769476
  57.8 35.5 %collective-permute-start.16 = (bf16[4,144,512]{2,1,0:T(8,128)(2,1)}, bf16[4,144,512]{2,1,0:T(8,128)(2,1)S(1)}, u32[]{:S(2)}, u32[]{:S(2)}) collective-permute-start(bf16[4,144,512]{2,1,0:T(8,128)(2,1)} %collective-permute-done.14.rest_9_), channel_id=1, source_target_pairs={{0,1},{1,0},{2,3},{3,2},{4,5},{5,4},{6,7},{7,6},{8,9},{9,8},{10,11... | collective-permute-start | bytes 1769480 | tf_op jit(solution)/shard_map/ppermute | solution.py:371
  58.4 35.0 %collective-permute-start.12 = (bf16[4,144,512]{2,1,0:T(8,128)(2,1)}, bf16[4,144,512]{2,1,0:T(8,128)(2,1)}, u32[]{:S(2)}, u32[]{:S(2)}) collective-permute-start(bf16[4,144,512]{2,1,0:T(8,128)(2,1)} %collective-permute-done.10.rest_5_), channel_id=1, source_target_pairs={{0,1},{1,0},{2,3},{3,2},{4,5},{5,4},{6,7},{7,6},{8,9},{9,8},{10,11... | collective-permute-start | bytes 1769480 | tf_op jit(solution)/shard_map/ppermute | solution.py:371
  69.7 23.7 %collective-permute-start.19 = (bf16[4,144,512]{2,1,0:T(8,128)(2,1)}, bf16[4,144,512]{2,1,0:T(8,128)(2,1)}, u32[]{:S(2)}, u32[]{:S(2)}) collective-permute-start(bf16[4,144,512]{2,1,0:T(8,128)(2,1)} %collective-permute-done.17.rest_12_), channel_id=1, source_target_pairs={{0,1},{1,0},{2,3},{3,2},{4,5},{5,4},{6,7},{7,6},{8,9},{9,8},{10,11... | collective-permute-start | bytes 1769480 | tf_op jit(solution)/shard_map/ppermute | solution.py:371
  69.7 23.7 %collective-permute-start.20 = (bf16[4,144,512]{2,1,0:T(8,128)(2,1)}, bf16[4,144,512]{2,1,0:T(8,128)(2,1)}, u32[]{:S(2)}, u32[]{:S(2)}) collective-permute-start(bf16[4,144,512]{2,1,0:T(8,128)(2,1)} %collective-permute-done.18.rest_13_), channel_id=1, source_target_pairs={{0,1},{1,0},{2,3},{3,2},{4,5},{5,4},{6,7},{7,6},{8,9},{9,8},{10,11... | collective-permute-start | bytes 1769480 | tf_op jit(solution)/shard_map/ppermute | solution.py:371
  72.5 20.8 %all-to-all-start.1 = ((bf16[32,16,128]{2,1,0:T(8,128)(2,1)}), bf16[32,16,128]{2,1,0:T(8,128)(2,1)S(1)}, u32[]{:S(2)}, u32[]{:S(2)}) async-start(bf16[32,16,128]{2,1,0:T(8,128)(2,1)} %get-tuple-element.9), calls=%async_computation.1 | async-start | bytes 262144 | tf_op jit(solution)/shard_map/all_to_all | solution.py:40
  93.3 0.8 copy-start.7

commit v3 on v2

--- a/solution.py
+++ b/solution.py
@@ -43,14 +43,17 @@
 UK = 5
 
 
-def united_kernel(hid, wt, out, wbuf, wsem):
+def united_kernel(hid_hbm, wt, out, hid, wbuf, hsem, wsem):
     step = D // UK
     copies = []
+    fetch = pltpu.make_async_copy(hid_hbm, hid, hsem)
+    fetch.start()
     for k in range(UK):
         cp = pltpu.make_async_copy(wt.at[:, pl.ds(k * step, step)], wbuf.at[k], wsem.at[k])
         cp.start()
         copies.append(cp)
     acc = jnp.zeros(out.shape, f32)
+    fetch.wait()
     for k in range(UK):
         copies[k].wait()
         acc = acc + lax.dot_general(
@@ -67,56 +70,61 @@
     return pl.pallas_call(
         united_kernel,
         out_shape=pltpu.VMEM((B, cols), bf16),
-        in_specs=[spec(VM), spec(HB)],
+        in_specs=[spec(HB), spec(HB)],
         out_specs=spec(VM),
-        scratch_shapes=[pltpu.VMEM((UK, cols, D // UK), bf16), pltpu.SemaphoreType.DMA((UK,))],
+        scratch_shapes=[
+            pltpu.VMEM((B, D), bf16),
+            pltpu.VMEM((UK, cols, D // UK), bf16),
+            pltpu.SemaphoreType.DMA,
+            pltpu.SemaphoreType.DMA((UK,)),
+        ],
         name="united",
-    )(*here(hid), down.T)
-
-
-def pack_kernel(lat, rope, q_up, pack_a, pack_b, out, cache, ropes, wide_q, sem):
-    fetch_q = pltpu.make_async_copy(q_up, wide_q, sem.at[5])
-    fetch_q.start()
+    )(hid, down.T)
+
+
+def tiles_kernel(q_up, out):
+    for k in range(32):
+        j = k % 24
+        out[k] = q_up[:, 128 * j : 128 * j + 128]
+
+
+def tiles_call(q_up):
+    return pl.pallas_call(
+        tiles_kernel,
+        out_shape=pltpu.VMEM((32, 48, 128), bf16),
+        in_specs=[spec(VM)],
+        out_specs=spec(VM),
+        name="tiles",
+    )(*here(q_up))
+
+
+def pack_kernel(lat, rope, pack_a, pack_b, ropes, sem):
     fetch_rope = pltpu.make_async_copy(rope, ropes, sem.at[0])
     fetch_rope.start()
     fetch = []
-    for h in range(2):
-        cp = pltpu.make_async_copy(lat.at[pl.ds(4 * h, 4)], cache.at[pl.ds(4 * h, 4), pl.ds(0, BP), :], sem.at[1 + h])
+    for h, dst in enumerate((pack_a, pack_b)):
+        cp = pltpu.make_async_copy(lat.at[pl.ds(4 * h, 4)], dst.at[:, pl.ds(0, BP), :], sem.at[1 + h])
         cp.start()
         fetch.append(cp)
-    fetch_q.wait()
-    for k in range(32):
-        j = k % 24
-        out[k] = wide_q[:, 128 * j : 128 * j + 128]
     fetch_rope.wait()
     for n in range(8):
+        dst = (pack_a, pack_b)[n // 4]
         for g in range(4):
-            cache[n, BP:, 128 * g : 128 * g + 128] = ropes[n, 16 * g : 16 * g + 16, :]
-    stores = []
-    for h, dst in enumerate((pack_a, pack_b)):
-        fetch[h].wait()
-        st = pltpu.make_async_copy(cache.at[pl.ds(4 * h, 4)], dst, sem.at[3 + h])
-        st.start()
-        stores.append(st)
-    for st in stores:
-        st.wait()
-
-
-def pack_call(lat, rope, q_up):
-    half = jax.ShapeDtypeStruct((4, BP + 16, LR), bf16)
+            dst[n % 4, BP:, 128 * g : 128 * g + 128] = ropes[n, 16 * g : 16 * g + 16, :]
+    for cp in fetch:
+        cp.wait()
+
+
+def pack_call(lat, rope):
+    half = pltpu.VMEM((4, BP + 16, LR), bf16)
     return pl.pallas_call(
         pack_kernel,
-        out_shape=(half, half, pltpu.VMEM((32, 48, 128), bf16)),
-        in_specs=[spec(HB)] * 3,
-        out_specs=(spec(HB), spec(HB), spec(VM)),
-        scratch_shapes=[
-            pltpu.VMEM((8, BP + 16, LR), bf16),
-            pltpu.VMEM((8, ROT, BP), bf16),
-            pltpu.VMEM((48, 3072), bf16),
-            pltpu.SemaphoreType.DMA((6,)),
-        ],
+        out_shape=(half, half),
+        in_specs=[spec(HB)] * 2,
+        out_specs=(spec(VM), spec(VM)),
+        scratch_shapes=[pltpu.VMEM((8, ROT, BP), bf16), pltpu.SemaphoreType.DMA((3,))],
         name="pack",
-    )(lat, rope, q_up)
+    )(lat, rope)
 
 
 def place_of():
@@ -183,38 +191,41 @@
     )(*here(*parts, q_gain, kv_gain, cos, sin, weights))
 
 
-def keys_kernel(src, dst, sem):
+def keys_kernel(table, src, dst, inv, sem):
     cp = pltpu.make_async_copy(src, dst, sem)
     cp.start()
+    base = place_of()[0] * 64
+
+    def fill(b, _):
+        for j in range(4):
+            inv[table[b, j] - base] = b * 4 + j
+        return 0
+
+    lax.fori_loop(0, B, fill, 0, unroll=4)
     cp.wait()
 
 
-def keys_call(key_up):
+def keys_call(table, key_up):
     return pl.pallas_call(
         keys_kernel,
-        out_shape=pltpu.VMEM(key_up.shape, bf16),
-        in_specs=[spec(HB)],
-        out_specs=spec(VM),
+        out_shape=(pltpu.VMEM(key_up.shape, bf16), jax.ShapeDtypeStruct((64,), jnp.int32)),
+        in_specs=[spec(SM), spec(HB)],
+        out_specs=(spec(VM), spec(SM)),
         scratch_shapes=[pltpu.SemaphoreType.DMA],
         name="keys",
-    )(key_up)
+    )(table, key_up)
 
 
 ORDER = [(dy, dc, h) for dy in (0, 3, 1, 2) for dc in (0, 1) for h in (0, 1)]
 
 
-def attend_kernel(table, lengths, q, wide, keys_v, *rest):
+def attend_kernel(inv, lengths, q, wide, keys_v, *rest):
     bufs, out = rest[:16], rest[16]
-    kv, q_s, s_s, p_s, o_s, own_s, inv, place, sem = rest[17:]
+    kv, q_s, s_s, p_s, o_s, own_s, place, sem = rest[17:]
     s, y, c = place_of()
     for i in range(16):
         pltpu.make_async_copy(bufs[i], kv.at[pl.ds(4 * i, 4)], sem.at[i // 4]).start()
 
-    def fill(e, _):
-        inv[table[e // 4, e % 4] - s * 64] = e
-        return 0
-
-    lax.fori_loop(0, 64, fill, 0, unroll=8)
     lane = lax.broadcasted_iota(jnp.int32, (B, BP), 1)
     for p in range(8):
         t0 = q[3 * p].astype(f32)
@@ -307,7 +318,7 @@
     lax.fori_loop(0, 32, pour, 0, unroll=8)
 
 
-def attend_call(table, lengths, q, wide, key_up, bufs):
+def attend_call(inv, lengths, q, wide, keys, bufs):
     return pl.pallas_call(
         attend_kernel,
         out_shape=pltpu.VMEM((32, 8, LR + 128), bf16),
@@ -321,11 +332,10 @@
             pltpu.VMEM((32, 8, LR + 128), f32),
             pltpu.VMEM((B, B, LR), f32),
             pltpu.SMEM((64,), jnp.int32),
-            pltpu.SMEM((64,), jnp.int32),
             pltpu.SemaphoreType.DMA((4,)),
         ],
         name="attend",
-    )(table, lengths, *here(q, wide, key_up), *bufs)
+    )(inv, lengths, *here(q, wide, keys), *bufs)
 
 
 def value_kernel(parts, value_up, out, vals, sem):
@@ -376,10 +386,10 @@
     freq = 10000.0 ** (-2.0 * (lane % 32).astype(f32) / ROT)
     angles = lengths.astype(f32)[:, None] * freq
     cos, sin = jnp.cos(angles), jnp.sin(angles)
-    half_a, half_b, tiles = pack_call(store, rope_pool, q_up)
+    half_a, half_b = pack_call(store, rope_pool)
     up_a = shift(half_a, "y", UP)
     down_b = shift(half_b, "y", DOWN)
-    q_tile = exchange(tiles, S)
+    q_tile = exchange(tiles_call(q_up), S)
     cols = united_call(hidden_in, united_down)
     spread = [cols] + [shift(cols, "y", [((i + d) % 4, i) for i in range(4)]) for d in (1, 2, 3)]
     parts = []
@@ -395,7 +405,8 @@
         bufs.append(near[dy][h] if dc == 0 else shift(near[dy][h], "c", SWAP))
     entry, wide, q_copies = query_call(parts, q_gain, kv_gain, cos, sin, q_tile)
     q_all = exchange(q_copies, S)
-    mixed = attend_call(table, lengths, q_all, wide, keys_call(key_up), bufs)
+    keys, inv = keys_call(table, key_up)
+    mixed = attend_call(inv, lengths, q_all, wide, keys, bufs)
     spans = exchange(mixed, S)
     res = value_call(spans, value_up)
     res = exchange(res, S)

time: 134 us -> 133 us (level)
    unnamed x22 -> x20, local copies, waits for them, and re-layouts: 3.03 us -> 2.11 us
    pallas_call x2 -> x3, Pallas kernels: 4.63 us -> 5.04 us  [the longest x1 2.9 us: keys_call(): pl.pallas_call(keys_kernel, out_shape=(pltpu.VMEM(key_up.shape, bf16), ja...]
  transfers between devices with their start and end apart: 23 -> 23, of which waited for: 11 -> 11; matrix products, arithmetic and copies ran while one was open for 1% -> 1% of each run, Pallas kernels for 4% -> 6%
where the time goes in v3:
time: 133 us; the launch traced here: 132 us
  waiting for transfers between devices  49.3 us (37%)
  starting transfers between devices  31.2 us (23%)
  blocking collectives  30.3 us (23%)
  Pallas kernels  18 us (14%)
  local copies, waits for them, and re-layouts  2.11 us (2%)
    ppermute x21, waiting for transfers between devices, shift(): return lax.ppermute(value, axis, pairs)  40.4 us
    all_to_all x2, blocking collectives, exchange(): return lax.all_to_all(pieces, axes, split_axis=0, concat_axis=0, tiled=True)  30.3 us
    all_to_all x2, starting transfers between devices, exchange(): return lax.all_to_all(pieces, axes, split_axis=0, concat_axis=0, tiled=True)  20.9 us
    ppermute x21, starting transfers between devices, shift(): return lax.ppermute(value, axis, pairs)  10.3 us
    all_to_all x2, waiting for transfers between devices, exchange(): return lax.all_to_all(pieces, axes, split_axis=0, concat_axis=0, tiled=True)  8.89 us
    pallas_call x1, Pallas kernels, attend_call(): pl.pallas_call(attend_kernel, out_shape=pltpu.VMEM((32, 8, LR + 128), bf1...  7.53 us
    pallas_call x1, Pallas kernels, united_call(): pl.pallas_call(united_kernel, out_shape=pltpu.VMEM((B, cols), bf16), in_s...  3.17 us
    pallas_call x1, Pallas kernels, keys_call(): pl.pallas_call(keys_kernel, out_shape=(pltpu.VMEM(key_up.shape, bf16), ja...  2.9 us
  transfers between devices with their start and end apart: 23, of which 11 were waited for; matrix products, arithmetic and copies ran while one was open for 1% of the time, Pallas kernels for 6%

profile of v3, /device:TPU:8, one launch (start us, length us, event | category | flops | bytes accessed | tf_op | source)
XLA Modules:
  0.0 131.8 jit_solution(17296841724585343407)
XLA Ops:
  0.6 0.0 copy-start.2
  0.6 1.3 %pack.1 = (bf16[4,144,512]{2,1,0:T(8,128)(2,1)S(1)}, bf16[4,144,512]{2,1,0:T(8,128)(2,1)S(1)}) custom-call(bf16[8,128,512]{2,1,0:T(8,128)(2,1)} %lat.1, bf16[8,64,128]{2,1,0:T(8,128)(2,1)} %rope.1), custom_call_target="tpu_custom_call" | custom-call | tf_op jit(solution)/shard_map/pack/pallas_call | solution.py:120
  2.0 0.0 copy-start
  2.0 0.0 copy-start.1
  2.0 2.2 %collective-permute-start.13 = (bf16[4,144,512]{2,1,0:T(8,128)(2,1)S(1)}, bf16[4,144,512]{2,1,0:T(8,128)(2,1)S(1)}, u32[]{:S(2)}, u32[]{:S(2)}) collective-permute-start(bf16[4,144,512]{2,1,0:T(8,128)(2,1)S(1)} %get-tuple-element.13.rest_0_), channel_id=1, source_target_pairs={{0,6},{2,0},{4,2},{6,4},{1,7},{3,1},{5,3},{7,5},{8,14},{10,8},{12,... | collective-permute-start | bytes 1769480 | tf_op jit(solution)/shard_map/ppermute | solution.py:381
  4.2 0.0 collective-permute-start.9
  4.2 0.0 collective-permute-start.7
  4.2 2.0 %collective-permute-start.14 = (bf16[4,144,512]{2,1,0:T(8,128)(2,1)S(1)}, bf16[4,144,512]{2,1,0:T(8,128)(2,1)}, u32[]{:S(2)}, u32[]{:S(2)}) collective-permute-start(bf16[4,144,512]{2,1,0:T(8,128)(2,1)S(1)} %get-tuple-element.14.rest_1_), channel_id=1, source_target_pairs={{0,6},{2,0},{4,2},{6,4},{1,7},{3,1},{5,3},{7,5},{8,14},{10,8},{12,... | collective-permute-start | bytes 1769480 | tf_op jit(solution)/shard_map/ppermute | solution.py:381
  6.3 3.2 %united.1.refs_0_ = bf16[16,264]{1,0:T(8,128)(2,1)S(1)} custom-call(bf16[16,5120]{1,0:T(8,128)(2,1)} %hid_hbm.1, bf16[264,5120]{1,0:T(8,128)(2,1)} %bitcast.6), custom_call_target="tpu_custom_call" | custom-call | tf_op jit(solution)/shard_map/united/pallas_call | solution.py:70
  9.5 0.1 collective-permute-start.5
  9.5 9.3 %collective-permute-done.5.refs_6_ = bf16[16,264]{1,0:T(8,128)(2,1)S(1)} collective-permute-done((bf16[16,264]{1,0:T(8,128)(2,1)S(1)}, bf16[16,264]{1,0:T(8,128)(2,1)S(1)}, u32[]{:S(2)}, u32[]{:S(2)}) %collective-permute-start.5) | collective-permute-done | bytes 8480 | tf_op jit(solution)/shard_map/ppermute | solution.py:381
  18.9 1.3 %collective-permute-start.3 = (bf16[16,264]{1,0:T(8,128)(2,1)S(1)}, bf16[16,264]{1,0:T(8,128)(2,1)S(1)}, u32[]{:S(2)}, u32[]{:S(2)}) collective-permute-start(bf16[16,264]{1,0:T(8,128)(2,1)S(1)} %united.1.refs_0_), channel_id=1, source_target_pairs={{4,0},{6,2},{0,4},{2,6},{5,1},{7,3},{1,5},{3,7},{12,8},{14,10},{8,... | collective-permute-start | bytes 25352 | tf_op jit(solution)/shard_map/ppermute | solution.py:381
  20.2 11.0 %collective-permute-done.3.refs_4_ = bf16[16,264]{1,0:T(8,128)(2,1)S(1)} collective-permute-done((bf16[16,264]{1,0:T(8,128)(2,1)S(1)}, bf16[16,264]{1,0:T(8,128)(2,1)S(1)}, u32[]{:S(2)}, u32[]{:S(2)}) %collective-permute-start.3) | collective-permute-done | bytes 8480 | tf_op jit(solution)/shard_map/ppermute | solution.py:381
  31.2 0.0 collective-permute-start.1
  31.2 3.7 %collective-permute-done.1.refs_2_ = bf16[16,264]{1,0:T(8,128)(2,1)S(1)} collective-permute-done((bf16[16,264]{1,0:T(8,128)(2,1)S(1)}, bf16[16,264]{1,0:T(8,128)(2,1)S(1)}, u32[]{:S(2)}, u32[]{:S(2)}) %collective-permute-start.1) | collective-permute-done | bytes 8480 | tf_op jit(solution)/shard_map/ppermute | solution.py:381
  34.9 0.0 collective-permute-start
  34.9 1.2 collective-permute-done.refs_1_
  36.1 0.2 collective-permute-start.6
  36.2 1.0 collective-permute-done.6.refs_7_
  37.2 0.2 collective-permute-start.4
  37.4 1.0 collective-permute-done.4.refs_5_
  38.4 0.2 collective-permute-start.2
  38.6 1.0 collective-permute-done.2.refs_3_
  39.6 0.0 collective-permute-start.10
  39.6 0.0 collective-permute-done.13.rest_8_
  39.6 0.3 collective-permute-start.8
  39.9 0.0 collective-permute-done.9.rest_4_
  39.9 0.3 collective-permute-start.15
  40.2 0.0 collective-permute-done.7.rest_2_
  40.2 2.4 %collective-permute-start.17 = (bf16[4,144,512]{2,1,0:T(8,128)(2,1)}, bf16[4,144,512]{2,1,0:T(8,128)(2,1)}, u32[]{:S(2)}, u32[]{:S(2)}) collective-permute-start(bf16[4,144,512]{2,1,0:T(8,128)(2,1)} %collective-permute-done.9.rest_4_), channel_id=1, source_target_pairs={{0,2},{2,4},{4,6},{6,0},{1,3},{3,5},{5,7},{7,1},{8,10},{10,12},{12... | collective-permute-start | bytes 1769480 | tf_op jit(solution)/shard_map/ppermute | solution.py:381
  42.7 0.0 collective-permute-done.14.rest_9_
  42.7 0.0 collective-permute-start.18
  42.7 0.0 copy-done.2
  42.7 0.8 tiles.1
  43.5 11.5 %all-to-all-start = ((bf16[32,48,128]{2,1,0:T(8,128)(2,1)}), bf16[32,48,128]{2,1,0:T(8,128)(2,1)S(1)}, u32[]{:S(2)}, u32[]{:S(2)}) async-start(bf16[32,48,128]{2,1,0:T(8,128)(2,1)} %tiles.1), calls=%async_computation | async-start | bytes 786432 | tf_op jit(solution)/shard_map/all_to_all | solution.py:40
  55.0 0.9 collective-permute-done.10.rest_5_
  55.9 0.0 collective-permute-start.11
  55.9 0.0 collective-permute-done.8.rest_3_
  55.9 0.5 collective-permute-start.16
  56.4 0.0 collective-permute-done.15.rest_10_
  56.4 0.1 collective-permute-start.12
  56.5 11.2 %collective-permute-done.17.rest_12_ = bf16[4,144,512]{2,1,0:T(8,128)(2,1)} collective-permute-done((bf16[4,144,512]{2,1,0:T(8,128)(2,1)}, bf16[4,144,512]{2,1,0:T(8,128)(2,1)}, u32[]{:S(2)}, u32[]{:S(2)}) %collective-permute-start.17) | collective-permute-done | bytes 589856 | tf_op jit(solution)/shard_map/ppermute | solution.py:381
  67.8 0.0 collective-permute-start.19
  67.8 0.0 collective-permute-done.18.rest_13_
  67.8 0.5 collective-permute-start.20
  68.3 0.1 multiply_sine_fusion
  68.4 1.8 %all-to-all-done.refs_12_ = bf16[32,48,128]{2,1,0:T(8,128)(2,1)S(1)} async-done(((bf16[32,48,128]{2,1,0:T(8,128)(2,1)}), bf16[32,48,128]{2,1,0:T(8,128)(2,1)S(1)}, u32[]{:S(2)}, u32[]{:S(2)}) %all-to-all-start) | async-done | bytes 393248 | tf_op jit(solution)/shard_map/all_to_all | solution.py:40
  70.2 0.0 copy-done.3
  70.2 1.1 query.1
  71.4 9.4 %all-to-all-start.1 = ((bf16[32,16,128]{2,1,0:T(8,128)(2,1)}), bf16[32,16,128]{2,1,0:T(8,128)(2,1)S(1)}, u32[]{:S(2)}, u32[]{:S(2)}) async-start(bf16[32,16,128]{2,1,0:T(8,128)(2,1)} %get-tuple-element.10), calls=%async_computation.1 | async-start | bytes 262144 | tf_op jit(solution)/shard_map/all_to_all | solution.py:40
  80.8 0.7 copy.13.table
  81.4 2.9 %keys.1 = (bf16[512,2048]{1,0:T(8,128)(2,1)S(1)}, s32[64]{0:T(128)}) custom-call(s32[16,4]{1,0:T(8,128)} %copy.13.table, bf16[512,2048]{1,0:T(8,128)(2,1)} %src.1), custom_call_target="tpu_custom_call" | custom-call | tf_op jit(solution)/shard_map/keys/pallas_call | solution.py:209
  84.4 7.0 %all-to-all-done.1.q = bf16[32,16,128]{2,1,0:T(8,128)(2,1)S(1)} async-done(((bf16[32,16,128]{2,1,0:T(8,128)(2,1)}), bf16[32,16,128]{2,1,0:T(8,128)(2,1)S(1)}, u32[]{:S(2)}, u32[]{:S(2)}) %all-to-all-start.1) | async-done | bytes 131104 | tf_op jit(solution)/shard_map/all_to_all | solution.py:40
  91.4 0.0 collective-permute-done.11.rest_6_
  91.4 0.0 collective-permute-done.16.rest_11_
  91.4 0.0 collective-permute-done.12.rest_7_
  91.4 0.0 collective-permute-done.19.rest_14_
  91.4 0.0 collective-permute-done.20.rest_15_
  91.4 0.8 copy-done.6
  92.2 7.5 %attend.1 = bf16[32,8,640]{2,1,0:T(8,128)(2,1)S(1)} custom-call(s32[64]{0:T(128)} %get-tuple-element.9.inv, s32[16]{0:T(128)} %lengths.1, bf16[32,16,128]{2,1,0:T(8,128)(2,1)S(1)} %all-to-all-done.1.q, f32[16,640]{1,0:T(8,128)S(1)} %get-tuple-element.11.wide, bf16[512,2048]{1,0:T(8,128)(2,1)S(1)} %get-tuple-element.12.keys_v, bf16[4,144,512]{2,1,0:T(8,128)(2,1)} %copy-done, ...), custom_call_target="tpu_custom_call" | custom-call | tf_op jit(solution)/shard_map/attend/pallas_call | solution.py:322
  99.7 16.6 %all_to_all.20.parts = bf16[32,8,640]{2,1,0:T(8,128)(2,1)S(1)} all-to-all(bf16[32,8,640]{2,1,0:T(8,128)(2,1)S(1)} %attend.1), channel_id=1, replica_groups=mesh['z'=8,'x'=4,'y'=4,'c'=2] {'z','x'}, dimensions={0} | all-to-all | bytes 655360 | tf_op jit(solution)/shard_map/all_to_all | solution.py:40
  116.3 1.2 value.1
  117.5 13.7 %all_to_all.21 = bf16[32,8,128]{2,1,0:T(8,128)(2,1)S(1)} all-to-all(bf16[32,8,128]{2,1,0:T(8,128)(2,1)S(1)} %value.1), channel_id=1, replica_groups=mesh['z'=8,'x'=4,'y'=4,'c'=2] {'z','x'}, dimensions={0} | all-to-all | bytes 131072 | tf_op jit(solution)/shard_map/all_to_all | solution.py:40
  131.2 0.6 copy.15
  (14 shorter events, 0.0 us)
Async XLA Ops:
  0.6 42.0 %copy-start.2 = (bf16[48,3072]{1,0:T(8,128)(2,1)S(1)}, bf16[48,3072]{1,0:T(8,128)(2,1)}, u32[]{:S(2)}) copy-start(bf16[48,3072]{1,0:T(8,128)(2,1)} %q_up.1) | copy-start | bytes 884740
  2.0 41.5 %copy-start = (bf16[4,144,512]{2,1,0:T(8,128)(2,1)}, bf16[4,144,512]{2,1,0:T(8,128)(2,1)S(1)}, u32[]{:S(2)}) copy-start(bf16[4,144,512]{2,1,0:T(8,128)(2,1)S(1)} %get-tuple-element.13.rest_0_) | copy-start | bytes 1769476
  2.0 41.5 %copy-start.1 = (bf16[4,144,512]{2,1,0:T(8,128)(2,1)}, bf16[4,144,512]{2,1,0:T(8,128)(2,1)S(1)}, u32[]{:S(2)}) copy-start(bf16[4,144,512]{2,1,0:T(8,128)(2,1)S(1)} %get-tuple-element.14.rest_1_) | copy-start | bytes 1769476
  2.0 37.6 %collective-permute-start.13 = (bf16[4,144,512]{2,1,0:T(8,128)(2,1)S(1)}, bf16[4,144,512]{2,1,0:T(8,128)(2,1)S(1)}, u32[]{:S(2)}, u32[]{:S(2)}) collective-permute-start(bf16[4,144,512]{2,1,0:T(8,128)(2,1)S(1)} %get-tuple-element.13.rest_0_), channel_id=1, source_target_pairs={{0,6},{2,0},{4,2},{6,4},{1,7},{3,1},{5,3},{7,5},{8,14},{10,8},{12,... | collective-permute-start | bytes 1769480 | tf_op jit(solution)/shard_map/ppermute | solution.py:381
  4.2 35.6 %collective-permute-start.9 = (bf16[4,144,512]{2,1,0:T(8,128)(2,1)S(1)}, bf16[4,144,512]{2,1,0:T(8,128)(2,1)}, u32[]{:S(2)}, u32[]{:S(2)}) collective-permute-start(bf16[4,144,512]{2,1,0:T(8,128)(2,1)S(1)} %get-tuple-element.13.rest_0_), channel_id=1, source_target_pairs={{0,2},{2,4},{4,6},{6,0},{1,3},{3,5},{5,7},{7,1},{8,10},{10,12},{12... | collective-permute-start | bytes 1769480 | tf_op jit(solution)/shard_map/ppermute | solution.py:381
  4.2 36.0 %collective-permute-start.7 = (bf16[4,144,512]{2,1,0:T(8,128)(2,1)S(1)}, bf16[4,144,512]{2,1,0:T(8,128)(2,1)}, u32[]{:S(2)}, u32[]{:S(2)}) collective-permute-start(bf16[4,144,512]{2,1,0:T(8,128)(2,1)S(1)} %get-tuple-element.13.rest_0_), channel_id=1, source_target_pairs={{0,1},{1,0},{2,3},{3,2},{4,5},{5,4},{6,7},{7,6},{8,9},{9,8},{10,11... | collective-permute-start | bytes 1769480 | tf_op jit(solution)/shard_map/ppermute | solution.py:381
  4.2 38.4 %collective-permute-start.14 = (bf16[4,144,512]{2,1,0:T(8,128)(2,1)S(1)}, bf16[4,144,512]{2,1,0:T(8,128)(2,1)}, u32[]{:S(2)}, u32[]{:S(2)}) collective-permute-start(bf16[4,144,512]{2,1,0:T(8,128)(2,1)S(1)} %get-tuple-element.14.rest_1_), channel_id=1, source_target_pairs={{0,6},{2,0},{4,2},{6,4},{1,7},{3,1},{5,3},{7,5},{8,14},{10,8},{12,... | collective-permute-start | bytes 1769480 | tf_op jit(solution)/shard_map/ppermute | solution.py:381
  6.3 48.7 %copy-start.8 = (s32[16]{0:T(128)S(1)}, s32[16]{0:T(128)}, u32[]{:S(2)}) copy-start(s32[16]{0:T(128)} %lengths.1) | copy-start | bytes 196
  6.3 64.0 %copy-start.3 = (f32[1536]{0:T(1024)S(1)}, f32[1536]{0:T(1024)}, u32[]{:S(2)}) copy-start(f32[1536]{0:T(1024)} %refs_8_.1) | copy-start | bytes 18436
  6.3 64.0 %copy-start.4 = (f32[512]{0:T(512)S(1)}, f32[512]{0:T(512)}, u32[]{:S(2)}) copy-start(f32[512]{0:T(512)} %refs_9_.1) | copy-start | bytes 6148
  6.3 74.5 %copy-start.7 = (s32[16,4]{0,1:T(4,128)S(1)}, s32[16,4]{0,1:T(4,128)}, u32[]{:S(2)}) copy-start(s32[16,4]{0,1:T(4,128)} %param.21) | copy-start | bytes 772
  9.5 9.4 %collective-permute-start.5 = (bf16[16,264]{1,0:T(8,128)(2,1)S(1)}, bf16[16,264]{1,0:T(8,128)(2,1)S(1)}, u32[]{:S(2)}, u32[]{:S(2)}) collective-permute-start(bf16[16,264]{1,0:T(8,128)(2,1)S(1)} %united.1.refs_0_), channel_id=1, source_target_pairs={{6,0},{0,2},{2,4},{4,6},{7,1},{1,3},{3,5},{5,7},{14,8},{8,10},{10,... | collective-permute-start | bytes 25352 | tf_op jit(solution)/shard_map/ppermute | solution.py:381
  18.9 12.3 %collective-permute-start.3 = (bf16[16,264]{1,0:T(8,128)(2,1)S(1)}, bf16[16,264]{1,0:T(8,128)(2,1)S(1)}, u32[]{:S(2)}, u32[]{:S(2)}) collective-permute-start(bf16[16,264]{1,0:T(8,128)(2,1)S(1)} %united.1.refs_0_), channel_id=1, source_target_pairs={{4,0},{6,2},{0,4},{2,6},{5,1},{7,3},{1,5},{3,7},{12,8},{14,10},{8,... | collective-permute-start | bytes 25352 | tf_op jit(solution)/shard_map/ppermute | solution.py:381
  31.2 3.7 %collective-permute-start.1 = (bf16[16,264]{1,0:T(8,128)(2,1)S(1)}, bf16[16,264]{1,0:T(8,128)(2,1)S(1)}, u32[]{:S(2)}, u32[]{:S(2)}) collective-permute-start(bf16[16,264]{1,0:T(8,128)(2,1)S(1)} %united.1.refs_0_), channel_id=1, source_target_pairs={{2,0},{4,2},{6,4},{0,6},{3,1},{5,3},{7,5},{1,7},{10,8},{12,10},{14... | collective-permute-start | bytes 25352 | tf_op jit(solution)/shard_map/ppermute | solution.py:381
  34.9 1.2 collective-permute-start
  36.1 1.2 collective-permute-start.6
  37.2 1.2 collective-permute-start.4
  38.4 1.2 collective-permute-start.2
  39.6 16.3 %collective-permute-start.10 = (bf16[4,144,512]{2,1,0:T(8,128)(2,1)S(1)}, bf16[4,144,512]{2,1,0:T(8,128)(2,1)}, u32[]{:S(2)}, u32[]{:S(2)}) collective-permute-start(bf16[4,144,512]{2,1,0:T(8,128)(2,1)S(1)} %get-tuple-element.14.rest_1_), channel_id=1, source_target_pairs={{0,2},{2,4},{4,6},{6,0},{1,3},{3,5},{5,7},{7,1},{8,10},{10,12},{12... | collective-permute-start | bytes 1769480 | tf_op jit(solution)/shard_map/ppermute | solution.py:381
  39.6 30.6 %copy-start.5 = (bf16[4,144,512]{2,1,0:T(8,128)(2,1)}, bf16[4,144,512]{2,1,0:T(8,128)(2,1)S(1)}, u32[]{:S(2)}) copy-start(bf16[4,144,512]{2,1,0:T(8,128)(2,1)S(1)} %collective-permute-done.13.rest_8_) | copy-start | bytes 1769476
  39.6 16.3 %collective-permute-start.8 = (bf16[4,144,512]{2,1,0:T(8,128)(2,1)S(1)}, bf16[4,144,512]{2,1,0:T(8,128)(2,1)}, u32[]{:S(2)}, u32[]{:S(2)}) collective-permute-start(bf16[4,144,512]{2,1,0:T(8,128)(2,1)S(1)} %get-tuple-element.14.rest_1_), channel_id=1, source_target_pairs={{0,1},{1,0},{2,3},{3,2},{4,5},{5,4},{6,7},{7,6},{8,9},{9,8},{10,11... | collective-permute-start | bytes 1769480 | tf_op jit(solution)/shard_map/ppermute | solution.py:381
  39.9 16.6 %collective-permute-start.15 = (bf16[4,144,512]{2,1,0:T(8,128)(2,1)S(1)}, bf16[4,144,512]{2,1,0:T(8,128)(2,1)}, u32[]{:S(2)}, u32[]{:S(2)}) collective-permute-start(bf16[4,144,512]{2,1,0:T(8,128)(2,1)S(1)} %collective-permute-done.13.rest_8_), channel_id=1, source_target_pairs={{0,1},{1,0},{2,3},{3,2},{4,5},{5,4},{6,7},{7,6},{8,9},{9,8},{10,11... | collective-permute-start | bytes 1769480 | tf_op jit(solution)/shard_map/ppermute | solution.py:381
  40.2 27.5 %collective-permute-start.17 = (bf16[4,144,512]{2,1,0:T(8,128)(2,1)}, bf16[4,144,512]{2,1,0:T(8,128)(2,1)}, u32[]{:S(2)}, u32[]{:S(2)}) collective-permute-start(bf16[4,144,512]{2,1,0:T(8,128)(2,1)} %collective-permute-done.9.rest_4_), channel_id=1, source_target_pairs={{0,2},{2,4},{4,6},{6,0},{1,3},{3,5},{5,7},{7,1},{8,10},{10,12},{12... | collective-permute-start | bytes 1769480 | tf_op jit(solution)/shard_map/ppermute | solution.py:381
  42.7 25.1 %collective-permute-start.18 = (bf16[4,144,512]{2,1,0:T(8,128)(2,1)}, bf16[4,144,512]{2,1,0:T(8,128)(2,1)}, u32[]{:S(2)}, u32[]{:S(2)}) collective-permute-start(bf16[4,144,512]{2,1,0:T(8,128)(2,1)} %collective-permute-done.14.rest_9_), channel_id=1, source_target_pairs={{0,6},{2,0},{4,2},{6,4},{1,7},{3,1},{5,3},{7,5},{8,14},{10,8},{12,... | collective-permute-start | bytes 1769480 | tf_op jit(solution)/shard_map/ppermute | solution.py:381
  43.5 26.8 %all-to-all-start = ((bf16[32,48,128]{2,1,0:T(8,128)(2,1)}), bf16[32,48,128]{2,1,0:T(8,128)(2,1)S(1)}, u32[]{:S(2)}, u32[]{:S(2)}) async-start(bf16[32,48,128]{2,1,0:T(8,128)(2,1)} %tiles.1), calls=%async_computation | async-start | bytes 786432 | tf_op jit(solution)/shard_map/all_to_all | solution.py:40
  55.9 35.5 %collective-permute-start.11 = (bf16[4,144,512]{2,1,0:T(8,128)(2,1)}, bf16[4,144,512]{2,1,0:T(8,128)(2,1)S(1)}, u32[]{:S(2)}, u32[]{:S(2)}) collective-permute-start(bf16[4,144,512]{2,1,0:T(8,128)(2,1)} %collective-permute-done.9.rest_4_), channel_id=1, source_target_pairs={{0,1},{1,0},{2,3},{3,2},{4,5},{5,4},{6,7},{7,6},{8,9},{9,8},{10,11... | collective-permute-start | bytes 1769480 | tf_op jit(solution)/shard_map/ppermute | solution.py:381
  55.9 35.5 %collective-permute-start.16 = (bf16[4,144,512]{2,1,0:T(8,128)(2,1)}, bf16[4,144,512]{2,1,0:T(8,128)(2,1)}, u32[]{:S(2)}, u32[]{:S(2)}) collective-permute-start(bf16[4,144,512]{2,1,0:T(8,128)(2,1)} %collective-permute-done.14.rest_9_), channel_id=1, source_target_pairs={{0,1},{1,0},{2,3},{3,2},{4,5},{5,4},{6,7},{7,6},{8,9},{9,8},{10,11... | collective-permute-start | bytes 1769480 | tf_op jit(solution)/shard_map/ppermute | solution.py:381
  56.4 35.0 %collective-permute-start.12 = (bf16[4,144,512]{2,1,0:T(8,128)(2,1)}, bf16[4,144,512]{2,1,0:T(8,128)(2,1)}, u32[]{:S(2)}, u32[]{:S(2)}) collective-permute-start(bf16[4,144,512]{2,1,0:T(8,128)(2,1)} %collective-permute-done.10.rest_5_), channel_id=1, source_target_pairs={{0,1},{1,0},{2,3},{3,2},{4,5},{5,4},{6,7},{7,6},{8,9},{9,8},{10,11... | collective-permute-start | bytes 1769480 | tf_op jit(solution)/shard_map/ppermute | solution.py:381
  67.8 23.7 %collective-permute-start.19 = (bf16[4,144,512]{2,1,0:T(8,128)(2,1)}, bf16[4,144,512]{2,1,0:T(8,128)(2,1)}, u32[]{:S(2)}, u32[]{:S(2)}) collective-permute-start(bf16[4,144,512]{2,1,0:T(8,128)(2,1)} %collective-permute-done.17.rest_12_), channel_id=1, source_target_pairs={{0,1},{1,0},{2,3},{3,2},{4,5},{5,4},{6,7},{7,6},{8,9},{9,8},{10,11... | collective-permute-start | bytes 1769480 | tf_op jit(solution)/shard_map/ppermute | solution.py:381
  67.8 23.7 %collective-permute-start.20 = (bf16[4,144,512]{2,1,0:T(8,128)(2,1)}, bf16[4,144,512]{2,1,0:T(8,128)(2,1)}, u32[]{:S(2)}, u32[]{:S(2)}) collective-permute-start(bf16[4,144,512]{2,1,0:T(8,128)(2,1)} %collective-permute-done.18.rest_13_), channel_id=1, source_target_pairs={{0,1},{1,0},{2,3},{3,2},{4,5},{5,4},{6,7},{7,6},{8,9},{9,8},{10,11... | collective-permute-start | bytes 1769480 | tf_op jit(solution)/shard_map/ppermute | solution.py:381
  71.4 20.0 %all-to-all-start.1 = ((bf16[32,16,128]{2,1,0:T(8,128)(2,1)}), bf16[32,16,128]{2,1,0:T(8,128)(2,1)S(1)}, u32[]{:S(2)}, u32[]{:S(2)}) async-start(bf16[32,16,128]{2,1,0:T(8,128)(2,1)} %get-tuple-element.10), calls=%async_computation.1 | async-start | bytes 262144 | tf_op jit(solution)/shard_map/all_to_all | solution.py:40
  91.4 0.8 copy-start.6

commit v4 on v3

--- a/solution.py
+++ b/solution.py
@@ -191,37 +191,42 @@
     )(*here(*parts, q_gain, kv_gain, cos, sin, weights))
 
 
-def keys_kernel(table, src, dst, inv, sem):
+def keys_kernel(table, lengths, src, dst, slots, sem):
     cp = pltpu.make_async_copy(src, dst, sem)
     cp.start()
-    base = place_of()[0] * 64
+    s = place_of()[0]
 
     def fill(b, _):
+        slots[64 + b] = lengths[b] - s * (4 * BP)
         for j in range(4):
-            inv[table[b, j] - base] = b * 4 + j
+            slots[table[b, j] - s * 64] = b * 4 + j
         return 0
 
     lax.fori_loop(0, B, fill, 0, unroll=4)
+    for i in range(80, 128):
+        slots[i] = 0
     cp.wait()
 
 
-def keys_call(table, key_up):
+def keys_call(table, lengths, key_up):
     return pl.pallas_call(
         keys_kernel,
-        out_shape=(pltpu.VMEM(key_up.shape, bf16), jax.ShapeDtypeStruct((64,), jnp.int32)),
-        in_specs=[spec(SM), spec(HB)],
+        out_shape=(pltpu.VMEM(key_up.shape, bf16), jax.ShapeDtypeStruct((128,), jnp.int32)),
+        in_specs=[spec(SM), spec(SM), spec(HB)],
         out_specs=(spec(VM), spec(SM)),
         scratch_shapes=[pltpu.SemaphoreType.DMA],
         name="keys",
-    )(table, key_up)
+    )(table, lengths, key_up)
 
 
 ORDER = [(dy, dc, h) for dy in (0, 3, 1, 2) for dc in (0, 1) for h in (0, 1)]
 
 
-def attend_kernel(inv, lengths, q, wide, keys_v, *rest):
+def attend_kernel(slots, q, wide, keys_v, *rest):
     bufs, out = rest[:16], rest[16]
-    kv, q_s, s_s, p_s, o_s, own_s, place, sem = rest[17:]
+    kv, q_s, s_s, p_s, o_s, own_s, place, inv, tsem, sem = rest[17:]
+    fetch = pltpu.make_async_copy(slots, inv, tsem)
+    fetch.start()
     s, y, c = place_of()
     for i in range(16):
         pltpu.make_async_copy(bufs[i], kv.at[pl.ds(4 * i, 4)], sem.at[i // 4]).start()
@@ -245,6 +250,8 @@
             q_s[:, h, :LR] = (lat * SCALE).astype(bf16).astype(f32)
             q_s[:, h, LR:] = ropes[j]
 
+    fetch.wait()
+
     def scores(g, _):
         here = kv.at[pl.ds(16 * g, 16)]
         pltpu.make_async_copy(here, here, sem.at[g]).wait()
@@ -268,7 +275,7 @@
 
     def softmax(bh, r):
         b = bh * 8 + r
-        room = lengths[b] - s * (4 * BP)
+        room = inv[64 + b]
         new = jnp.sum(q_s[b] * wide[pl.ds(b, 1), :], axis=1, keepdims=True)
         mine = jnp.full((B, 1), s, jnp.int32) == 0
         live = [lane < room - j * BP for j in range(4)]
@@ -318,11 +325,11 @@
     lax.fori_loop(0, 32, pour, 0, unroll=8)
 
 
-def attend_call(inv, lengths, q, wide, keys, bufs):
+def attend_call(slots, q, wide, keys, bufs):
     return pl.pallas_call(
         attend_kernel,
         out_shape=pltpu.VMEM((32, 8, LR + 128), bf16),
-        in_specs=[spec(SM)] * 2 + [spec(VM)] * 3 + [spec(HB)] * 16,
+        in_specs=[spec(HB)] + [spec(VM)] * 3 + [spec(HB)] * 16,
         out_specs=spec(VM),
         scratch_shapes=[
             pltpu.VMEM((64, BP + 16, LR), bf16),
@@ -332,10 +339,12 @@
             pltpu.VMEM((32, 8, LR + 128), f32),
             pltpu.VMEM((B, B, LR), f32),
             pltpu.SMEM((64,), jnp.int32),
+            pltpu.SMEM((128,), jnp.int32),
+            pltpu.SemaphoreType.DMA,
             pltpu.SemaphoreType.DMA((4,)),
         ],
         name="attend",
-    )(inv, lengths, *here(q, wide, keys), *bufs)
+    )(slots, *here(q, wide, keys), *bufs)
 
 
 def value_kernel(parts, value_up, out, vals, sem):
@@ -405,8 +414,8 @@
         bufs.append(near[dy][h] if dc == 0 else shift(near[dy][h], "c", SWAP))
     entry, wide, q_copies = query_call(parts, q_gain, kv_gain, cos, sin, q_tile)
     q_all = exchange(q_copies, S)
-    keys, inv = keys_call(table, key_up)
-    mixed = attend_call(inv, lengths, q_all, wide, keys, bufs)
+    keys, slots = keys_call(table, lengths, key_up)
+    mixed = attend_call(slots, q_all, wide, keys, bufs)
     spans = exchange(mixed, S)
     res = value_call(spans, value_up)
     res = exchange(res, S)

time: 133 us -> 132 us (level)
  no operation moved by 1% of the time
where the time goes in v4:
time: 132 us; the launch traced here: 131 us
  waiting for transfers between devices  49.3 us (37%)
  starting transfers between devices  31.2 us (24%)
  blocking collectives  30.3 us (23%)
  Pallas kernels  17.5 us (13%)
  local copies, waits for them, and re-layouts  2.11 us (2%)
    ppermute x21, waiting for transfers between devices, shift(): return lax.ppermute(value, axis, pairs)  40.4 us
    all_to_all x2, blocking collectives, exchange(): return lax.all_to_all(pieces, axes, split_axis=0, concat_axis=0, tiled=True)  30.3 us
    all_to_all x2, starting transfers between devices, exchange(): return lax.all_to_all(pieces, axes, split_axis=0, concat_axis=0, tiled=True)  20.9 us
    ppermute x21, starting transfers between devices, shift(): return lax.ppermute(value, axis, pairs)  10.3 us
    all_to_all x2, waiting for transfers between devices, exchange(): return lax.all_to_all(pieces, axes, split_axis=0, concat_axis=0, tiled=True)  8.88 us
    pallas_call x1, Pallas kernels, attend_call(): pl.pallas_call(attend_kernel, out_shape=pltpu.VMEM((32, 8, LR + 128), bf1...  7 us
    pallas_call x1, Pallas kernels, united_call(): pl.pallas_call(united_kernel, out_shape=pltpu.VMEM((B, cols), bf16), in_s...  3.17 us
    pallas_call x1, Pallas kernels, keys_call(): pl.pallas_call(keys_kernel, out_shape=(pltpu.VMEM(key_up.shape, bf16), ja...  2.91 us
  transfers between devices with their start and end apart: 23, of which 11 were waited for; matrix products, arithmetic and copies ran while one was open for 1% of the time, Pallas kernels for 6%

profile of v4, /device:TPU:8, one launch (start us, length us, event | category | flops | bytes accessed | tf_op | source)
XLA Modules:
  0.0 131.3 jit_solution(5082986929195319741)
XLA Ops:
  0.6 0.0 copy-start.2
  0.6 1.3 %pack.1 = (bf16[4,144,512]{2,1,0:T(8,128)(2,1)S(1)}, bf16[4,144,512]{2,1,0:T(8,128)(2,1)S(1)}) custom-call(bf16[8,128,512]{2,1,0:T(8,128)(2,1)} %lat.1, bf16[8,64,128]{2,1,0:T(8,128)(2,1)} %rope.1), custom_call_target="tpu_custom_call" | custom-call | tf_op jit(solution)/shard_map/pack/pallas_call | solution.py:120
  2.0 0.0 copy-start
  2.0 0.0 copy-start.1
  2.0 2.2 %collective-permute-start.13 = (bf16[4,144,512]{2,1,0:T(8,128)(2,1)S(1)}, bf16[4,144,512]{2,1,0:T(8,128)(2,1)S(1)}, u32[]{:S(2)}, u32[]{:S(2)}) collective-permute-start(bf16[4,144,512]{2,1,0:T(8,128)(2,1)S(1)} %get-tuple-element.13.rest_0_), channel_id=1, source_target_pairs={{0,6},{2,0},{4,2},{6,4},{1,7},{3,1},{5,3},{7,5},{8,14},{10,8},{12,... | collective-permute-start | bytes 1769480 | tf_op jit(solution)/shard_map/ppermute | solution.py:390
  4.2 0.0 collective-permute-start.9
  4.2 0.0 collective-permute-start.7
  4.2 2.0 %collective-permute-start.14 = (bf16[4,144,512]{2,1,0:T(8,128)(2,1)S(1)}, bf16[4,144,512]{2,1,0:T(8,128)(2,1)}, u32[]{:S(2)}, u32[]{:S(2)}) collective-permute-start(bf16[4,144,512]{2,1,0:T(8,128)(2,1)S(1)} %get-tuple-element.14.rest_1_), channel_id=1, source_target_pairs={{0,6},{2,0},{4,2},{6,4},{1,7},{3,1},{5,3},{7,5},{8,14},{10,8},{12,... | collective-permute-start | bytes 1769480 | tf_op jit(solution)/shard_map/ppermute | solution.py:390
  6.3 3.2 %united.1.refs_0_ = bf16[16,264]{1,0:T(8,128)(2,1)S(1)} custom-call(bf16[16,5120]{1,0:T(8,128)(2,1)} %hid_hbm.1, bf16[264,5120]{1,0:T(8,128)(2,1)} %bitcast.6), custom_call_target="tpu_custom_call" | custom-call | tf_op jit(solution)/shard_map/united/pallas_call | solution.py:70
  9.5 0.1 collective-permute-start.5
  9.5 9.3 %collective-permute-done.5.refs_6_ = bf16[16,264]{1,0:T(8,128)(2,1)S(1)} collective-permute-done((bf16[16,264]{1,0:T(8,128)(2,1)S(1)}, bf16[16,264]{1,0:T(8,128)(2,1)S(1)}, u32[]{:S(2)}, u32[]{:S(2)}) %collective-permute-start.5) | collective-permute-done | bytes 8480 | tf_op jit(solution)/shard_map/ppermute | solution.py:390
  18.9 1.3 %collective-permute-start.3 = (bf16[16,264]{1,0:T(8,128)(2,1)S(1)}, bf16[16,264]{1,0:T(8,128)(2,1)S(1)}, u32[]{:S(2)}, u32[]{:S(2)}) collective-permute-start(bf16[16,264]{1,0:T(8,128)(2,1)S(1)} %united.1.refs_0_), channel_id=1, source_target_pairs={{4,0},{6,2},{0,4},{2,6},{5,1},{7,3},{1,5},{3,7},{12,8},{14,10},{8,... | collective-permute-start | bytes 25352 | tf_op jit(solution)/shard_map/ppermute | solution.py:390
  20.2 11.0 %collective-permute-done.3.refs_4_ = bf16[16,264]{1,0:T(8,128)(2,1)S(1)} collective-permute-done((bf16[16,264]{1,0:T(8,128)(2,1)S(1)}, bf16[16,264]{1,0:T(8,128)(2,1)S(1)}, u32[]{:S(2)}, u32[]{:S(2)}) %collective-permute-start.3) | collective-permute-done | bytes 8480 | tf_op jit(solution)/shard_map/ppermute | solution.py:390
  31.2 0.0 collective-permute-start.1
  31.2 3.7 %collective-permute-done.1.refs_2_ = bf16[16,264]{1,0:T(8,128)(2,1)S(1)} collective-permute-done((bf16[16,264]{1,0:T(8,128)(2,1)S(1)}, bf16[16,264]{1,0:T(8,128)(2,1)S(1)}, u32[]{:S(2)}, u32[]{:S(2)}) %collective-permute-start.1) | collective-permute-done | bytes 8480 | tf_op jit(solution)/shard_map/ppermute | solution.py:390
  34.9 0.0 collective-permute-start
  34.9 1.2 collective-permute-done.refs_1_
  36.1 0.2 collective-permute-start.6
  36.2 1.0 collective-permute-done.6.refs_7_
  37.2 0.2 collective-permute-start.4
  37.4 1.0 collective-permute-done.4.refs_5_
  38.4 0.2 collective-permute-start.2
  38.6 1.0 collective-permute-done.2.refs_3_
  39.6 0.0 collective-permute-start.10
  39.6 0.0 collective-permute-done.13.rest_8_
  39.6 0.3 collective-permute-start.8
  39.9 0.0 collective-permute-done.9.rest_4_
  39.9 0.3 collective-permute-start.15
  40.2 0.0 collective-permute-done.7.rest_2_
  40.2 2.4 %collective-permute-start.17 = (bf16[4,144,512]{2,1,0:T(8,128)(2,1)}, bf16[4,144,512]{2,1,0:T(8,128)(2,1)}, u32[]{:S(2)}, u32[]{:S(2)}) collective-permute-start(bf16[4,144,512]{2,1,0:T(8,128)(2,1)} %collective-permute-done.9.rest_4_), channel_id=1, source_target_pairs={{0,2},{2,4},{4,6},{6,0},{1,3},{3,5},{5,7},{7,1},{8,10},{10,12},{12... | collective-permute-start | bytes 1769480 | tf_op jit(solution)/shard_map/ppermute | solution.py:390
  42.7 0.0 collective-permute-done.14.rest_9_
  42.7 0.0 collective-permute-start.18
  42.7 0.0 copy-done.2
  42.7 0.8 tiles.1
  43.5 11.5 %all-to-all-start = ((bf16[32,48,128]{2,1,0:T(8,128)(2,1)}), bf16[32,48,128]{2,1,0:T(8,128)(2,1)S(1)}, u32[]{:S(2)}, u32[]{:S(2)}) async-start(bf16[32,48,128]{2,1,0:T(8,128)(2,1)} %tiles.1), calls=%async_computation | async-start | bytes 786432 | tf_op jit(solution)/shard_map/all_to_all | solution.py:40
  55.0 0.9 collective-permute-done.10.rest_5_
  55.9 0.0 collective-permute-start.11
  55.9 0.0 collective-permute-done.8.rest_3_
  55.9 0.5 collective-permute-start.16
  56.4 0.0 collective-permute-done.15.rest_10_
  56.4 0.1 collective-permute-start.12
  56.5 11.2 %collective-permute-done.17.rest_12_ = bf16[4,144,512]{2,1,0:T(8,128)(2,1)} collective-permute-done((bf16[4,144,512]{2,1,0:T(8,128)(2,1)}, bf16[4,144,512]{2,1,0:T(8,128)(2,1)}, u32[]{:S(2)}, u32[]{:S(2)}) %collective-permute-start.17) | collective-permute-done | bytes 589856 | tf_op jit(solution)/shard_map/ppermute | solution.py:390
  67.8 0.0 collective-permute-start.19
  67.8 0.0 collective-permute-done.18.rest_13_
  67.8 0.5 collective-permute-start.20
  68.3 0.1 multiply_sine_fusion
  68.4 1.8 %all-to-all-done.refs_12_ = bf16[32,48,128]{2,1,0:T(8,128)(2,1)S(1)} async-done(((bf16[32,48,128]{2,1,0:T(8,128)(2,1)}), bf16[32,48,128]{2,1,0:T(8,128)(2,1)S(1)}, u32[]{:S(2)}, u32[]{:S(2)}) %all-to-all-start) | async-done | bytes 393248 | tf_op jit(solution)/shard_map/all_to_all | solution.py:40
  70.2 0.0 copy-done.3
  70.2 1.1 query.1
  71.4 9.4 %all-to-all-start.1 = ((bf16[32,16,128]{2,1,0:T(8,128)(2,1)}), bf16[32,16,128]{2,1,0:T(8,128)(2,1)S(1)}, u32[]{:S(2)}, u32[]{:S(2)}) async-start(bf16[32,16,128]{2,1,0:T(8,128)(2,1)} %get-tuple-element.10), calls=%async_computation.1 | async-start | bytes 262144 | tf_op jit(solution)/shard_map/all_to_all | solution.py:40
  80.8 0.7 copy.13.table
  81.4 2.9 %keys.1 = (bf16[512,2048]{1,0:T(8,128)(2,1)S(1)}, s32[128]{0:T(128)}) custom-call(s32[16,4]{1,0:T(8,128)} %copy.13.table, s32[16]{0:T(128)} %lengths.1, bf16[512,2048]{1,0:T(8,128)(2,1)} %src.1), custom_call_target="tpu_custom_call" | custom-call | tf_op jit(solution)/shard_map/keys/pallas_call | solution.py:212
  84.4 7.0 %all-to-all-done.1.q = bf16[32,16,128]{2,1,0:T(8,128)(2,1)S(1)} async-done(((bf16[32,16,128]{2,1,0:T(8,128)(2,1)}), bf16[32,16,128]{2,1,0:T(8,128)(2,1)S(1)}, u32[]{:S(2)}, u32[]{:S(2)}) %all-to-all-start.1) | async-done | bytes 131104 | tf_op jit(solution)/shard_map/all_to_all | solution.py:40
  91.4 0.0 collective-permute-done.11.rest_6_
  91.4 0.0 collective-permute-done.16.rest_11_
  91.4 0.0 collective-permute-done.12.rest_7_
  91.4 0.0 collective-permute-done.19.rest_14_
  91.4 0.0 collective-permute-done.20.rest_15_
  91.4 0.8 copy-done.6
  92.2 7.0 %attend.1 = bf16[32,8,640]{2,1,0:T(8,128)(2,1)S(1)} custom-call(s32[128]{0:T(128)} %get-tuple-element.9.slots, bf16[32,16,128]{2,1,0:T(8,128)(2,1)S(1)} %all-to-all-done.1.q, f32[16,640]{1,0:T(8,128)S(1)} %get-tuple-element.11.wide, bf16[512,2048]{1,0:T(8,128)(2,1)S(1)} %get-tuple-element.12.keys_v, bf16[4,144,512]{2,1,0:T(8,128)(2,1)} %copy-done, ...), custom_call_target="tpu_custom_call" | custom-call | tf_op jit(solution)/shard_map/attend/pallas_call | solution.py:329
  99.2 16.6 %all_to_all.20.parts = bf16[32,8,640]{2,1,0:T(8,128)(2,1)S(1)} all-to-all(bf16[32,8,640]{2,1,0:T(8,128)(2,1)S(1)} %attend.1), channel_id=1, replica_groups=mesh['z'=8,'x'=4,'y'=4,'c'=2] {'z','x'}, dimensions={0} | all-to-all | bytes 655360 | tf_op jit(solution)/shard_map/all_to_all | solution.py:40
  115.8 1.2 value.1
  117.0 13.7 %all_to_all.21 = bf16[32,8,128]{2,1,0:T(8,128)(2,1)S(1)} all-to-all(bf16[32,8,128]{2,1,0:T(8,128)(2,1)S(1)} %value.1), channel_id=1, replica_groups=mesh['z'=8,'x'=4,'y'=4,'c'=2] {'z','x'}, dimensions={0} | all-to-all | bytes 131072 | tf_op jit(solution)/shard_map/all_to_all | solution.py:40
  130.7 0.6 copy.15
  (14 shorter events, 0.0 us)
Async XLA Ops:
  0.6 42.0 %copy-start.2 = (bf16[48,3072]{1,0:T(8,128)(2,1)S(1)}, bf16[48,3072]{1,0:T(8,128)(2,1)}, u32[]{:S(2)}) copy-start(bf16[48,3072]{1,0:T(8,128)(2,1)} %q_up.1) | copy-start | bytes 884740
  2.0 41.5 %copy-start = (bf16[4,144,512]{2,1,0:T(8,128)(2,1)}, bf16[4,144,512]{2,1,0:T(8,128)(2,1)S(1)}, u32[]{:S(2)}) copy-start(bf16[4,144,512]{2,1,0:T(8,128)(2,1)S(1)} %get-tuple-element.13.rest_0_) | copy-start | bytes 1769476
  2.0 41.5 %copy-start.1 = (bf16[4,144,512]{2,1,0:T(8,128)(2,1)}, bf16[4,144,512]{2,1,0:T(8,128)(2,1)S(1)}, u32[]{:S(2)}) copy-start(bf16[4,144,512]{2,1,0:T(8,128)(2,1)S(1)} %get-tuple-element.14.rest_1_) | copy-start | bytes 1769476
  2.0 37.6 %collective-permute-start.13 = (bf16[4,144,512]{2,1,0:T(8,128)(2,1)S(1)}, bf16[4,144,512]{2,1,0:T(8,128)(2,1)S(1)}, u32[]{:S(2)}, u32[]{:S(2)}) collective-permute-start(bf16[4,144,512]{2,1,0:T(8,128)(2,1)S(1)} %get-tuple-element.13.rest_0_), channel_id=1, source_target_pairs={{0,6},{2,0},{4,2},{6,4},{1,7},{3,1},{5,3},{7,5},{8,14},{10,8},{12,... | collective-permute-start | bytes 1769480 | tf_op jit(solution)/shard_map/ppermute | solution.py:390
  4.2 35.6 %collective-permute-start.9 = (bf16[4,144,512]{2,1,0:T(8,128)(2,1)S(1)}, bf16[4,144,512]{2,1,0:T(8,128)(2,1)}, u32[]{:S(2)}, u32[]{:S(2)}) collective-permute-start(bf16[4,144,512]{2,1,0:T(8,128)(2,1)S(1)} %get-tuple-element.13.rest_0_), channel_id=1, source_target_pairs={{0,2},{2,4},{4,6},{6,0},{1,3},{3,5},{5,7},{7,1},{8,10},{10,12},{12... | collective-permute-start | bytes 1769480 | tf_op jit(solution)/shard_map/ppermute | solution.py:390
  4.2 36.0 %collective-permute-start.7 = (bf16[4,144,512]{2,1,0:T(8,128)(2,1)S(1)}, bf16[4,144,512]{2,1,0:T(8,128)(2,1)}, u32[]{:S(2)}, u32[]{:S(2)}) collective-permute-start(bf16[4,144,512]{2,1,0:T(8,128)(2,1)S(1)} %get-tuple-element.13.rest_0_), channel_id=1, source_target_pairs={{0,1},{1,0},{2,3},{3,2},{4,5},{5,4},{6,7},{7,6},{8,9},{9,8},{10,11... | collective-permute-start | bytes 1769480 | tf_op jit(solution)/shard_map/ppermute | solution.py:390
  4.2 38.4 %collective-permute-start.14 = (bf16[4,144,512]{2,1,0:T(8,128)(2,1)S(1)}, bf16[4,144,512]{2,1,0:T(8,128)(2,1)}, u32[]{:S(2)}, u32[]{:S(2)}) collective-permute-start(bf16[4,144,512]{2,1,0:T(8,128)(2,1)S(1)} %get-tuple-element.14.rest_1_), channel_id=1, source_target_pairs={{0,6},{2,0},{4,2},{6,4},{1,7},{3,1},{5,3},{7,5},{8,14},{10,8},{12,... | collective-permute-start | bytes 1769480 | tf_op jit(solution)/shard_map/ppermute | solution.py:390
  6.3 48.7 %copy-start.8 = (s32[16]{0:T(128)S(1)}, s32[16]{0:T(128)}, u32[]{:S(2)}) copy-start(s32[16]{0:T(128)} %lengths.1) | copy-start | bytes 196
  6.3 64.0 %copy-start.3 = (f32[1536]{0:T(1024)S(1)}, f32[1536]{0:T(1024)}, u32[]{:S(2)}) copy-start(f32[1536]{0:T(1024)} %refs_8_.1) | copy-start | bytes 18436
  6.3 64.0 %copy-start.4 = (f32[512]{0:T(512)S(1)}, f32[512]{0:T(512)}, u32[]{:S(2)}) copy-start(f32[512]{0:T(512)} %refs_9_.1) | copy-start | bytes 6148
  6.3 74.5 %copy-start.7 = (s32[16,4]{0,1:T(4,128)S(1)}, s32[16,4]{0,1:T(4,128)}, u32[]{:S(2)}) copy-start(s32[16,4]{0,1:T(4,128)} %param.21) | copy-start | bytes 772
  9.5 9.4 %collective-permute-start.5 = (bf16[16,264]{1,0:T(8,128)(2,1)S(1)}, bf16[16,264]{1,0:T(8,128)(2,1)S(1)}, u32[]{:S(2)}, u32[]{:S(2)}) collective-permute-start(bf16[16,264]{1,0:T(8,128)(2,1)S(1)} %united.1.refs_0_), channel_id=1, source_target_pairs={{6,0},{0,2},{2,4},{4,6},{7,1},{1,3},{3,5},{5,7},{14,8},{8,10},{10,... | collective-permute-start | bytes 25352 | tf_op jit(solution)/shard_map/ppermute | solution.py:390
  18.9 12.3 %collective-permute-start.3 = (bf16[16,264]{1,0:T(8,128)(2,1)S(1)}, bf16[16,264]{1,0:T(8,128)(2,1)S(1)}, u32[]{:S(2)}, u32[]{:S(2)}) collective-permute-start(bf16[16,264]{1,0:T(8,128)(2,1)S(1)} %united.1.refs_0_), channel_id=1, source_target_pairs={{4,0},{6,2},{0,4},{2,6},{5,1},{7,3},{1,5},{3,7},{12,8},{14,10},{8,... | collective-permute-start | bytes 25352 | tf_op jit(solution)/shard_map/ppermute | solution.py:390
  31.2 3.7 %collective-permute-start.1 = (bf16[16,264]{1,0:T(8,128)(2,1)S(1)}, bf16[16,264]{1,0:T(8,128)(2,1)S(1)}, u32[]{:S(2)}, u32[]{:S(2)}) collective-permute-start(bf16[16,264]{1,0:T(8,128)(2,1)S(1)} %united.1.refs_0_), channel_id=1, source_target_pairs={{2,0},{4,2},{6,4},{0,6},{3,1},{5,3},{7,5},{1,7},{10,8},{12,10},{14... | collective-permute-start | bytes 25352 | tf_op jit(solution)/shard_map/ppermute | solution.py:390
  34.9 1.2 collective-permute-start
  36.1 1.2 collective-permute-start.6
  37.2 1.2 collective-permute-start.4
  38.4 1.2 collective-permute-start.2
  39.6 16.3 %collective-permute-start.10 = (bf16[4,144,512]{2,1,0:T(8,128)(2,1)S(1)}, bf16[4,144,512]{2,1,0:T(8,128)(2,1)}, u32[]{:S(2)}, u32[]{:S(2)}) collective-permute-start(bf16[4,144,512]{2,1,0:T(8,128)(2,1)S(1)} %get-tuple-element.14.rest_1_), channel_id=1, source_target_pairs={{0,2},{2,4},{4,6},{6,0},{1,3},{3,5},{5,7},{7,1},{8,10},{10,12},{12... | collective-permute-start | bytes 1769480 | tf_op jit(solution)/shard_map/ppermute | solution.py:390
  39.6 30.6 %copy-start.5 = (bf16[4,144,512]{2,1,0:T(8,128)(2,1)}, bf16[4,144,512]{2,1,0:T(8,128)(2,1)S(1)}, u32[]{:S(2)}) copy-start(bf16[4,144,512]{2,1,0:T(8,128)(2,1)S(1)} %collective-permute-done.13.rest_8_) | copy-start | bytes 1769476
  39.6 16.3 %collective-permute-start.8 = (bf16[4,144,512]{2,1,0:T(8,128)(2,1)S(1)}, bf16[4,144,512]{2,1,0:T(8,128)(2,1)}, u32[]{:S(2)}, u32[]{:S(2)}) collective-permute-start(bf16[4,144,512]{2,1,0:T(8,128)(2,1)S(1)} %get-tuple-element.14.rest_1_), channel_id=1, source_target_pairs={{0,1},{1,0},{2,3},{3,2},{4,5},{5,4},{6,7},{7,6},{8,9},{9,8},{10,11... | collective-permute-start | bytes 1769480 | tf_op jit(solution)/shard_map/ppermute | solution.py:390
  39.9 16.6 %collective-permute-start.15 = (bf16[4,144,512]{2,1,0:T(8,128)(2,1)S(1)}, bf16[4,144,512]{2,1,0:T(8,128)(2,1)}, u32[]{:S(2)}, u32[]{:S(2)}) collective-permute-start(bf16[4,144,512]{2,1,0:T(8,128)(2,1)S(1)} %collective-permute-done.13.rest_8_), channel_id=1, source_target_pairs={{0,1},{1,0},{2,3},{3,2},{4,5},{5,4},{6,7},{7,6},{8,9},{9,8},{10,11... | collective-permute-start | bytes 1769480 | tf_op jit(solution)/shard_map/ppermute | solution.py:390
  40.2 27.5 %collective-permute-start.17 = (bf16[4,144,512]{2,1,0:T(8,128)(2,1)}, bf16[4,144,512]{2,1,0:T(8,128)(2,1)}, u32[]{:S(2)}, u32[]{:S(2)}) collective-permute-start(bf16[4,144,512]{2,1,0:T(8,128)(2,1)} %collective-permute-done.9.rest_4_), channel_id=1, source_target_pairs={{0,2},{2,4},{4,6},{6,0},{1,3},{3,5},{5,7},{7,1},{8,10},{10,12},{12... | collective-permute-start | bytes 1769480 | tf_op jit(solution)/shard_map/ppermute | solution.py:390
  42.7 25.1 %collective-permute-start.18 = (bf16[4,144,512]{2,1,0:T(8,128)(2,1)}, bf16[4,144,512]{2,1,0:T(8,128)(2,1)}, u32[]{:S(2)}, u32[]{:S(2)}) collective-permute-start(bf16[4,144,512]{2,1,0:T(8,128)(2,1)} %collective-permute-done.14.rest_9_), channel_id=1, source_target_pairs={{0,6},{2,0},{4,2},{6,4},{1,7},{3,1},{5,3},{7,5},{8,14},{10,8},{12,... | collective-permute-start | bytes 1769480 | tf_op jit(solution)/shard_map/ppermute | solution.py:390
  43.5 26.8 %all-to-all-start = ((bf16[32,48,128]{2,1,0:T(8,128)(2,1)}), bf16[32,48,128]{2,1,0:T(8,128)(2,1)S(1)}, u32[]{:S(2)}, u32[]{:S(2)}) async-start(bf16[32,48,128]{2,1,0:T(8,128)(2,1)} %tiles.1), calls=%async_computation | async-start | bytes 786432 | tf_op jit(solution)/shard_map/all_to_all | solution.py:40
  55.9 35.5 %collective-permute-start.11 = (bf16[4,144,512]{2,1,0:T(8,128)(2,1)}, bf16[4,144,512]{2,1,0:T(8,128)(2,1)S(1)}, u32[]{:S(2)}, u32[]{:S(2)}) collective-permute-start(bf16[4,144,512]{2,1,0:T(8,128)(2,1)} %collective-permute-done.9.rest_4_), channel_id=1, source_target_pairs={{0,1},{1,0},{2,3},{3,2},{4,5},{5,4},{6,7},{7,6},{8,9},{9,8},{10,11... | collective-permute-start | bytes 1769480 | tf_op jit(solution)/shard_map/ppermute | solution.py:390
  55.9 35.5 %collective-permute-start.16 = (bf16[4,144,512]{2,1,0:T(8,128)(2,1)}, bf16[4,144,512]{2,1,0:T(8,128)(2,1)}, u32[]{:S(2)}, u32[]{:S(2)}) collective-permute-start(bf16[4,144,512]{2,1,0:T(8,128)(2,1)} %collective-permute-done.14.rest_9_), channel_id=1, source_target_pairs={{0,1},{1,0},{2,3},{3,2},{4,5},{5,4},{6,7},{7,6},{8,9},{9,8},{10,11... | collective-permute-start | bytes 1769480 | tf_op jit(solution)/shard_map/ppermute | solution.py:390
  56.4 35.0 %collective-permute-start.12 = (bf16[4,144,512]{2,1,0:T(8,128)(2,1)}, bf16[4,144,512]{2,1,0:T(8,128)(2,1)}, u32[]{:S(2)}, u32[]{:S(2)}) collective-permute-start(bf16[4,144,512]{2,1,0:T(8,128)(2,1)} %collective-permute-done.10.rest_5_), channel_id=1, source_target_pairs={{0,1},{1,0},{2,3},{3,2},{4,5},{5,4},{6,7},{7,6},{8,9},{9,8},{10,11... | collective-permute-start | bytes 1769480 | tf_op jit(solution)/shard_map/ppermute | solution.py:390
  67.8 23.7 %collective-permute-start.19 = (bf16[4,144,512]{2,1,0:T(8,128)(2,1)}, bf16[4,144,512]{2,1,0:T(8,128)(2,1)}, u32[]{:S(2)}, u32[]{:S(2)}) collective-permute-start(bf16[4,144,512]{2,1,0:T(8,128)(2,1)} %collective-permute-done.17.rest_12_), channel_id=1, source_target_pairs={{0,1},{1,0},{2,3},{3,2},{4,5},{5,4},{6,7},{7,6},{8,9},{9,8},{10,11... | collective-permute-start | bytes 1769480 | tf_op jit(solution)/shard_map/ppermute | solution.py:390
  67.8 23.7 %collective-permute-start.20 = (bf16[4,144,512]{2,1,0:T(8,128)(2,1)}, bf16[4,144,512]{2,1,0:T(8,128)(2,1)}, u32[]{:S(2)}, u32[]{:S(2)}) collective-permute-start(bf16[4,144,512]{2,1,0:T(8,128)(2,1)} %collective-permute-done.18.rest_13_), channel_id=1, source_target_pairs={{0,1},{1,0},{2,3},{3,2},{4,5},{5,4},{6,7},{7,6},{8,9},{9,8},{10,11... | collective-permute-start | bytes 1769480 | tf_op jit(solution)/shard_map/ppermute | solution.py:390
  71.4 20.0 %all-to-all-start.1 = ((bf16[32,16,128]{2,1,0:T(8,128)(2,1)}), bf16[32,16,128]{2,1,0:T(8,128)(2,1)S(1)}, u32[]{:S(2)}, u32[]{:S(2)}) async-start(bf16[32,16,128]{2,1,0:T(8,128)(2,1)} %get-tuple-element.10), calls=%async_computation.1 | async-start | bytes 262144 | tf_op jit(solution)/shard_map/all_to_all | solution.py:40
  91.4 0.8 copy-start.6

commit v5 on v4

--- a/solution.py
+++ b/solution.py
@@ -98,31 +98,25 @@
     )(*here(q_up))
 
 
-def pack_kernel(lat, rope, pack_a, pack_b, ropes, sem):
+def pack_kernel(lat, rope, out, ropes, sem):
     fetch_rope = pltpu.make_async_copy(rope, ropes, sem.at[0])
     fetch_rope.start()
-    fetch = []
-    for h, dst in enumerate((pack_a, pack_b)):
-        cp = pltpu.make_async_copy(lat.at[pl.ds(4 * h, 4)], dst.at[:, pl.ds(0, BP), :], sem.at[1 + h])
-        cp.start()
-        fetch.append(cp)
+    fetch = pltpu.make_async_copy(lat, out.at[:, pl.ds(0, BP), :], sem.at[1])
+    fetch.start()
     fetch_rope.wait()
     for n in range(8):
-        dst = (pack_a, pack_b)[n // 4]
         for g in range(4):
-            dst[n % 4, BP:, 128 * g : 128 * g + 128] = ropes[n, 16 * g : 16 * g + 16, :]
-    for cp in fetch:
-        cp.wait()
+            out[n, BP:, 128 * g : 128 * g + 128] = ropes[n, 16 * g : 16 * g + 16, :]
+    fetch.wait()
 
 
 def pack_call(lat, rope):
-    half = pltpu.VMEM((4, BP + 16, LR), bf16)
     return pl.pallas_call(
         pack_kernel,
-        out_shape=(half, half),
+        out_shape=pltpu.VMEM((8, BP + 16, LR), bf16),
         in_specs=[spec(HB)] * 2,
-        out_specs=(spec(VM), spec(VM)),
-        scratch_shapes=[pltpu.VMEM((8, ROT, BP), bf16), pltpu.SemaphoreType.DMA((3,))],
+        out_specs=spec(VM),
+        scratch_shapes=[pltpu.VMEM((8, ROT, BP), bf16), pltpu.SemaphoreType.DMA((2,))],
         name="pack",
     )(lat, rope)
 
@@ -137,12 +131,14 @@
 
 
 def query_kernel(*refs):
-    pieces, (q_gain, kv_gain, cos, sin_part, weights, entry, wide, out, parts) = refs[:8], refs[8:]
+    pairs, (q_gain, kv_gain, cos, sin_part, weights, entry, wide, out, parts) = refs[:4], refs[4:]
     s, y, c = place_of()
     width = 264
-    for i in range(8):
-        cp = c if i % 2 == 0 else 1 - c
-        parts[lax.rem(y + i // 2, 4) * 2 + cp] = pieces[i][...].astype(f32)
+    step = 1 - 2 * c
+    for ref, dy, core in zip(pairs, (0, step, -step, 2), (c, c, 1 - c, c)):
+        at = lax.rem(y + dy + 4, 4) * 2
+        parts[at + core] = ref[0].astype(f32)
+        parts[at + 1 - core] = ref[1].astype(f32)
     tiles = [None] * 17
     for i in range(8):
         piece = parts[i]
@@ -184,16 +180,14 @@
             pltpu.VMEM((B, LR + 128), f32),
             pltpu.VMEM((32, B, 128), bf16),
         ),
-        in_specs=[spec(VM)] * 13,
+        in_specs=[spec(VM)] * 9,
         out_specs=(spec(VM),) * 3,
         scratch_shapes=[pltpu.VMEM((8, B, 264), f32)],
         name="query",
     )(*here(*parts, q_gain, kv_gain, cos, sin, weights))
 
 
-def keys_kernel(table, lengths, src, dst, slots, sem):
-    cp = pltpu.make_async_copy(src, dst, sem)
-    cp.start()
+def slots_kernel(table, lengths, slots):
     s = place_of()[0]
 
     def fill(b, _):
@@ -205,34 +199,37 @@
     lax.fori_loop(0, B, fill, 0, unroll=4)
     for i in range(80, 128):
         slots[i] = 0
-    cp.wait()
-
-
-def keys_call(table, lengths, key_up):
-    return pl.pallas_call(
-        keys_kernel,
-        out_shape=(pltpu.VMEM(key_up.shape, bf16), jax.ShapeDtypeStruct((128,), jnp.int32)),
-        in_specs=[spec(SM), spec(SM), spec(HB)],
-        out_specs=(spec(VM), spec(SM)),
-        scratch_shapes=[pltpu.SemaphoreType.DMA],
-        name="keys",
-    )(table, lengths, key_up)
-
-
-ORDER = [(dy, dc, h) for dy in (0, 3, 1, 2) for dc in (0, 1) for h in (0, 1)]
-
-
-def attend_kernel(slots, q, wide, keys_v, *rest):
-    bufs, out = rest[:16], rest[16]
-    kv, q_s, s_s, p_s, o_s, own_s, place, inv, tsem, sem = rest[17:]
+
+
+def slots_call(table, lengths):
+    return pl.pallas_call(
+        slots_kernel,
+        out_shape=jax.ShapeDtypeStruct((128,), jnp.int32),
+        in_specs=[spec(SM), spec(SM)],
+        out_specs=spec(SM),
+        name="slots",
+    )(table, lengths)
+
+
+def attend_kernel(slots, q, wide, key_up, *rest):
+    bufs, out = rest[:8], rest[8]
+    keys_v, kv, q_s, s_s, p_s, o_s, own_s, place, inv, ksem, tsem, sem = rest[9:]
     fetch = pltpu.make_async_copy(slots, inv, tsem)
     fetch.start()
     s, y, c = place_of()
-    for i in range(16):
-        pltpu.make_async_copy(bufs[i], kv.at[pl.ds(4 * i, 4)], sem.at[i // 4]).start()
+    loads = []
+    for n in range(4):
+        cols = pl.ds(512 * n, 512)
+        cp = pltpu.make_async_copy(key_up.at[:, cols], keys_v.at[:, cols], ksem.at[n])
+        cp.start()
+        loads.append(cp)
+    for i in range(8):
+        pltpu.make_async_copy(bufs[i], kv.at[pl.ds(8 * i, 8)], sem.at[i // 2]).start()
 
     lane = lax.broadcasted_iota(jnp.int32, (B, BP), 1)
     for p in range(8):
+        if p % 2 == 0:
+            loads[p // 2].wait()
         t0 = q[3 * p].astype(f32)
         t1 = pltpu.roll(q[3 * p + 1].astype(f32), 64, 1)
         t2 = pltpu.roll(q[3 * p + 2].astype(f32), 64, 1)
@@ -255,11 +252,11 @@
     def scores(g, _):
         here = kv.at[pl.ds(16 * g, 16)]
         pltpu.make_async_copy(here, here, sem.at[g]).wait()
-        dy = jnp.where(g == 0, 0, jnp.where(g == 1, 3, jnp.where(g == 2, 1, 2)))
-        ys = lax.rem(y + dy, 4)
         for dc in range(2):
             cs = c if dc == 0 else 1 - c
-            first = (ys * 2 + cs) * 8
+            alpha = 3 - 2 * cs
+            dy = jnp.where(g == 0, 0, jnp.where(g == 1, alpha, jnp.where(g == 2, 2, 4 - alpha)))
+            first = (lax.rem(y + dy, 4) * 2 + cs) * 8
             for k in range(8):
                 at = g * 16 + dc * 8 + k
                 e = inv[first + k]
@@ -325,13 +322,14 @@
     lax.fori_loop(0, 32, pour, 0, unroll=8)
 
 
-def attend_call(slots, q, wide, keys, bufs):
+def attend_call(slots, q, wide, key_up, bufs):
     return pl.pallas_call(
         attend_kernel,
         out_shape=pltpu.VMEM((32, 8, LR + 128), bf16),
-        in_specs=[spec(HB)] + [spec(VM)] * 3 + [spec(HB)] * 16,
+        in_specs=[spec(HB)] + [spec(VM)] * 2 + [spec(HB)] * 9,
         out_specs=spec(VM),
         scratch_shapes=[
+            pltpu.VMEM((LR, 2048), bf16),
             pltpu.VMEM((64, BP + 16, LR), bf16),
             pltpu.VMEM((B, B, LR + 128), f32),
             pltpu.VMEM((64, B, BP), f32),
@@ -340,11 +338,12 @@
             pltpu.VMEM((B, B, LR), f32),
             pltpu.SMEM((64,), jnp.int32),
             pltpu.SMEM((128,), jnp.int32),
+            pltpu.SemaphoreType.DMA((4,)),
             pltpu.SemaphoreType.DMA,
             pltpu.SemaphoreType.DMA((4,)),
         ],
         name="attend",
-    )(slots, *here(q, wide, keys), *bufs)
+    )(slots, *here(q, wide), key_up, *(pltpu.with_memory_space_constraint(v, HB) for v in bufs))
 
 
 def value_kernel(parts, value_up, out, vals, sem):
@@ -381,13 +380,9 @@
     )(*here(parts), value_up)
 
 
-UP = [(i, (i + 1) % 4) for i in range(4)]
-DOWN = [(i, (i + 3) % 4) for i in range(4)]
+ALPHA = [(2 * y + c, 2 * ((y + 1 - 2 * c) % 4) + c) for y in range(4) for c in range(2)]
+BETA = [(b, a) for a, b in ALPHA]
 SWAP = [(0, 1), (1, 0)]
-
-
-def shift(value, axis, pairs):
-    return lax.ppermute(value, axis, pairs)
 
 
 def body(hidden_in, united_down, q_gain, kv_gain, q_up, key_up, value_up, store, rope_pool, lengths, table):
@@ -395,27 +390,21 @@
     freq = 10000.0 ** (-2.0 * (lane % 32).astype(f32) / ROT)
     angles = lengths.astype(f32)[:, None] * freq
     cos, sin = jnp.cos(angles), jnp.sin(angles)
-    half_a, half_b = pack_call(store, rope_pool)
-    up_a = shift(half_a, "y", UP)
-    down_b = shift(half_b, "y", DOWN)
+    mine = pack_call(store, rope_pool)
+    alpha = lax.ppermute(mine, T, ALPHA)
+    far = lax.ppermute(alpha, T, ALPHA)
+    beta = lax.ppermute(mine, T, BETA)
     q_tile = exchange(tiles_call(q_up), S)
     cols = united_call(hidden_in, united_down)
-    spread = [cols] + [shift(cols, "y", [((i + d) % 4, i) for i in range(4)]) for d in (1, 2, 3)]
-    parts = []
-    for d in range(4):
-        parts += [spread[d], shift(spread[d], "c", SWAP)]
-    up_b = shift(half_b, "y", UP)
-    down_a = shift(half_a, "y", DOWN)
-    far_a = shift(up_a, "y", UP)
-    far_b = shift(down_b, "y", DOWN)
-    near = {0: (half_a, half_b), 3: (up_a, up_b), 1: (down_a, down_b), 2: (far_a, far_b)}
+    pair = jnp.stack([cols, lax.ppermute(cols, "c", SWAP)])
+    near = lax.ppermute(pair, T, BETA)
+    parts = [pair, near, lax.ppermute(near, "c", SWAP), lax.ppermute(near, T, BETA)]
     bufs = []
-    for dy, dc, h in ORDER:
-        bufs.append(near[dy][h] if dc == 0 else shift(near[dy][h], "c", SWAP))
+    for value in (mine, alpha, far, beta):
+        bufs += [value, lax.ppermute(value, "c", SWAP)]
     entry, wide, q_copies = query_call(parts, q_gain, kv_gain, cos, sin, q_tile)
     q_all = exchange(q_copies, S)
-    keys, slots = keys_call(table, lengths, key_up)
-    mixed = attend_call(slots, q_all, wide, keys, bufs)
+    mixed = attend_call(slots_call(table, lengths), q_all, wide, key_up, bufs)
     spans = exchange(mixed, S)
     res = value_call(spans, value_up)
     res = exchange(res, S)

time: 132 us -> 138 us (1.045)
  waiting for transfers between devices: 49.3 us -> 60.7 us
  starting transfers between devices: 31.2 us -> 24 us
    ppermute x21 -> x11, waiting for transfers between devices: 40.4 us -> 49.5 us  [the longest x1 26.6 us: body(): alpha = lax.ppermute(mine, T, ALPHA)]
    all_to_all x2, starting transfers between devices: 20.9 us -> 16.9 us  [exchange(): return lax.all_to_all(pieces, axes, split_axis=0, concat_axis=0, tiled=True)]
    ppermute x21 -> x11, starting transfers between devices: 10.3 us -> 7.03 us  [the longest x1 1.65 us: body(): alpha = lax.ppermute(mine, T, ALPHA)]
    all_to_all x2, waiting for transfers between devices: 8.88 us -> 11.2 us  [exchange(): return lax.all_to_all(pieces, axes, split_axis=0, concat_axis=0, tiled=True)]
    pallas_call x1, Pallas kernels: 7 us -> 9.35 us  [attend_call(): pl.pallas_call(attend_kernel, out_shape=pltpu.VMEM((32, 8, LR + 128), bf1...]
    pallas_call x2, Pallas kernels: 4.25 us -> 2.84 us  [the longest x1 1.49 us: slots_call(): pl.pallas_call(slots_kernel, out_shape=jax.ShapeDtypeStruct((128,), jnp.i...]
  transfers between devices with their start and end apart: 23 -> 13, of which waited for: 11 -> 8; matrix products, arithmetic and copies ran while one was open for 1% -> 1% of each run, Pallas kernels for 6% -> 5%
where the time goes in v5:
time: 138 us; the launch traced here: 136 us
  waiting for transfers between devices  60.7 us (44%)
  blocking collectives  30.6 us (22%)
  starting transfers between devices  24 us (17%)
  Pallas kernels  18.4 us (13%)
    all_to_all x2, blocking collectives, exchange(): return lax.all_to_all(pieces, axes, split_axis=0, concat_axis=0, tiled=True)  30.6 us
    ppermute x1, waiting for transfers between devices, body(): alpha = lax.ppermute(mine, T, ALPHA)  26.6 us
    all_to_all x2, starting transfers between devices, exchange(): return lax.all_to_all(pieces, axes, split_axis=0, concat_axis=0, tiled=True)  16.9 us
    ppermute x1, waiting for transfers between devices, body(): far = lax.ppermute(alpha, T, ALPHA)  16.4 us
    all_to_all x2, waiting for transfers between devices, exchange(): return lax.all_to_all(pieces, axes, split_axis=0, concat_axis=0, tiled=True)  11.2 us
    pallas_call x1, Pallas kernels, attend_call(): pl.pallas_call(attend_kernel, out_shape=pltpu.VMEM((32, 8, LR + 128), bf1...  9.35 us
    pallas_call x1, Pallas kernels, united_call(): pl.pallas_call(united_kernel, out_shape=pltpu.VMEM((B, cols), bf16), in_s...  3.14 us
  transfers between devices with their start and end apart: 13, of which 8 were waited for; matrix products, arithmetic and copies ran while one was open for 1% of the time, Pallas kernels for 5%

profile of v5, /device:TPU:8, one launch (start us, length us, event | category | flops | bytes accessed | tf_op | source)
XLA Modules:
  0.0 136.0 jit_solution(9551535093763018419)
XLA Ops:
  0.6 0.0 copy-start.1
  0.6 1.4 pack.1.rest_0_
  2.0 0.0 copy-start
  2.0 1.7 %collective-permute-start.5 = (bf16[8,144,512]{2,1,0:T(8,128)(2,1)S(1)}, bf16[8,144,512]{2,1,0:T(8,128)(2,1)S(1)}, u32[]{:S(2)}, u32[]{:S(2)}) collective-permute-start(bf16[8,144,512]{2,1,0:T(8,128)(2,1)S(1)} %pack.1.rest_0_), channel_id=1, source_target_pairs={{0,2},{1,7},{2,4},{3,1},{4,6},{5,3},{6,0},{7,5},{8,10},{9,15},{10,... | collective-permute-start | bytes 3538952 | tf_op jit(solution)/shard_map/ppermute | solution.py:394
  3.7 0.7 collective-permute-start.9
  4.3 26.6 %collective-permute-done.5.rest_2_ = bf16[8,144,512]{2,1,0:T(8,128)(2,1)S(1)} collective-permute-done((bf16[8,144,512]{2,1,0:T(8,128)(2,1)S(1)}, bf16[8,144,512]{2,1,0:T(8,128)(2,1)S(1)}, u32[]{:S(2)}, u32[]{:S(2)}) %collective-permute-start.5) | collective-permute-done | bytes 1179680 | tf_op jit(solution)/shard_map/ppermute | solution.py:394
  30.9 0.0 copy-start.4
  30.9 0.6 collective-permute-start.7
  31.5 0.0 collective-permute-start.4
  31.6 0.5 collective-permute-start.6
  32.1 0.0 collective-permute-done.9.rest_6_
  32.1 0.0 collective-permute-start.10
  32.1 16.4 %collective-permute-done.7.rest_4_ = bf16[8,144,512]{2,1,0:T(8,128)(2,1)} collective-permute-done((bf16[8,144,512]{2,1,0:T(8,128)(2,1)S(1)}, bf16[8,144,512]{2,1,0:T(8,128)(2,1)}, u32[]{:S(2)}, u32[]{:S(2)}) %collective-permute-start.7) | collective-permute-done | bytes 1179680 | tf_op jit(solution)/shard_map/ppermute | solution.py:395
  48.5 0.0 collective-permute-start.8
  48.5 0.0 copy-done.1
  48.5 0.8 tiles.1
  49.3 9.8 %all-to-all-start = ((bf16[32,48,128]{2,1,0:T(8,128)(2,1)}), bf16[32,48,128]{2,1,0:T(8,128)(2,1)S(1)}, u32[]{:S(2)}, u32[]{:S(2)}) async-start(bf16[32,48,128]{2,1,0:T(8,128)(2,1)} %tiles.1), calls=%async_computation | async-start | bytes 786432 | tf_op jit(solution)/shard_map/all_to_all | solution.py:40
  59.1 0.0 copy-start.6
  59.1 0.0 copy-start.2
  59.1 0.0 copy-start.3
  59.1 0.0 copy-start.5
  59.1 3.1 %united.1 = bf16[16,264]{1,0:T(8,128)(2,1)S(1)} custom-call(bf16[16,5120]{1,0:T(8,128)(2,1)} %hid_hbm.1, bf16[264,5120]{1,0:T(8,128)(2,1)} %bitcast.9), custom_call_target="tpu_custom_call" | custom-call | tf_op jit(solution)/shard_map/united/pallas_call | solution.py:70
  62.3 0.0 copy-done
  62.3 0.0 copy-done.4
  62.3 0.3 collective-permute-start
  62.6 1.0 collective-permute-done
  63.6 1.7 %collective-permute-start.1 = (bf16[2,16,264]{2,1,0:T(8,128)(2,1)S(1)}, bf16[2,16,264]{2,1,0:T(8,128)(2,1)S(1)}, u32[]{:S(2)}, u32[]{:S(2)}) collective-permute-start(bf16[2,16,264]{2,1,0:T(8,128)(2,1)S(1)} %pad_maximum_fusion.refs_0_), channel_id=1, source_target_pairs={{2,0},{7,1},{4,2},{1,3},{6,4},{3,5},{0,6},{5,7},{10,8},{15,9},{12,... | collective-permute-start | bytes 50696 | tf_op jit(solution)/shard_map/ppermute | solution.py:400
  65.2 2.3 %collective-permute-done.1.refs_1_ = bf16[2,16,264]{2,1,0:T(8,128)(2,1)S(1)} collective-permute-done((bf16[2,16,264]{2,1,0:T(8,128)(2,1)S(1)}, bf16[2,16,264]{2,1,0:T(8,128)(2,1)S(1)}, u32[]{:S(2)}, u32[]{:S(2)}) %collective-permute-start.1) | collective-permute-done | bytes 16928 | tf_op jit(solution)/shard_map/ppermute | solution.py:400
  67.5 1.6 %collective-permute-start.3 = (bf16[2,16,264]{2,1,0:T(8,128)(2,1)S(1)}, bf16[2,16,264]{2,1,0:T(8,128)(2,1)S(1)}, u32[]{:S(2)}, u32[]{:S(2)}) collective-permute-start(bf16[2,16,264]{2,1,0:T(8,128)(2,1)S(1)} %collective-permute-done.1.refs_1_), channel_id=1, source_target_pairs={{2,0},{7,1},{4,2},{1,3},{6,4},{3,5},{0,6},{5,7},{10,8},{15,9},{12,... | collective-permute-start | bytes 50696 | tf_op jit(solution)/shard_map/ppermute | solution.py:401
  69.1 0.0 copy-done.6
  69.1 2.2 %collective-permute-done.3.refs_3_ = bf16[2,16,264]{2,1,0:T(8,128)(2,1)S(1)} collective-permute-done((bf16[2,16,264]{2,1,0:T(8,128)(2,1)S(1)}, bf16[2,16,264]{2,1,0:T(8,128)(2,1)S(1)}, u32[]{:S(2)}, u32[]{:S(2)}) %collective-permute-start.3) | collective-permute-done | bytes 16928 | tf_op jit(solution)/shard_map/ppermute | solution.py:401
  71.3 0.0 collective-permute-start.2
  71.3 0.1 multiply_sine_fusion
  71.4 1.1 collective-permute-done.2.refs_2_
  72.5 2.6 %all-to-all-done.refs_8_ = bf16[32,48,128]{2,1,0:T(8,128)(2,1)S(1)} async-done(((bf16[32,48,128]{2,1,0:T(8,128)(2,1)}), bf16[32,48,128]{2,1,0:T(8,128)(2,1)S(1)}, u32[]{:S(2)}, u32[]{:S(2)}) %all-to-all-start) | async-done | bytes 393248 | tf_op jit(solution)/shard_map/all_to_all | solution.py:40
  75.1 0.0 copy-done.2
  75.1 0.0 copy-done.3
  75.1 1.1 query.1
  76.2 7.2 %all-to-all-start.1 = ((bf16[32,16,128]{2,1,0:T(8,128)(2,1)}), bf16[32,16,128]{2,1,0:T(8,128)(2,1)S(1)}, u32[]{:S(2)}, u32[]{:S(2)}) async-start(bf16[32,16,128]{2,1,0:T(8,128)(2,1)} %get-tuple-element.5), calls=%async_computation.1 | async-start | bytes 262144 | tf_op jit(solution)/shard_map/all_to_all | solution.py:40
  83.4 0.0 copy-done.5
  83.4 0.7 copy.13.table
  84.1 1.5 %slots.1 = s32[128]{0:T(128)} custom-call(s32[16,4]{1,0:T(8,128)} %copy.13.table, s32[16]{0:T(128)} %lengths.1), custom_call_target="tpu_custom_call" | custom-call | tf_op jit(solution)/shard_map/slots/pallas_call | solution.py:205
  85.6 8.6 %all-to-all-done.1.q = bf16[32,16,128]{2,1,0:T(8,128)(2,1)S(1)} async-done(((bf16[32,16,128]{2,1,0:T(8,128)(2,1)}), bf16[32,16,128]{2,1,0:T(8,128)(2,1)S(1)}, u32[]{:S(2)}, u32[]{:S(2)}) %all-to-all-start.1) | async-done | bytes 131104 | tf_op jit(solution)/shard_map/all_to_all | solution.py:40
  94.2 0.0 collective-permute-done.4.rest_1_
  94.2 0.0 collective-permute-done.10.rest_7_
  94.2 0.0 collective-permute-done.6.rest_3_
  94.2 0.0 collective-permute-done.8.rest_5_
  94.2 9.3 %attend.1 = bf16[32,8,640]{2,1,0:T(8,128)(2,1)S(1)} custom-call(s32[128]{0:T(128)} %slots.1, bf16[32,16,128]{2,1,0:T(8,128)(2,1)S(1)} %all-to-all-done.1.q, f32[16,640]{1,0:T(8,128)S(1)} %get-tuple-element.6.wide, bf16[512,2048]{1,0:T(8,128)(2,1)} %key_up.1, bf16[8,144,512]{2,1,0:T(8,128)(2,1)} %copy-done, ...), custom_call_target="tpu_custom_call" | custom-call | tf_op jit(solution)/shard_map/attend/pallas_call | solution.py:326
  103.6 16.6 %all_to_all.20.parts = bf16[32,8,640]{2,1,0:T(8,128)(2,1)S(1)} all-to-all(bf16[32,8,640]{2,1,0:T(8,128)(2,1)S(1)} %attend.1), channel_id=1, replica_groups=mesh['z'=8,'x'=4,'y'=4,'c'=2] {'z','x'}, dimensions={0} | all-to-all | bytes 655360 | tf_op jit(solution)/shard_map/all_to_all | solution.py:40
  120.2 1.2 value.1
  121.3 14.0 %all_to_all.21 = bf16[32,8,128]{2,1,0:T(8,128)(2,1)S(1)} all-to-all(bf16[32,8,128]{2,1,0:T(8,128)(2,1)S(1)} %value.1), channel_id=1, replica_groups=mesh['z'=8,'x'=4,'y'=4,'c'=2] {'z','x'}, dimensions={0} | all-to-all | bytes 131072 | tf_op jit(solution)/shard_map/all_to_all | solution.py:40
  135.4 0.6 copy.15
  (3 shorter events, 0.0 us)
Async XLA Ops:
  0.6 47.9 %copy-start.1 = (bf16[48,3072]{1,0:T(8,128)(2,1)S(1)}, bf16[48,3072]{1,0:T(8,128)(2,1)}, u32[]{:S(2)}) copy-start(bf16[48,3072]{1,0:T(8,128)(2,1)} %q_up.1) | copy-start | bytes 884740
  2.0 60.3 %copy-start = (bf16[8,144,512]{2,1,0:T(8,128)(2,1)}, bf16[8,144,512]{2,1,0:T(8,128)(2,1)S(1)}, u32[]{:S(2)}) copy-start(bf16[8,144,512]{2,1,0:T(8,128)(2,1)S(1)} %pack.1.rest_0_) | copy-start | bytes 3538948
  2.0 28.9 %collective-permute-start.5 = (bf16[8,144,512]{2,1,0:T(8,128)(2,1)S(1)}, bf16[8,144,512]{2,1,0:T(8,128)(2,1)S(1)}, u32[]{:S(2)}, u32[]{:S(2)}) collective-permute-start(bf16[8,144,512]{2,1,0:T(8,128)(2,1)S(1)} %pack.1.rest_0_), channel_id=1, source_target_pairs={{0,2},{1,7},{2,4},{3,1},{4,6},{5,3},{6,0},{7,5},{8,10},{9,15},{10,... | collective-permute-start | bytes 3538952 | tf_op jit(solution)/shard_map/ppermute | solution.py:394
  3.7 28.4 %collective-permute-start.9 = (bf16[8,144,512]{2,1,0:T(8,128)(2,1)S(1)}, bf16[8,144,512]{2,1,0:T(8,128)(2,1)}, u32[]{:S(2)}, u32[]{:S(2)}) collective-permute-start(bf16[8,144,512]{2,1,0:T(8,128)(2,1)S(1)} %pack.1.rest_0_), channel_id=1, source_target_pairs={{2,0},{7,1},{4,2},{1,3},{6,4},{3,5},{0,6},{5,7},{10,8},{15,9},{12,... | collective-permute-start | bytes 3538952 | tf_op jit(solution)/shard_map/ppermute | solution.py:396
  30.9 31.4 %copy-start.4 = (bf16[8,144,512]{2,1,0:T(8,128)(2,1)}, bf16[8,144,512]{2,1,0:T(8,128)(2,1)S(1)}, u32[]{:S(2)}) copy-start(bf16[8,144,512]{2,1,0:T(8,128)(2,1)S(1)} %collective-permute-done.5.rest_2_) | copy-start | bytes 3538948
  30.9 17.6 %collective-permute-start.7 = (bf16[8,144,512]{2,1,0:T(8,128)(2,1)S(1)}, bf16[8,144,512]{2,1,0:T(8,128)(2,1)}, u32[]{:S(2)}, u32[]{:S(2)}) collective-permute-start(bf16[8,144,512]{2,1,0:T(8,128)(2,1)S(1)} %collective-permute-done.5.rest_2_), channel_id=1, source_target_pairs={{0,2},{1,7},{2,4},{3,1},{4,6},{5,3},{6,0},{7,5},{8,10},{9,15},{10,... | collective-permute-start | bytes 3538952 | tf_op jit(solution)/shard_map/ppermute | solution.py:395
  31.5 62.7 %collective-permute-start.4 = (bf16[8,144,512]{2,1,0:T(8,128)(2,1)S(1)}, bf16[8,144,512]{2,1,0:T(8,128)(2,1)}, u32[]{:S(2)}, u32[]{:S(2)}) collective-permute-start(bf16[8,144,512]{2,1,0:T(8,128)(2,1)S(1)} %pack.1.rest_0_), channel_id=1, source_target_pairs={{0,1},{1,0},{2,3},{3,2},{4,5},{5,4},{6,7},{7,6},{8,9},{9,8},{10,11... | collective-permute-start | bytes 3538952 | tf_op jit(solution)/shard_map/ppermute | solution.py:404
  31.6 62.7 %collective-permute-start.6 = (bf16[8,144,512]{2,1,0:T(8,128)(2,1)S(1)}, bf16[8,144,512]{2,1,0:T(8,128)(2,1)}, u32[]{:S(2)}, u32[]{:S(2)}) collective-permute-start(bf16[8,144,512]{2,1,0:T(8,128)(2,1)S(1)} %collective-permute-done.5.rest_2_), channel_id=1, source_target_pairs={{0,1},{1,0},{2,3},{3,2},{4,5},{5,4},{6,7},{7,6},{8,9},{9,8},{10,11... | collective-permute-start | bytes 3538952 | tf_op jit(solution)/shard_map/ppermute | solution.py:404
  32.1 62.2 %collective-permute-start.10 = (bf16[8,144,512]{2,1,0:T(8,128)(2,1)}, bf16[8,144,512]{2,1,0:T(8,128)(2,1)}, u32[]{:S(2)}, u32[]{:S(2)}) collective-permute-start(bf16[8,144,512]{2,1,0:T(8,128)(2,1)} %collective-permute-done.9.rest_6_), channel_id=1, source_target_pairs={{0,1},{1,0},{2,3},{3,2},{4,5},{5,4},{6,7},{7,6},{8,9},{9,8},{10,11... | collective-permute-start | bytes 3538952 | tf_op jit(solution)/shard_map/ppermute | solution.py:404
  48.5 45.8 %collective-permute-start.8 = (bf16[8,144,512]{2,1,0:T(8,128)(2,1)}, bf16[8,144,512]{2,1,0:T(8,128)(2,1)}, u32[]{:S(2)}, u32[]{:S(2)}) collective-permute-start(bf16[8,144,512]{2,1,0:T(8,128)(2,1)} %collective-permute-done.7.rest_4_), channel_id=1, source_target_pairs={{0,1},{1,0},{2,3},{3,2},{4,5},{5,4},{6,7},{7,6},{8,9},{9,8},{10,11... | collective-permute-start | bytes 3538952 | tf_op jit(solution)/shard_map/ppermute | solution.py:404
  49.3 25.8 %all-to-all-start = ((bf16[32,48,128]{2,1,0:T(8,128)(2,1)}), bf16[32,48,128]{2,1,0:T(8,128)(2,1)S(1)}, u32[]{:S(2)}, u32[]{:S(2)}) async-start(bf16[32,48,128]{2,1,0:T(8,128)(2,1)} %tiles.1), calls=%async_computation | async-start | bytes 786432 | tf_op jit(solution)/shard_map/all_to_all | solution.py:40
  59.1 10.0 %copy-start.6 = (s32[16]{0:T(128)S(1)}, s32[16]{0:T(128)}, u32[]{:S(2)}) copy-start(s32[16]{0:T(128)} %lengths.1) | copy-start | bytes 196
  59.1 16.0 %copy-start.2 = (f32[1536]{0:T(1024)S(1)}, f32[1536]{0:T(1024)}, u32[]{:S(2)}) copy-start(f32[1536]{0:T(1024)} %refs_4_.1) | copy-start | bytes 18436
  59.1 16.0 %copy-start.3 = (f32[512]{0:T(512)S(1)}, f32[512]{0:T(512)}, u32[]{:S(2)}) copy-start(f32[512]{0:T(512)} %refs_5_.1) | copy-start | bytes 6148
  59.1 24.3 %copy-start.5 = (s32[16,4]{0,1:T(4,128)S(1)}, s32[16,4]{0,1:T(4,128)}, u32[]{:S(2)}) copy-start(s32[16,4]{0,1:T(4,128)} %param.21) | copy-start | bytes 772
  62.3 1.3 collective-permute-start
  63.6 3.9 %collective-permute-start.1 = (bf16[2,16,264]{2,1,0:T(8,128)(2,1)S(1)}, bf16[2,16,264]{2,1,0:T(8,128)(2,1)S(1)}, u32[]{:S(2)}, u32[]{:S(2)}) collective-permute-start(bf16[2,16,264]{2,1,0:T(8,128)(2,1)S(1)} %pad_maximum_fusion.refs_0_), channel_id=1, source_target_pairs={{2,0},{7,1},{4,2},{1,3},{6,4},{3,5},{0,6},{5,7},{10,8},{15,9},{12,... | collective-permute-start | bytes 50696 | tf_op jit(solution)/shard_map/ppermute | solution.py:400
  67.5 3.8 %collective-permute-start.3 = (bf16[2,16,264]{2,1,0:T(8,128)(2,1)S(1)}, bf16[2,16,264]{2,1,0:T(8,128)(2,1)S(1)}, u32[]{:S(2)}, u32[]{:S(2)}) collective-permute-start(bf16[2,16,264]{2,1,0:T(8,128)(2,1)S(1)} %collective-permute-done.1.refs_1_), channel_id=1, source_target_pairs={{2,0},{7,1},{4,2},{1,3},{6,4},{3,5},{0,6},{5,7},{10,8},{15,9},{12,... | collective-permute-start | bytes 50696 | tf_op jit(solution)/shard_map/ppermute | solution.py:401
  71.3 1.2 collective-permute-start.2
  76.2 18.0 %all-to-all-start.1 = ((bf16[32,16,128]{2,1,0:T(8,128)(2,1)}), bf16[32,16,128]{2,1,0:T(8,128)(2,1)S(1)}, u32[]{:S(2)}, u32[]{:S(2)}) async-start(bf16[32,16,128]{2,1,0:T(8,128)(2,1)} %get-tuple-element.5), calls=%async_computation.1 | async-start | bytes 262144 | tf_op jit(solution)/shard_map/all_to_all | solution.py:40

commit v6 on v5

--- a/solution.py
+++ b/solution.py
@@ -193,7 +193,7 @@
     def fill(b, _):
         slots[64 + b] = lengths[b] - s * (4 * BP)
         for j in range(4):
-            slots[table[b, j] - s * 64] = b * 4 + j
+            slots[table[j, b] - s * 64] = b * 4 + j
         return 0
 
     lax.fori_loop(0, B, fill, 0, unroll=4)
@@ -208,28 +208,37 @@
         in_specs=[spec(SM), spec(SM)],
         out_specs=spec(SM),
         name="slots",
-    )(table, lengths)
-
-
-def attend_kernel(slots, q, wide, key_up, *rest):
+    )(table.T, lengths)
+
+
+def keys_kernel(src, dst, sem):
+    cp = pltpu.make_async_copy(src, dst, sem)
+    cp.start()
+    cp.wait()
+
+
+def keys_call(key_up):
+    return pl.pallas_call(
+        keys_kernel,
+        out_shape=pltpu.VMEM(key_up.shape, bf16),
+        in_specs=[spec(HB)],
+        out_specs=spec(VM),
+        scratch_shapes=[pltpu.SemaphoreType.DMA],
+        name="keys",
+    )(key_up)
+
+
+def attend_kernel(slots, q, wide, keys_v, *rest):
     bufs, out = rest[:8], rest[8]
-    keys_v, kv, q_s, s_s, p_s, o_s, own_s, place, inv, ksem, tsem, sem = rest[9:]
+    kv, q_s, s_s, p_s, o_s, own_s, place, inv, tsem, sem = rest[9:]
     fetch = pltpu.make_async_copy(slots, inv, tsem)
     fetch.start()
     s, y, c = place_of()
-    loads = []
-    for n in range(4):
-        cols = pl.ds(512 * n, 512)
-        cp = pltpu.make_async_copy(key_up.at[:, cols], keys_v.at[:, cols], ksem.at[n])
-        cp.start()
-        loads.append(cp)
     for i in range(8):
         pltpu.make_async_copy(bufs[i], kv.at[pl.ds(8 * i, 8)], sem.at[i // 2]).start()
 
     lane = lax.broadcasted_iota(jnp.int32, (B, BP), 1)
     for p in range(8):
-        if p % 2 == 0:
-            loads[p // 2].wait()
         t0 = q[3 * p].astype(f32)
         t1 = pltpu.roll(q[3 * p + 1].astype(f32), 64, 1)
         t2 = pltpu.roll(q[3 * p + 2].astype(f32), 64, 1)
@@ -322,14 +331,13 @@
     lax.fori_loop(0, 32, pour, 0, unroll=8)
 
 
-def attend_call(slots, q, wide, key_up, bufs):
+def attend_call(slots, q, wide, keys, bufs):
     return pl.pallas_call(
         attend_kernel,
         out_shape=pltpu.VMEM((32, 8, LR + 128), bf16),
-        in_specs=[spec(HB)] + [spec(VM)] * 2 + [spec(HB)] * 9,
+        in_specs=[spec(HB)] + [spec(VM)] * 3 + [spec(HB)] * 8,
         out_specs=spec(VM),
         scratch_shapes=[
-            pltpu.VMEM((LR, 2048), bf16),
             pltpu.VMEM((64, BP + 16, LR), bf16),
             pltpu.VMEM((B, B, LR + 128), f32),
             pltpu.VMEM((64, B, BP), f32),
@@ -338,12 +346,11 @@
             pltpu.VMEM((B, B, LR), f32),
             pltpu.SMEM((64,), jnp.int32),
             pltpu.SMEM((128,), jnp.int32),
-            pltpu.SemaphoreType.DMA((4,)),
             pltpu.SemaphoreType.DMA,
             pltpu.SemaphoreType.DMA((4,)),
         ],
         name="attend",
-    )(slots, *here(q, wide), key_up, *(pltpu.with_memory_space_constraint(v, HB) for v in bufs))
+    )(slots, *here(q, wide, keys), *(pltpu.with_memory_space_constraint(v, HB) for v in bufs))
 
 
 def value_kernel(parts, value_up, out, vals, sem):
@@ -404,7 +411,7 @@
         bufs += [value, lax.ppermute(value, "c", SWAP)]
     entry, wide, q_copies = query_call(parts, q_gain, kv_gain, cos, sin, q_tile)
     q_all = exchange(q_copies, S)
-    mixed = attend_call(slots_call(table, lengths), q_all, wide, key_up, bufs)
+    mixed = attend_call(slots_call(table, lengths), q_all, wide, keys_call(key_up), bufs)
     spans = exchange(mixed, S)
     res = value_call(spans, value_up)
     res = exchange(res, S)

time: 138 us -> 137 us (level)
    pallas_call x1, Pallas kernels: 9.35 us -> 7.3 us  [attend_call(): pl.pallas_call(attend_kernel, out_shape=pltpu.VMEM((32, 8, LR + 128), bf1...]
    pallas_call x0 -> x1, Pallas kernels: none -> 1.6 us  [keys_call(): pl.pallas_call(keys_kernel, out_shape=pltpu.VMEM(key_up.shape, bf16), in_...]
  transfers between devices with their start and end apart: 13 -> 13, of which waited for: 8 -> 8; matrix products, arithmetic and copies ran while one was open for 1% -> 0% of each run, Pallas kernels for 5% -> 6%
where the time goes in v6:
time: 137 us; the launch traced here: 134 us
  waiting for transfers between devices  60.2 us (44%)
  blocking collectives  30.6 us (22%)
  starting transfers between devices  24 us (18%)
  Pallas kernels  17.9 us (13%)
    all_to_all x2, blocking collectives, exchange(): return lax.all_to_all(pieces, axes, split_axis=0, concat_axis=0, tiled=True)  30.6 us
    ppermute x1, waiting for transfers between devices, body(): alpha = lax.ppermute(mine, T, ALPHA)  26.7 us
    all_to_all x2, starting transfers between devices, exchange(): return lax.all_to_all(pieces, axes, split_axis=0, concat_axis=0, tiled=True)  16.9 us
    ppermute x1, waiting for transfers between devices, body(): far = lax.ppermute(alpha, T, ALPHA)  16.6 us
    all_to_all x2, waiting for transfers between devices, exchange(): return lax.all_to_all(pieces, axes, split_axis=0, concat_axis=0, tiled=True)  10.4 us
    pallas_call x1, Pallas kernels, attend_call(): pl.pallas_call(attend_kernel, out_shape=pltpu.VMEM((32, 8, LR + 128), bf1...  7.3 us
    pallas_call x1, Pallas kernels, united_call(): pl.pallas_call(united_kernel, out_shape=pltpu.VMEM((B, cols), bf16), in_s...  3.14 us
  transfers between devices with their start and end apart: 13, of which 8 were waited for; matrix products, arithmetic and copies ran while one was open for 0% of the time, Pallas kernels for 6%

profile of v6, /device:TPU:8, one launch (start us, length us, event | category | flops | bytes accessed | tf_op | source)
XLA Modules:
  0.0 134.2 jit_solution(5193399310996140805)
XLA Ops:
  0.6 0.0 copy-start.1
  0.6 1.4 %pack.1.rest_0_ = bf16[8,144,512]{2,1,0:T(8,128)(2,1)S(1)} custom-call(bf16[8,128,512]{2,1,0:T(8,128)(2,1)} %lat.1, bf16[8,64,128]{2,1,0:T(8,128)(2,1)} %rope.1), custom_call_target="tpu_custom_call" | custom-call | tf_op jit(solution)/shard_map/pack/pallas_call | solution.py:114
  2.0 0.0 copy-start
  2.0 1.7 %collective-permute-start.5 = (bf16[8,144,512]{2,1,0:T(8,128)(2,1)S(1)}, bf16[8,144,512]{2,1,0:T(8,128)(2,1)}, u32[]{:S(2)}, u32[]{:S(2)}) collective-permute-start(bf16[8,144,512]{2,1,0:T(8,128)(2,1)S(1)} %pack.1.rest_0_), channel_id=1, source_target_pairs={{0,2},{1,7},{2,4},{3,1},{4,6},{5,3},{6,0},{7,5},{8,10},{9,15},{10,... | collective-permute-start | bytes 3538952 | tf_op jit(solution)/shard_map/ppermute | solution.py:401
  3.7 0.7 collective-permute-start.9
  4.3 26.7 %collective-permute-done.5.rest_2_ = bf16[8,144,512]{2,1,0:T(8,128)(2,1)} collective-permute-done((bf16[8,144,512]{2,1,0:T(8,128)(2,1)S(1)}, bf16[8,144,512]{2,1,0:T(8,128)(2,1)}, u32[]{:S(2)}, u32[]{:S(2)}) %collective-permute-start.5) | collective-permute-done | bytes 1179680 | tf_op jit(solution)/shard_map/ppermute | solution.py:401
  31.0 0.6 collective-permute-start.7
  31.7 0.0 collective-permute-start.4
  31.7 0.5 collective-permute-start.6
  32.2 0.0 collective-permute-done.9.rest_6_
  32.2 0.0 collective-permute-start.10
  32.2 16.6 %collective-permute-done.7.rest_4_ = bf16[8,144,512]{2,1,0:T(8,128)(2,1)} collective-permute-done((bf16[8,144,512]{2,1,0:T(8,128)(2,1)}, bf16[8,144,512]{2,1,0:T(8,128)(2,1)}, u32[]{:S(2)}, u32[]{:S(2)}) %collective-permute-start.7) | collective-permute-done | bytes 1179680 | tf_op jit(solution)/shard_map/ppermute | solution.py:402
  48.8 0.0 collective-permute-start.8
  48.8 0.0 copy-done.1
  48.8 0.8 tiles.1
  49.6 9.8 %all-to-all-start = ((bf16[32,48,128]{2,1,0:T(8,128)(2,1)}), bf16[32,48,128]{2,1,0:T(8,128)(2,1)S(1)}, u32[]{:S(2)}, u32[]{:S(2)}) async-start(bf16[32,48,128]{2,1,0:T(8,128)(2,1)} %tiles.1), calls=%async_computation | async-start | bytes 786432 | tf_op jit(solution)/shard_map/all_to_all | solution.py:40
  59.4 0.0 copy-start.4
  59.4 0.0 copy-start.2
  59.4 0.0 copy-start.3
  59.4 3.1 %united.1 = bf16[16,264]{1,0:T(8,128)(2,1)S(1)} custom-call(bf16[16,5120]{1,0:T(8,128)(2,1)} %hid_hbm.1, bf16[264,5120]{1,0:T(8,128)(2,1)} %bitcast.10), custom_call_target="tpu_custom_call" | custom-call | tf_op jit(solution)/shard_map/united/pallas_call | solution.py:70
  62.6 0.0 copy-done
  62.6 0.3 collective-permute-start
  62.9 1.0 collective-permute-done
  63.9 1.7 %collective-permute-start.1 = (bf16[2,16,264]{2,1,0:T(8,128)(2,1)S(1)}, bf16[2,16,264]{2,1,0:T(8,128)(2,1)S(1)}, u32[]{:S(2)}, u32[]{:S(2)}) collective-permute-start(bf16[2,16,264]{2,1,0:T(8,128)(2,1)S(1)} %pad_maximum_fusion.refs_0_), channel_id=1, source_target_pairs={{2,0},{7,1},{4,2},{1,3},{6,4},{3,5},{0,6},{5,7},{10,8},{15,9},{12,... | collective-permute-start | bytes 50696 | tf_op jit(solution)/shard_map/ppermute | solution.py:407
  65.5 2.3 %collective-permute-done.1.refs_1_ = bf16[2,16,264]{2,1,0:T(8,128)(2,1)S(1)} collective-permute-done((bf16[2,16,264]{2,1,0:T(8,128)(2,1)S(1)}, bf16[2,16,264]{2,1,0:T(8,128)(2,1)S(1)}, u32[]{:S(2)}, u32[]{:S(2)}) %collective-permute-start.1) | collective-permute-done | bytes 16928 | tf_op jit(solution)/shard_map/ppermute | solution.py:407
  67.8 1.6 %collective-permute-start.3 = (bf16[2,16,264]{2,1,0:T(8,128)(2,1)S(1)}, bf16[2,16,264]{2,1,0:T(8,128)(2,1)S(1)}, u32[]{:S(2)}, u32[]{:S(2)}) collective-permute-start(bf16[2,16,264]{2,1,0:T(8,128)(2,1)S(1)} %collective-permute-done.1.refs_1_), channel_id=1, source_target_pairs={{2,0},{7,1},{4,2},{1,3},{6,4},{3,5},{0,6},{5,7},{10,8},{15,9},{12,... | collective-permute-start | bytes 50696 | tf_op jit(solution)/shard_map/ppermute | solution.py:408
  69.4 0.0 copy-done.4
  69.4 2.2 %collective-permute-done.3.refs_3_ = bf16[2,16,264]{2,1,0:T(8,128)(2,1)S(1)} collective-permute-done((bf16[2,16,264]{2,1,0:T(8,128)(2,1)S(1)}, bf16[2,16,264]{2,1,0:T(8,128)(2,1)S(1)}, u32[]{:S(2)}, u32[]{:S(2)}) %collective-permute-start.3) | collective-permute-done | bytes 16928 | tf_op jit(solution)/shard_map/ppermute | solution.py:408
  71.6 0.0 collective-permute-start.2
  71.6 0.1 multiply_sine_fusion
  71.7 1.1 collective-permute-done.2.refs_2_
  72.8 2.6 %all-to-all-done.refs_8_ = bf16[32,48,128]{2,1,0:T(8,128)(2,1)S(1)} async-done(((bf16[32,48,128]{2,1,0:T(8,128)(2,1)}), bf16[32,48,128]{2,1,0:T(8,128)(2,1)S(1)}, u32[]{:S(2)}, u32[]{:S(2)}) %all-to-all-start) | async-done | bytes 393248 | tf_op jit(solution)/shard_map/all_to_all | solution.py:40
  75.4 0.0 copy-done.2
  75.4 0.0 copy-done.3
  75.4 1.1 query.1
  76.5 7.2 %all-to-all-start.1 = ((bf16[32,16,128]{2,1,0:T(8,128)(2,1)}), bf16[32,16,128]{2,1,0:T(8,128)(2,1)S(1)}, u32[]{:S(2)}, u32[]{:S(2)}) async-start(bf16[32,16,128]{2,1,0:T(8,128)(2,1)} %get-tuple-element.5), calls=%async_computation.1 | async-start | bytes 262144 | tf_op jit(solution)/shard_map/all_to_all | solution.py:40
  83.7 1.4 %slots.1 = s32[128]{0:T(128)} custom-call(s32[4,16]{1,0:T(4,128)} %bitcast.13, s32[16]{0:T(128)} %lengths.1), custom_call_target="tpu_custom_call" | custom-call | tf_op jit(solution)/shard_map/slots/pallas_call | solution.py:205
  85.1 1.6 %keys.1.keys_v = bf16[512,2048]{1,0:T(8,128)(2,1)S(1)} custom-call(bf16[512,2048]{1,0:T(8,128)(2,1)} %src.1), custom_call_target="tpu_custom_call" | custom-call | tf_op jit(solution)/shard_map/keys/pallas_call | solution.py:221
  86.7 7.8 %all-to-all-done.1.q = bf16[32,16,128]{2,1,0:T(8,128)(2,1)S(1)} async-done(((bf16[32,16,128]{2,1,0:T(8,128)(2,1)}), bf16[32,16,128]{2,1,0:T(8,128)(2,1)S(1)}, u32[]{:S(2)}, u32[]{:S(2)}) %all-to-all-start.1) | async-done | bytes 131104 | tf_op jit(solution)/shard_map/all_to_all | solution.py:40
  94.5 0.0 collective-permute-done.4.rest_1_
  94.5 0.0 collective-permute-done.10.rest_7_
  94.5 0.0 collective-permute-done.6.rest_3_
  94.5 0.0 collective-permute-done.8.rest_5_
  94.5 7.3 %attend.1 = bf16[32,8,640]{2,1,0:T(8,128)(2,1)S(1)} custom-call(s32[128]{0:T(128)} %slots.1, bf16[32,16,128]{2,1,0:T(8,128)(2,1)S(1)} %all-to-all-done.1.q, f32[16,640]{1,0:T(8,128)S(1)} %get-tuple-element.6.wide, bf16[512,2048]{1,0:T(8,128)(2,1)S(1)} %keys.1.keys_v, bf16[8,144,512]{2,1,0:T(8,128)(2,1)} %copy-done, ...), custom_call_target="tpu_custom_call" | custom-call | tf_op jit(solution)/shard_map/attend/pallas_call | solution.py:335
  101.8 16.6 %all_to_all.20.parts = bf16[32,8,640]{2,1,0:T(8,128)(2,1)S(1)} all-to-all(bf16[32,8,640]{2,1,0:T(8,128)(2,1)S(1)} %attend.1), channel_id=1, replica_groups=mesh['z'=8,'x'=4,'y'=4,'c'=2] {'z','x'}, dimensions={0} | all-to-all | bytes 655360 | tf_op jit(solution)/shard_map/all_to_all | solution.py:40
  118.4 1.2 value.1
  119.6 14.0 %all_to_all.21 = bf16[32,8,128]{2,1,0:T(8,128)(2,1)S(1)} all-to-all(bf16[32,8,128]{2,1,0:T(8,128)(2,1)S(1)} %value.1), channel_id=1, replica_groups=mesh['z'=8,'x'=4,'y'=4,'c'=2] {'z','x'}, dimensions={0} | all-to-all | bytes 131072 | tf_op jit(solution)/shard_map/all_to_all | solution.py:40
  133.6 0.6 copy.14
  (3 shorter events, 0.0 us)
Async XLA Ops:
  0.6 48.2 %copy-start.1 = (bf16[48,3072]{1,0:T(8,128)(2,1)S(1)}, bf16[48,3072]{1,0:T(8,128)(2,1)}, u32[]{:S(2)}) copy-start(bf16[48,3072]{1,0:T(8,128)(2,1)} %q_up.1) | copy-start | bytes 884740
  2.0 60.6 %copy-start = (bf16[8,144,512]{2,1,0:T(8,128)(2,1)}, bf16[8,144,512]{2,1,0:T(8,128)(2,1)S(1)}, u32[]{:S(2)}) copy-start(bf16[8,144,512]{2,1,0:T(8,128)(2,1)S(1)} %pack.1.rest_0_) | copy-start | bytes 3538948
  2.0 29.0 %collective-permute-start.5 = (bf16[8,144,512]{2,1,0:T(8,128)(2,1)S(1)}, bf16[8,144,512]{2,1,0:T(8,128)(2,1)}, u32[]{:S(2)}, u32[]{:S(2)}) collective-permute-start(bf16[8,144,512]{2,1,0:T(8,128)(2,1)S(1)} %pack.1.rest_0_), channel_id=1, source_target_pairs={{0,2},{1,7},{2,4},{3,1},{4,6},{5,3},{6,0},{7,5},{8,10},{9,15},{10,... | collective-permute-start | bytes 3538952 | tf_op jit(solution)/shard_map/ppermute | solution.py:401
  3.7 28.5 %collective-permute-start.9 = (bf16[8,144,512]{2,1,0:T(8,128)(2,1)S(1)}, bf16[8,144,512]{2,1,0:T(8,128)(2,1)}, u32[]{:S(2)}, u32[]{:S(2)}) collective-permute-start(bf16[8,144,512]{2,1,0:T(8,128)(2,1)S(1)} %pack.1.rest_0_), channel_id=1, source_target_pairs={{2,0},{7,1},{4,2},{1,3},{6,4},{3,5},{0,6},{5,7},{10,8},{15,9},{12,... | collective-permute-start | bytes 3538952 | tf_op jit(solution)/shard_map/ppermute | solution.py:403
  31.0 17.8 %collective-permute-start.7 = (bf16[8,144,512]{2,1,0:T(8,128)(2,1)}, bf16[8,144,512]{2,1,0:T(8,128)(2,1)}, u32[]{:S(2)}, u32[]{:S(2)}) collective-permute-start(bf16[8,144,512]{2,1,0:T(8,128)(2,1)} %collective-permute-done.5.rest_2_), channel_id=1, source_target_pairs={{0,2},{1,7},{2,4},{3,1},{4,6},{5,3},{6,0},{7,5},{8,10},{9,15},{10,... | collective-permute-start | bytes 3538952 | tf_op jit(solution)/shard_map/ppermute | solution.py:402
  31.7 62.9 %collective-permute-start.4 = (bf16[8,144,512]{2,1,0:T(8,128)(2,1)S(1)}, bf16[8,144,512]{2,1,0:T(8,128)(2,1)}, u32[]{:S(2)}, u32[]{:S(2)}) collective-permute-start(bf16[8,144,512]{2,1,0:T(8,128)(2,1)S(1)} %pack.1.rest_0_), channel_id=1, source_target_pairs={{0,1},{1,0},{2,3},{3,2},{4,5},{5,4},{6,7},{7,6},{8,9},{9,8},{10,11... | collective-permute-start | bytes 3538952 | tf_op jit(solution)/shard_map/ppermute | solution.py:411
  31.7 62.9 %collective-permute-start.6 = (bf16[8,144,512]{2,1,0:T(8,128)(2,1)}, bf16[8,144,512]{2,1,0:T(8,128)(2,1)}, u32[]{:S(2)}, u32[]{:S(2)}) collective-permute-start(bf16[8,144,512]{2,1,0:T(8,128)(2,1)} %collective-permute-done.5.rest_2_), channel_id=1, source_target_pairs={{0,1},{1,0},{2,3},{3,2},{4,5},{5,4},{6,7},{7,6},{8,9},{9,8},{10,11... | collective-permute-start | bytes 3538952 | tf_op jit(solution)/shard_map/ppermute | solution.py:411
  32.2 62.4 %collective-permute-start.10 = (bf16[8,144,512]{2,1,0:T(8,128)(2,1)}, bf16[8,144,512]{2,1,0:T(8,128)(2,1)}, u32[]{:S(2)}, u32[]{:S(2)}) collective-permute-start(bf16[8,144,512]{2,1,0:T(8,128)(2,1)} %collective-permute-done.9.rest_6_), channel_id=1, source_target_pairs={{0,1},{1,0},{2,3},{3,2},{4,5},{5,4},{6,7},{7,6},{8,9},{9,8},{10,11... | collective-permute-start | bytes 3538952 | tf_op jit(solution)/shard_map/ppermute | solution.py:411
  48.8 45.7 %collective-permute-start.8 = (bf16[8,144,512]{2,1,0:T(8,128)(2,1)}, bf16[8,144,512]{2,1,0:T(8,128)(2,1)}, u32[]{:S(2)}, u32[]{:S(2)}) collective-permute-start(bf16[8,144,512]{2,1,0:T(8,128)(2,1)} %collective-permute-done.7.rest_4_), channel_id=1, source_target_pairs={{0,1},{1,0},{2,3},{3,2},{4,5},{5,4},{6,7},{7,6},{8,9},{9,8},{10,11... | collective-permute-start | bytes 3538952 | tf_op jit(solution)/shard_map/ppermute | solution.py:411
  49.6 25.8 %all-to-all-start = ((bf16[32,48,128]{2,1,0:T(8,128)(2,1)}), bf16[32,48,128]{2,1,0:T(8,128)(2,1)S(1)}, u32[]{:S(2)}, u32[]{:S(2)}) async-start(bf16[32,48,128]{2,1,0:T(8,128)(2,1)} %tiles.1), calls=%async_computation | async-start | bytes 786432 | tf_op jit(solution)/shard_map/all_to_all | solution.py:40
  59.4 10.0 %copy-start.4 = (s32[16]{0:T(128)S(1)}, s32[16]{0:T(128)}, u32[]{:S(2)}) copy-start(s32[16]{0:T(128)} %lengths.1) | copy-start | bytes 196
  59.4 16.0 %copy-start.2 = (f32[1536]{0:T(1024)S(1)}, f32[1536]{0:T(1024)}, u32[]{:S(2)}) copy-start(f32[1536]{0:T(1024)} %refs_4_.1) | copy-start | bytes 18436
  59.4 16.0 %copy-start.3 = (f32[512]{0:T(512)S(1)}, f32[512]{0:T(512)}, u32[]{:S(2)}) copy-start(f32[512]{0:T(512)} %refs_5_.1) | copy-start | bytes 6148
  62.6 1.3 collective-permute-start
  63.9 3.9 %collective-permute-start.1 = (bf16[2,16,264]{2,1,0:T(8,128)(2,1)S(1)}, bf16[2,16,264]{2,1,0:T(8,128)(2,1)S(1)}, u32[]{:S(2)}, u32[]{:S(2)}) collective-permute-start(bf16[2,16,264]{2,1,0:T(8,128)(2,1)S(1)} %pad_maximum_fusion.refs_0_), channel_id=1, source_target_pairs={{2,0},{7,1},{4,2},{1,3},{6,4},{3,5},{0,6},{5,7},{10,8},{15,9},{12,... | collective-permute-start | bytes 50696 | tf_op jit(solution)/shard_map/ppermute | solution.py:407
  67.8 3.8 %collective-permute-start.3 = (bf16[2,16,264]{2,1,0:T(8,128)(2,1)S(1)}, bf16[2,16,264]{2,1,0:T(8,128)(2,1)S(1)}, u32[]{:S(2)}, u32[]{:S(2)}) collective-permute-start(bf16[2,16,264]{2,1,0:T(8,128)(2,1)S(1)} %collective-permute-done.1.refs_1_), channel_id=1, source_target_pairs={{2,0},{7,1},{4,2},{1,3},{6,4},{3,5},{0,6},{5,7},{10,8},{15,9},{12,... | collective-permute-start | bytes 50696 | tf_op jit(solution)/shard_map/ppermute | solution.py:408
  71.6 1.2 collective-permute-start.2
  76.5 18.0 %all-to-all-start.1 = ((bf16[32,16,128]{2,1,0:T(8,128)(2,1)}), bf16[32,16,128]{2,1,0:T(8,128)(2,1)S(1)}, u32[]{:S(2)}, u32[]{:S(2)}) async-start(bf16[32,16,128]{2,1,0:T(8,128)(2,1)} %get-tuple-element.5), calls=%async_computation.1 | async-start | bytes 262144 | tf_op jit(solution)/shard_map/all_to_all | solution.py:40

commit v7 on v6

--- a/solution.py
+++ b/solution.py
@@ -28,12 +28,20 @@
 HB = pltpu.MemorySpace.HBM
 
 
+def grant(mib):
+    return pltpu.CompilerParams(vmem_limit_bytes=mib << 20)
+
+
 def spec(space):
     return pl.BlockSpec(memory_space=space)
 
 
 def here(*values):
     return tuple(pltpu.with_memory_space_constraint(v, VM) for v in values)
+
+
+def there(*values):
+    return tuple(pltpu.with_memory_space_constraint(v, HB) for v in values)
 
 
 def exchange(pieces, axes):
@@ -225,59 +233,111 @@
         out_specs=spec(VM),
         scratch_shapes=[pltpu.SemaphoreType.DMA],
         name="keys",
-    )(key_up)
-
-
-def attend_kernel(slots, q, wide, keys_v, *rest):
-    bufs, out = rest[:8], rest[8]
-    kv, q_s, s_s, p_s, o_s, own_s, place, inv, tsem, sem = rest[9:]
-    fetch = pltpu.make_async_copy(slots, inv, tsem)
-    fetch.start()
-    s, y, c = place_of()
-    for i in range(8):
-        pltpu.make_async_copy(bufs[i], kv.at[pl.ds(8 * i, 8)], sem.at[i // 2]).start()
-
-    lane = lax.broadcasted_iota(jnp.int32, (B, BP), 1)
+        compiler_params=grant(54),
+    )(*there(key_up))
+
+
+def stage_kernel(*refs):
+    bufs, kv, sem = refs[:6], refs[6], refs[7]
+    loads = [pltpu.make_async_copy(ref, kv.at[pl.ds(8 * i, 8)], sem.at[i]) for i, ref in enumerate(bufs)]
+    for cp in loads:
+        cp.start()
+    for cp in loads:
+        cp.wait()
+
+
+def stage_call(bufs):
+    return pl.pallas_call(
+        stage_kernel,
+        out_shape=pltpu.VMEM((48, BP + 16, LR), bf16),
+        in_specs=[spec(HB)] * 6,
+        out_specs=spec(VM),
+        scratch_shapes=[pltpu.SemaphoreType.DMA((6,))],
+        name="stage",
+        compiler_params=grant(54),
+    )(*there(*bufs))
+
+
+def absorb_kernel(q, keys, q_s):
+    lane = lax.broadcasted_iota(jnp.int32, (B, 128), 1)
     for p in range(8):
         t0 = q[3 * p].astype(f32)
-        t1 = pltpu.roll(q[3 * p + 1].astype(f32), 64, 1)
+        r0 = q[3 * p + 1].astype(f32)
+        t1 = pltpu.roll(r0, 64, 1)
         t2 = pltpu.roll(q[3 * p + 2].astype(f32), 64, 1)
-        r0 = q[3 * p + 1].astype(f32)
         nopes = (t0, jnp.where(lane < ROT, t1, t2))
         ropes = (jnp.where(lane < ROT, r0, 0.0), jnp.where(lane < ROT, t2, 0.0))
         for j in range(2):
             h = 2 * p + j
             lat = lax.dot_general(
                 nopes[j].astype(bf16),
-                keys_v[:, 128 * h : 128 * h + 128],
+                keys[:, 128 * h : 128 * h + 128],
                 (((1,), (1,)), ((), ())),
                 preferred_element_type=f32,
             )
             q_s[:, h, :LR] = (lat * SCALE).astype(bf16).astype(f32)
             q_s[:, h, LR:] = ropes[j]
 
-    fetch.wait()
-
-    def scores(g, _):
-        here = kv.at[pl.ds(16 * g, 16)]
-        pltpu.make_async_copy(here, here, sem.at[g]).wait()
+
+def absorb_call(q, keys):
+    return pl.pallas_call(
+        absorb_kernel,
+        out_shape=pltpu.VMEM((B, 16, LR + 128), f32),
+        in_specs=[spec(VM)] * 2,
+        out_specs=spec(VM),
+        name="absorb",
+        compiler_params=grant(54),
+    )(*here(q, keys))
+
+
+def attend_kernel(slots, q_s, wide, kv, late_a, late_b, out, kvb, s_s, p_s, mix_s, o_s, inv, tsem, sem):
+    fetch = pltpu.make_async_copy(slots, inv, tsem)
+    fetch.start()
+    late = [pltpu.make_async_copy(ref, kvb.at[pl.ds(8 * i, 8)], sem.at[i]) for i, ref in enumerate((late_a, late_b))]
+    for cp in late:
+        cp.start()
+    s, y, c = place_of()
+    lane = lax.broadcasted_iota(jnp.int32, (B, BP), 1)
+
+    def first_of(g, dc):
+        cs = c if dc == 0 else 1 - c
+        alpha = 3 - 2 * cs
+        dy = jnp.where(g == 0, 0, jnp.where(g == 1, alpha, jnp.where(g == 2, 2, 4 - alpha)))
+        return (lax.rem(y + dy, 4) * 2 + cs) * 8
+
+    def scores(ref, base, g):
         for dc in range(2):
-            cs = c if dc == 0 else 1 - c
-            alpha = 3 - 2 * cs
-            dy = jnp.where(g == 0, 0, jnp.where(g == 1, alpha, jnp.where(g == 2, 2, 4 - alpha)))
-            first = (lax.rem(y + dy, 4) * 2 + cs) * 8
+            first = first_of(g, dc)
             for k in range(8):
-                at = g * 16 + dc * 8 + k
+                at = base + dc * 8 + k
                 e = inv[first + k]
-                place[e] = at
                 qb = q_s[e // 4].astype(bf16)
-                keys = kv[at, :BP, :]
-                rope = jnp.concatenate([kv[at, BP:, 128 * n : 128 * n + 128] for n in range(4)], axis=0)
+                keys = ref[at, :BP, :]
+                rope = jnp.concatenate([ref[at, BP:, 128 * n : 128 * n + 128] for n in range(4)], axis=0)
                 sc = lax.dot_general(qb[:, :LR], keys, (((1,), (1,)), ((), ())), preferred_element_type=f32)
                 s_s[e] = sc + jnp.dot(qb[:, LR : LR + ROT], rope, preferred_element_type=f32)
-        return 0
-
-    lax.fori_loop(0, 4, scores, 0)
+
+    def mixing(ref, base, g):
+        for dc in range(2):
+            first = first_of(g, dc)
+            for k in range(8):
+                e = inv[first + k]
+                b = e // 4
+                got = jnp.dot(p_s[e], ref[base + dc * 8 + k, :BP, :], preferred_element_type=f32)
+                mix_s[b] = mix_s[b] + got
+
+    def groups(step):
+        def early(g, _):
+            step(kv, 16 * g, g)
+            return 0
+
+        lax.fori_loop(0, 3, early, 0)
+
+    fetch.wait()
+    groups(scores)
+    for cp in late:
+        cp.wait()
+    scores(kvb, 0, jnp.int32(3))
 
     def softmax(bh, r):
         b = bh * 8 + r
@@ -301,17 +361,12 @@
         for n, v in enumerate((m1, m2, m3, l1, l2, l3)):
             stats = jnp.where(lane == n, v, stats)
         o_s[pl.ds(bh * 16, 16), r, LR:] = stats
-        own_s[b] = new.astype(bf16).astype(f32) * wide[pl.ds(b, 1), :LR]
-        p_s[b] = jnp.concatenate(p, axis=1).astype(bf16)
-
-    def mixing(bh, r):
-        b = bh * 8 + r
-        p = p_s[b]
-        mix = own_s[b]
+        mix_s[b] = new.astype(bf16).astype(f32) * wide[pl.ds(b, 1), :LR]
         for j in range(4):
-            keys = kv[place[b * 4 + j], :BP, :]
-            mix = mix + jnp.dot(p[:, 128 * j : 128 * j + 128], keys, preferred_element_type=f32)
-        o_s[pl.ds(bh * 16, 16), r, :LR] = mix
+            p_s[b * 4 + j] = p[j].astype(bf16)
+
+    def spread(bh, r):
+        o_s[pl.ds(bh * 16, 16), r, :LR] = mix_s[bh * 8 + r]
 
     def halves(step):
         def both(bh, _):
@@ -322,7 +377,9 @@
         lax.fori_loop(0, 2, both, 0)
 
     halves(softmax)
-    halves(mixing)
+    groups(mixing)
+    mixing(kvb, 0, jnp.int32(3))
+    halves(spread)
 
     def pour(i, _):
         out[i] = o_s[i].astype(bf16)
@@ -331,26 +388,25 @@
     lax.fori_loop(0, 32, pour, 0, unroll=8)
 
 
-def attend_call(slots, q, wide, keys, bufs):
+def attend_call(slots, q, wide, kv, late):
     return pl.pallas_call(
         attend_kernel,
         out_shape=pltpu.VMEM((32, 8, LR + 128), bf16),
-        in_specs=[spec(HB)] + [spec(VM)] * 3 + [spec(HB)] * 8,
+        in_specs=[spec(HB)] + [spec(VM)] * 3 + [spec(HB)] * 2,
         out_specs=spec(VM),
         scratch_shapes=[
-            pltpu.VMEM((64, BP + 16, LR), bf16),
-            pltpu.VMEM((B, B, LR + 128), f32),
+            pltpu.VMEM((16, BP + 16, LR), bf16),
             pltpu.VMEM((64, B, BP), f32),
-            pltpu.VMEM((B, B, 4 * BP), bf16),
+            pltpu.VMEM((64, B, BP), bf16),
+            pltpu.VMEM((B, B, LR), f32),
             pltpu.VMEM((32, 8, LR + 128), f32),
-            pltpu.VMEM((B, B, LR), f32),
-            pltpu.SMEM((64,), jnp.int32),
             pltpu.SMEM((128,), jnp.int32),
             pltpu.SemaphoreType.DMA,
-            pltpu.SemaphoreType.DMA((4,)),
+            pltpu.SemaphoreType.DMA((2,)),
         ],
         name="attend",
-    )(slots, *here(q, wide, keys), *(pltpu.with_memory_space_constraint(v, HB) for v in bufs))
+        compiler_params=grant(54),
+    )(*there(slots), *here(q, wide, kv), *there(*late))
 
 
 def value_kernel(parts, value_up, out, vals, sem):
@@ -411,7 +467,8 @@
         bufs += [value, lax.ppermute(value, "c", SWAP)]
     entry, wide, q_copies = query_call(parts, q_gain, kv_gain, cos, sin, q_tile)
     q_all = exchange(q_copies, S)
-    mixed = attend_call(slots_call(table, lengths), q_all, wide, keys_call(key_up), bufs)
+    q_packs = absorb_call(q_all, keys_call(key_up))
+    mixed = attend_call(slots_call(table, lengths), q_packs, wide, stage_call(bufs[:6]), bufs[6:])
     spans = exchange(mixed, S)
     res = value_call(spans, value_up)
     res = exchange(res, S)

time: 137 us -> 140 us (1.022)
  starting transfers between devices: 24 us -> 30.7 us
  waiting for transfers between devices: 60.2 us -> 54.5 us
  Pallas kernels: 17.9 us -> 20.6 us
    ppermute x1, waiting for transfers between devices: 26.7 us -> 14.9 us  [body(): alpha = lax.ppermute(mine, T, ALPHA)]
    ppermute x1, waiting for transfers between devices: 16.6 us -> 25.4 us  [body(): far = lax.ppermute(alpha, T, ALPHA)]
    pallas_call x0 -> x2, Pallas kernels: none -> 3.81 us  [the longest x1 3.1 us: stage_call(): pl.pallas_call(stage_kernel, out_shape=pltpu.VMEM((48, BP + 16, LR), bf16...]
    all_to_all x2, starting transfers between devices: 16.9 us -> 19.4 us  [exchange(): return lax.all_to_all(pieces, axes, split_axis=0, concat_axis=0, tiled=True)]
    all_to_all x2, waiting for transfers between devices: 10.4 us -> 8.97 us  [exchange(): return lax.all_to_all(pieces, axes, split_axis=0, concat_axis=0, tiled=True)]
  transfers between devices with their start and end apart: 13 -> 13, of which waited for: 8 -> 8; matrix products, arithmetic and copies ran while one was open for 0% -> 0% of each run, Pallas kernels for 6% -> 9%
where the time goes in v7:
time: 140 us; the launch traced here: 138 us
  waiting for transfers between devices  54.5 us (39%)
  starting transfers between devices  30.7 us (22%)
  blocking collectives  30.2 us (22%)
  Pallas kernels  20.6 us (15%)
    all_to_all x2, blocking collectives, exchange(): return lax.all_to_all(pieces, axes, split_axis=0, concat_axis=0, tiled=True)  30.2 us
    ppermute x1, waiting for transfers between devices, body(): far = lax.ppermute(alpha, T, ALPHA)  25.4 us
    all_to_all x2, starting transfers between devices, exchange(): return lax.all_to_all(pieces, axes, split_axis=0, concat_axis=0, tiled=True)  19.4 us
    ppermute x1, waiting for transfers between devices, body(): alpha = lax.ppermute(mine, T, ALPHA)  14.9 us
    all_to_all x2, waiting for transfers between devices, exchange(): return lax.all_to_all(pieces, axes, split_axis=0, concat_axis=0, tiled=True)  8.97 us
    pallas_call x1, Pallas kernels, attend_call(): pl.pallas_call(attend_kernel, out_shape=pltpu.VMEM((32, 8, LR + 128), bf1...  6.17 us
    pallas_call x1, Pallas kernels, united_call(): pl.pallas_call(united_kernel, out_shape=pltpu.VMEM((B, cols), bf16), in_s...  3.14 us
    pallas_call x1, Pallas kernels, stage_call(): pl.pallas_call(stage_kernel, out_shape=pltpu.VMEM((48, BP + 16, LR), bf16...  3.1 us
  transfers between devices with their start and end apart: 13, of which 8 were waited for; matrix products, arithmetic and copies ran while one was open for 0% of the time, Pallas kernels for 9%

profile of v7, /device:TPU:8, one launch (start us, length us, event | category | flops | bytes accessed | tf_op | source)
XLA Modules:
  0.0 137.7 jit_solution(737077179200672770)
XLA Ops:
  0.6 0.0 copy-start.1
  0.6 1.4 pack.1.refs_0_
  2.0 0.0 copy-start
  2.0 1.7 %collective-permute-start.5 = (bf16[8,144,512]{2,1,0:T(8,128)(2,1)S(1)}, bf16[8,144,512]{2,1,0:T(8,128)(2,1)}, u32[]{:S(2)}, u32[]{:S(2)}) collective-permute-start(bf16[8,144,512]{2,1,0:T(8,128)(2,1)S(1)} %pack.1.refs_0_), channel_id=1, source_target_pairs={{0,2},{1,7},{2,4},{3,1},{4,6},{5,3},{6,0},{7,5},{8,10},{9,15},{10,... | collective-permute-start | bytes 3538952 | tf_op jit(solution)/shard_map/ppermute | solution.py:457
  3.7 14.9 %collective-permute-done.5.refs_2_ = bf16[8,144,512]{2,1,0:T(8,128)(2,1)} collective-permute-done((bf16[8,144,512]{2,1,0:T(8,128)(2,1)S(1)}, bf16[8,144,512]{2,1,0:T(8,128)(2,1)}, u32[]{:S(2)}, u32[]{:S(2)}) %collective-permute-start.5) | collective-permute-done | bytes 1179680 | tf_op jit(solution)/shard_map/ppermute | solution.py:457
  18.5 1.4 %collective-permute-start.7 = (bf16[8,144,512]{2,1,0:T(8,128)(2,1)}, bf16[8,144,512]{2,1,0:T(8,128)(2,1)}, u32[]{:S(2)}, u32[]{:S(2)}) collective-permute-start(bf16[8,144,512]{2,1,0:T(8,128)(2,1)} %collective-permute-done.5.refs_2_), channel_id=1, source_target_pairs={{0,2},{1,7},{2,4},{3,1},{4,6},{5,3},{6,0},{7,5},{8,10},{9,15},{10,... | collective-permute-start | bytes 3538952 | tf_op jit(solution)/shard_map/ppermute | solution.py:458
  20.0 1.8 %collective-permute-start.9 = (bf16[8,144,512]{2,1,0:T(8,128)(2,1)S(1)}, bf16[8,144,512]{2,1,0:T(8,128)(2,1)}, u32[]{:S(2)}, u32[]{:S(2)}) collective-permute-start(bf16[8,144,512]{2,1,0:T(8,128)(2,1)S(1)} %pack.1.refs_0_), channel_id=1, source_target_pairs={{2,0},{7,1},{4,2},{1,3},{6,4},{3,5},{0,6},{5,7},{10,8},{15,9},{12,... | collective-permute-start | bytes 3538952 | tf_op jit(solution)/shard_map/ppermute | solution.py:459
  21.8 0.0 collective-permute-start.4
  21.8 0.5 collective-permute-start.6
  22.3 25.4 %collective-permute-done.7.refs_4_ = bf16[8,144,512]{2,1,0:T(8,128)(2,1)} collective-permute-done((bf16[8,144,512]{2,1,0:T(8,128)(2,1)}, bf16[8,144,512]{2,1,0:T(8,128)(2,1)}, u32[]{:S(2)}, u32[]{:S(2)}) %collective-permute-start.7) | collective-permute-done | bytes 1179680 | tf_op jit(solution)/shard_map/ppermute | solution.py:458
  47.7 0.0 collective-permute-start.8
  47.7 0.0 collective-permute-done.9.late_a
  47.7 0.5 collective-permute-start.10
  48.2 0.0 copy-done.1
  48.2 0.8 tiles.1
  49.1 11.0 %all-to-all-start = ((bf16[32,48,128]{2,1,0:T(8,128)(2,1)}), bf16[32,48,128]{2,1,0:T(8,128)(2,1)S(1)}, u32[]{:S(2)}, u32[]{:S(2)}) async-start(bf16[32,48,128]{2,1,0:T(8,128)(2,1)} %tiles.1), calls=%async_computation | async-start | bytes 786432 | tf_op jit(solution)/shard_map/all_to_all | solution.py:48
  60.1 0.0 copy-start.4
  60.1 0.0 copy-start.2
  60.1 0.0 copy-start.3
  60.1 3.1 %united.1 = bf16[16,264]{1,0:T(8,128)(2,1)S(1)} custom-call(bf16[16,5120]{1,0:T(8,128)(2,1)} %hid_hbm.1, bf16[264,5120]{1,0:T(8,128)(2,1)} %bitcast.10), custom_call_target="tpu_custom_call" | custom-call | tf_op jit(solution)/shard_map/united/pallas_call | solution.py:78
  63.2 0.0 copy-done
  63.3 0.1 collective-permute-start
  63.4 1.2 collective-permute-done
  64.5 2.9 %collective-permute-start.1 = (bf16[2,16,264]{2,1,0:T(8,128)(2,1)S(1)}, bf16[2,16,264]{2,1,0:T(8,128)(2,1)S(1)}, u32[]{:S(2)}, u32[]{:S(2)}) collective-permute-start(bf16[2,16,264]{2,1,0:T(8,128)(2,1)S(1)} %pad_maximum_fusion.refs_0_), channel_id=1, source_target_pairs={{2,0},{7,1},{4,2},{1,3},{6,4},{3,5},{0,6},{5,7},{10,8},{15,9},{12,... | collective-permute-start | bytes 50696 | tf_op jit(solution)/shard_map/ppermute | solution.py:463
  67.4 1.5 %collective-permute-done.1.refs_1_ = bf16[2,16,264]{2,1,0:T(8,128)(2,1)S(1)} collective-permute-done((bf16[2,16,264]{2,1,0:T(8,128)(2,1)S(1)}, bf16[2,16,264]{2,1,0:T(8,128)(2,1)S(1)}, u32[]{:S(2)}, u32[]{:S(2)}) %collective-permute-start.1) | collective-permute-done | bytes 16928 | tf_op jit(solution)/shard_map/ppermute | solution.py:463
  68.9 0.0 collective-permute-start.2
  68.9 0.0 copy-done.4
  69.0 1.2 collective-permute-done.2.refs_2_
  70.1 2.5 %collective-permute-start.3 = (bf16[2,16,264]{2,1,0:T(8,128)(2,1)S(1)}, bf16[2,16,264]{2,1,0:T(8,128)(2,1)S(1)}, u32[]{:S(2)}, u32[]{:S(2)}) collective-permute-start(bf16[2,16,264]{2,1,0:T(8,128)(2,1)S(1)} %collective-permute-done.1.refs_1_), channel_id=1, source_target_pairs={{2,0},{7,1},{4,2},{1,3},{6,4},{3,5},{0,6},{5,7},{10,8},{15,9},{12,... | collective-permute-start | bytes 50696 | tf_op jit(solution)/shard_map/ppermute | solution.py:464
  72.6 0.1 multiply_sine_fusion
  72.7 1.4 %collective-permute-done.3.refs_3_ = bf16[2,16,264]{2,1,0:T(8,128)(2,1)S(1)} collective-permute-done((bf16[2,16,264]{2,1,0:T(8,128)(2,1)S(1)}, bf16[2,16,264]{2,1,0:T(8,128)(2,1)S(1)}, u32[]{:S(2)}, u32[]{:S(2)}) %collective-permute-start.3) | collective-permute-done | bytes 16928 | tf_op jit(solution)/shard_map/ppermute | solution.py:464
  74.1 1.4 %all-to-all-done.refs_8_ = bf16[32,48,128]{2,1,0:T(8,128)(2,1)S(1)} async-done(((bf16[32,48,128]{2,1,0:T(8,128)(2,1)}), bf16[32,48,128]{2,1,0:T(8,128)(2,1)S(1)}, u32[]{:S(2)}, u32[]{:S(2)}) %all-to-all-start) | async-done | bytes 393248 | tf_op jit(solution)/shard_map/all_to_all | solution.py:48
  75.5 0.0 copy-done.2
  75.5 0.0 copy-done.3
  75.5 1.1 query.1
  76.6 8.4 %all-to-all-start.1 = ((bf16[32,16,128]{2,1,0:T(8,128)(2,1)}), bf16[32,16,128]{2,1,0:T(8,128)(2,1)S(1)}, u32[]{:S(2)}, u32[]{:S(2)}) async-start(bf16[32,16,128]{2,1,0:T(8,128)(2,1)} %get-tuple-element.5), calls=%async_computation.1 | async-start | bytes 262144 | tf_op jit(solution)/shard_map/all_to_all | solution.py:48
  85.0 1.6 %keys.1 = bf16[512,2048]{1,0:T(8,128)(2,1)S(1)} custom-call(bf16[512,2048]{1,0:T(8,128)(2,1)} %src.1), custom_call_target="tpu_custom_call" | custom-call | tf_op jit(solution)/shard_map/keys/pallas_call | solution.py:229
  86.6 1.4 %slots.1 = s32[128]{0:T(128)} custom-call(s32[4,16]{1,0:T(4,128)} %bitcast.13, s32[16]{0:T(128)} %lengths.1), custom_call_target="tpu_custom_call" | custom-call | tf_op jit(solution)/shard_map/slots/pallas_call | solution.py:213
  88.0 7.6 %all-to-all-done.1.q = bf16[32,16,128]{2,1,0:T(8,128)(2,1)S(1)} async-done(((bf16[32,16,128]{2,1,0:T(8,128)(2,1)}), bf16[32,16,128]{2,1,0:T(8,128)(2,1)S(1)}, u32[]{:S(2)}, u32[]{:S(2)}) %all-to-all-start.1) | async-done | bytes 131104 | tf_op jit(solution)/shard_map/all_to_all | solution.py:48
  95.6 0.7 absorb.1.q_s
  96.3 0.0 collective-permute-done.4.refs_1_
  96.3 0.0 collective-permute-done.6.refs_3_
  96.4 0.0 collective-permute-done.8.refs_5_
  96.4 3.1 %stage.1.kv = bf16[48,144,512]{2,1,0:T(8,128)(2,1)S(1)} custom-call(bf16[8,144,512]{2,1,0:T(8,128)(2,1)} %copy-done, bf16[8,144,512]{2,1,0:T(8,128)(2,1)} %collective-permute-done.4.refs_1_, bf16[8,144,512]{2,1,0:T(8,128)(2,1)} %collective-permute-done.5.refs_2_, bf16[8,144,512]{2,1,0:T(8,128)(2,1)} %collective-permute-done.6.refs_3_, ...), custom_call_target="tpu_custom_call" | custom-call | tf_op jit(solution)/shard_map/stage/pallas_call | solution.py:250
  99.5 0.0 collective-permute-done.10.late_b
  99.5 6.2 %attend.1 = bf16[32,8,640]{2,1,0:T(8,128)(2,1)S(1)} custom-call(s32[128]{0:T(128)} %slots.1, f32[16,16,640]{2,1,0:T(8,128)S(1)} %absorb.1.q_s, f32[16,640]{1,0:T(8,128)S(1)} %get-tuple-element.6.wide, bf16[48,144,512]{2,1,0:T(8,128)(2,1)S(1)} %stage.1.kv, bf16[8,144,512]{2,1,0:T(8,128)(2,1)} %collective-permute-done.9.late_a, ...), custom_call_target="tpu_custom_call" | custom-call | tf_op jit(solution)/shard_map/attend/pallas_call | solution.py:392
  105.7 16.4 %all_to_all.20.parts = bf16[32,8,640]{2,1,0:T(8,128)(2,1)S(1)} all-to-all(bf16[32,8,640]{2,1,0:T(8,128)(2,1)S(1)} %attend.1), channel_id=1, replica_groups=mesh['z'=8,'x'=4,'y'=4,'c'=2] {'z','x'}, dimensions={0} | all-to-all | bytes 655360 | tf_op jit(solution)/shard_map/all_to_all | solution.py:48
  122.1 1.2 value.1
  123.3 13.8 %all_to_all.21 = bf16[32,8,128]{2,1,0:T(8,128)(2,1)S(1)} all-to-all(bf16[32,8,128]{2,1,0:T(8,128)(2,1)S(1)} %value.1), channel_id=1, replica_groups=mesh['z'=8,'x'=4,'y'=4,'c'=2] {'z','x'}, dimensions={0} | all-to-all | bytes 131072 | tf_op jit(solution)/shard_map/all_to_all | solution.py:48
  137.1 0.6 copy.14
  (3 shorter events, 0.0 us)
Async XLA Ops:
  0.6 47.6 %copy-start.1 = (bf16[48,3072]{1,0:T(8,128)(2,1)S(1)}, bf16[48,3072]{1,0:T(8,128)(2,1)}, u32[]{:S(2)}) copy-start(bf16[48,3072]{1,0:T(8,128)(2,1)} %q_up.1) | copy-start | bytes 884740
  2.0 61.2 %copy-start = (bf16[8,144,512]{2,1,0:T(8,128)(2,1)}, bf16[8,144,512]{2,1,0:T(8,128)(2,1)S(1)}, u32[]{:S(2)}) copy-start(bf16[8,144,512]{2,1,0:T(8,128)(2,1)S(1)} %pack.1.refs_0_) | copy-start | bytes 3538948
  2.0 16.5 %collective-permute-start.5 = (bf16[8,144,512]{2,1,0:T(8,128)(2,1)S(1)}, bf16[8,144,512]{2,1,0:T(8,128)(2,1)}, u32[]{:S(2)}, u32[]{:S(2)}) collective-permute-start(bf16[8,144,512]{2,1,0:T(8,128)(2,1)S(1)} %pack.1.refs_0_), channel_id=1, source_target_pairs={{0,2},{1,7},{2,4},{3,1},{4,6},{5,3},{6,0},{7,5},{8,10},{9,15},{10,... | collective-permute-start | bytes 3538952 | tf_op jit(solution)/shard_map/ppermute | solution.py:457
  18.5 29.2 %collective-permute-start.7 = (bf16[8,144,512]{2,1,0:T(8,128)(2,1)}, bf16[8,144,512]{2,1,0:T(8,128)(2,1)}, u32[]{:S(2)}, u32[]{:S(2)}) collective-permute-start(bf16[8,144,512]{2,1,0:T(8,128)(2,1)} %collective-permute-done.5.refs_2_), channel_id=1, source_target_pairs={{0,2},{1,7},{2,4},{3,1},{4,6},{5,3},{6,0},{7,5},{8,10},{9,15},{10,... | collective-permute-start | bytes 3538952 | tf_op jit(solution)/shard_map/ppermute | solution.py:458
  20.0 27.7 %collective-permute-start.9 = (bf16[8,144,512]{2,1,0:T(8,128)(2,1)S(1)}, bf16[8,144,512]{2,1,0:T(8,128)(2,1)}, u32[]{:S(2)}, u32[]{:S(2)}) collective-permute-start(bf16[8,144,512]{2,1,0:T(8,128)(2,1)S(1)} %pack.1.refs_0_), channel_id=1, source_target_pairs={{2,0},{7,1},{4,2},{1,3},{6,4},{3,5},{0,6},{5,7},{10,8},{15,9},{12,... | collective-permute-start | bytes 3538952 | tf_op jit(solution)/shard_map/ppermute | solution.py:459
  21.8 74.6 %collective-permute-start.4 = (bf16[8,144,512]{2,1,0:T(8,128)(2,1)S(1)}, bf16[8,144,512]{2,1,0:T(8,128)(2,1)}, u32[]{:S(2)}, u32[]{:S(2)}) collective-permute-start(bf16[8,144,512]{2,1,0:T(8,128)(2,1)S(1)} %pack.1.refs_0_), channel_id=1, source_target_pairs={{0,1},{1,0},{2,3},{3,2},{4,5},{5,4},{6,7},{7,6},{8,9},{9,8},{10,11... | collective-permute-start | bytes 3538952 | tf_op jit(solution)/shard_map/ppermute | solution.py:467
  21.8 74.6 %collective-permute-start.6 = (bf16[8,144,512]{2,1,0:T(8,128)(2,1)}, bf16[8,144,512]{2,1,0:T(8,128)(2,1)}, u32[]{:S(2)}, u32[]{:S(2)}) collective-permute-start(bf16[8,144,512]{2,1,0:T(8,128)(2,1)} %collective-permute-done.5.refs_2_), channel_id=1, source_target_pairs={{0,1},{1,0},{2,3},{3,2},{4,5},{5,4},{6,7},{7,6},{8,9},{9,8},{10,11... | collective-permute-start | bytes 3538952 | tf_op jit(solution)/shard_map/ppermute | solution.py:467
  47.7 48.6 %collective-permute-start.8 = (bf16[8,144,512]{2,1,0:T(8,128)(2,1)}, bf16[8,144,512]{2,1,0:T(8,128)(2,1)}, u32[]{:S(2)}, u32[]{:S(2)}) collective-permute-start(bf16[8,144,512]{2,1,0:T(8,128)(2,1)} %collective-permute-done.7.refs_4_), channel_id=1, source_target_pairs={{0,1},{1,0},{2,3},{3,2},{4,5},{5,4},{6,7},{7,6},{8,9},{9,8},{10,11... | collective-permute-start | bytes 3538952 | tf_op jit(solution)/shard_map/ppermute | solution.py:467
  47.7 51.7 %collective-permute-start.10 = (bf16[8,144,512]{2,1,0:T(8,128)(2,1)}, bf16[8,144,512]{2,1,0:T(8,128)(2,1)}, u32[]{:S(2)}, u32[]{:S(2)}) collective-permute-start(bf16[8,144,512]{2,1,0:T(8,128)(2,1)} %collective-permute-done.9.late_a), channel_id=1, source_target_pairs={{0,1},{1,0},{2,3},{3,2},{4,5},{5,4},{6,7},{7,6},{8,9},{9,8},{10,11... | collective-permute-start | bytes 3538952 | tf_op jit(solution)/shard_map/ppermute | solution.py:467
  49.1 26.5 %all-to-all-start = ((bf16[32,48,128]{2,1,0:T(8,128)(2,1)}), bf16[32,48,128]{2,1,0:T(8,128)(2,1)S(1)}, u32[]{:S(2)}, u32[]{:S(2)}) async-start(bf16[32,48,128]{2,1,0:T(8,128)(2,1)} %tiles.1), calls=%async_computation | async-start | bytes 786432 | tf_op jit(solution)/shard_map/all_to_all | solution.py:48
  60.1 8.9 %copy-start.4 = (s32[16]{0:T(128)S(1)}, s32[16]{0:T(128)}, u32[]{:S(2)}) copy-start(s32[16]{0:T(128)} %lengths.1) | copy-start | bytes 196
  60.1 15.5 %copy-start.2 = (f32[1536]{0:T(1024)S(1)}, f32[1536]{0:T(1024)}, u32[]{:S(2)}) copy-start(f32[1536]{0:T(1024)} %refs_4_.1) | copy-start | bytes 18436
  60.1 15.4 %copy-start.3 = (f32[512]{0:T(512)S(1)}, f32[512]{0:T(512)}, u32[]{:S(2)}) copy-start(f32[512]{0:T(512)} %refs_5_.1) | copy-start | bytes 6148
  63.3 1.3 collective-permute-start
  64.5 4.4 %collective-permute-start.1 = (bf16[2,16,264]{2,1,0:T(8,128)(2,1)S(1)}, bf16[2,16,264]{2,1,0:T(8,128)(2,1)S(1)}, u32[]{:S(2)}, u32[]{:S(2)}) collective-permute-start(bf16[2,16,264]{2,1,0:T(8,128)(2,1)S(1)} %pad_maximum_fusion.refs_0_), channel_id=1, source_target_pairs={{2,0},{7,1},{4,2},{1,3},{6,4},{3,5},{0,6},{5,7},{10,8},{15,9},{12,... | collective-permute-start | bytes 50696 | tf_op jit(solution)/shard_map/ppermute | solution.py:463
  68.9 1.2 collective-permute-start.2
  70.1 4.0 %collective-permute-start.3 = (bf16[2,16,264]{2,1,0:T(8,128)(2,1)S(1)}, bf16[2,16,264]{2,1,0:T(8,128)(2,1)S(1)}, u32[]{:S(2)}, u32[]{:S(2)}) collective-permute-start(bf16[2,16,264]{2,1,0:T(8,128)(2,1)S(1)} %collective-permute-done.1.refs_1_), channel_id=1, source_target_pairs={{2,0},{7,1},{4,2},{1,3},{6,4},{3,5},{0,6},{5,7},{10,8},{15,9},{12,... | collective-permute-start | bytes 50696 | tf_op jit(solution)/shard_map/ppermute | solution.py:464
  76.6 19.0 %all-to-all-start.1 = ((bf16[32,16,128]{2,1,0:T(8,128)(2,1)}), bf16[32,16,128]{2,1,0:T(8,128)(2,1)S(1)}, u32[]{:S(2)}, u32[]{:S(2)}) async-start(bf16[32,16,128]{2,1,0:T(8,128)(2,1)} %get-tuple-element.5), calls=%async_computation.1 | async-start | bytes 262144 | tf_op jit(solution)/shard_map/all_to_all | solution.py:48

commit v8 on v6

--- a/solution.py
+++ b/solution.py
@@ -34,6 +34,10 @@
 
 def here(*values):
     return tuple(pltpu.with_memory_space_constraint(v, VM) for v in values)
+
+
+def there(*values):
+    return tuple(pltpu.with_memory_space_constraint(v, HB) for v in values)
 
 
 def exchange(pieces, axes):
@@ -225,37 +229,50 @@
         out_specs=spec(VM),
         scratch_shapes=[pltpu.SemaphoreType.DMA],
         name="keys",
-    )(key_up)
-
-
-def attend_kernel(slots, q, wide, keys_v, *rest):
-    bufs, out = rest[:8], rest[8]
-    kv, q_s, s_s, p_s, o_s, own_s, place, inv, tsem, sem = rest[9:]
-    fetch = pltpu.make_async_copy(slots, inv, tsem)
-    fetch.start()
-    s, y, c = place_of()
-    for i in range(8):
-        pltpu.make_async_copy(bufs[i], kv.at[pl.ds(8 * i, 8)], sem.at[i // 2]).start()
-
-    lane = lax.broadcasted_iota(jnp.int32, (B, BP), 1)
+    )(*there(key_up))
+
+
+def absorb_kernel(q, keys, q_s):
+    lane = lax.broadcasted_iota(jnp.int32, (B, 128), 1)
     for p in range(8):
         t0 = q[3 * p].astype(f32)
-        t1 = pltpu.roll(q[3 * p + 1].astype(f32), 64, 1)
+        r0 = q[3 * p + 1].astype(f32)
+        t1 = pltpu.roll(r0, 64, 1)
         t2 = pltpu.roll(q[3 * p + 2].astype(f32), 64, 1)
-        r0 = q[3 * p + 1].astype(f32)
         nopes = (t0, jnp.where(lane < ROT, t1, t2))
         ropes = (jnp.where(lane < ROT, r0, 0.0), jnp.where(lane < ROT, t2, 0.0))
         for j in range(2):
             h = 2 * p + j
             lat = lax.dot_general(
                 nopes[j].astype(bf16),
-                keys_v[:, 128 * h : 128 * h + 128],
+                keys[:, 128 * h : 128 * h + 128],
                 (((1,), (1,)), ((), ())),
                 preferred_element_type=f32,
             )
             q_s[:, h, :LR] = (lat * SCALE).astype(bf16).astype(f32)
             q_s[:, h, LR:] = ropes[j]
 
+
+def absorb_call(q, keys):
+    return pl.pallas_call(
+        absorb_kernel,
+        out_shape=pltpu.VMEM((B, 16, LR + 128), f32),
+        in_specs=[spec(VM)] * 2,
+        out_specs=spec(VM),
+        name="absorb",
+    )(*here(q, keys))
+
+
+def attend_kernel(slots, q_s, wide, *rest):
+    bufs, out = rest[:8], rest[8]
+    kv, s_s, p_s, o_s, own_s, place, inv, tsem, sem = rest[9:]
+    fetch = pltpu.make_async_copy(slots, inv, tsem)
+    fetch.start()
+    s, y, c = place_of()
+    for i in range(8):
+        pltpu.make_async_copy(bufs[i], kv.at[pl.ds(8 * i, 8)], sem.at[i // 2]).start()
+
+    lane = lax.broadcasted_iota(jnp.int32, (B, BP), 1)
     fetch.wait()
 
     def scores(g, _):
@@ -331,15 +348,14 @@
     lax.fori_loop(0, 32, pour, 0, unroll=8)
 
 
-def attend_call(slots, q, wide, keys, bufs):
+def attend_call(slots, q, wide, bufs):
     return pl.pallas_call(
         attend_kernel,
         out_shape=pltpu.VMEM((32, 8, LR + 128), bf16),
-        in_specs=[spec(HB)] + [spec(VM)] * 3 + [spec(HB)] * 8,
+        in_specs=[spec(HB)] + [spec(VM)] * 2 + [spec(HB)] * 8,
         out_specs=spec(VM),
         scratch_shapes=[
             pltpu.VMEM((64, BP + 16, LR), bf16),
-            pltpu.VMEM((B, B, LR + 128), f32),
             pltpu.VMEM((64, B, BP), f32),
             pltpu.VMEM((B, B, 4 * BP), bf16),
             pltpu.VMEM((32, 8, LR + 128), f32),
@@ -350,7 +366,7 @@
             pltpu.SemaphoreType.DMA((4,)),
         ],
         name="attend",
-    )(slots, *here(q, wide, keys), *(pltpu.with_memory_space_constraint(v, HB) for v in bufs))
+    )(*there(slots), *here(q, wide), *there(*bufs))
 
 
 def value_kernel(parts, value_up, out, vals, sem):
@@ -411,7 +427,8 @@
         bufs += [value, lax.ppermute(value, "c", SWAP)]
     entry, wide, q_copies = query_call(parts, q_gain, kv_gain, cos, sin, q_tile)
     q_all = exchange(q_copies, S)
-    mixed = attend_call(slots_call(table, lengths), q_all, wide, keys_call(key_up), bufs)
+    q_packs = absorb_call(q_all, keys_call(key_up))
+    mixed = attend_call(slots_call(table, lengths), q_packs, wide, bufs)
     spans = exchange(mixed, S)
     res = value_call(spans, value_up)
     res = exchange(res, S)

time: 137 us -> 136 us (level)
  transfers between devices with their start and end apart: 13 -> 13, of which waited for: 8 -> 8; matrix products, arithmetic and copies ran while one was open for 0% -> 0% of each run, Pallas kernels for 6% -> 7%
where the time goes in v8:
time: 136 us; the launch traced here: 134 us
  waiting for transfers between devices  59.8 us (44%)
  blocking collectives  29.5 us (22%)
  starting transfers between devices  24.2 us (18%)
  Pallas kernels  19.1 us (14%)
    all_to_all x2, blocking collectives, exchange(): return lax.all_to_all(pieces, axes, split_axis=0, concat_axis=0, tiled=True)  29.5 us
    ppermute x1, waiting for transfers between devices, body(): alpha = lax.ppermute(mine, T, ALPHA)  26.8 us
    all_to_all x2, starting transfers between devices, exchange(): return lax.all_to_all(pieces, axes, split_axis=0, concat_axis=0, tiled=True)  16.9 us
    ppermute x1, waiting for transfers between devices, body(): far = lax.ppermute(alpha, T, ALPHA)  16.6 us
    all_to_all x2, waiting for transfers between devices, exchange(): return lax.all_to_all(pieces, axes, split_axis=0, concat_axis=0, tiled=True)  10.2 us
    pallas_call x1, Pallas kernels, attend_call(): pl.pallas_call(attend_kernel, out_shape=pltpu.VMEM((32, 8, LR + 128), bf1...  6.69 us
    pallas_call x1, Pallas kernels, united_call(): pl.pallas_call(united_kernel, out_shape=pltpu.VMEM((B, cols), bf16), in_s...  3.14 us
  transfers between devices with their start and end apart: 13, of which 8 were waited for; matrix products, arithmetic and copies ran while one was open for 0% of the time, Pallas kernels for 7%

profile of v8, /device:TPU:8, one launch (start us, length us, event | category | flops | bytes accessed | tf_op | source)
XLA Modules:
  0.0 134.2 jit_solution(13491524224789219906)
XLA Ops:
  0.6 0.0 copy-start
  0.6 2.4 %pack.1.rest_0_ = bf16[8,144,512]{2,1,0:T(8,128)(2,1)} custom-call(bf16[8,128,512]{2,1,0:T(8,128)(2,1)} %lat.1, bf16[8,64,128]{2,1,0:T(8,128)(2,1)} %rope.1), custom_call_target="tpu_custom_call" | custom-call | tf_op jit(solution)/shard_map/pack/pallas_call | solution.py:118
  3.0 1.7 %collective-permute-start.5 = (bf16[8,144,512]{2,1,0:T(8,128)(2,1)}, bf16[8,144,512]{2,1,0:T(8,128)(2,1)}, u32[]{:S(2)}, u32[]{:S(2)}) collective-permute-start(bf16[8,144,512]{2,1,0:T(8,128)(2,1)} %pack.1.rest_0_), channel_id=1, source_target_pairs={{0,2},{1,7},{2,4},{3,1},{4,6},{5,3},{6,0},{7,5},{8,10},{9,15},{10,... | collective-permute-start | bytes 3538952 | tf_op jit(solution)/shard_map/ppermute | solution.py:417
  4.7 0.7 collective-permute-start.9
  5.4 26.8 %collective-permute-done.5.rest_2_ = bf16[8,144,512]{2,1,0:T(8,128)(2,1)} collective-permute-done((bf16[8,144,512]{2,1,0:T(8,128)(2,1)}, bf16[8,144,512]{2,1,0:T(8,128)(2,1)}, u32[]{:S(2)}, u32[]{:S(2)}) %collective-permute-start.5) | collective-permute-done | bytes 1179680 | tf_op jit(solution)/shard_map/ppermute | solution.py:417
  32.2 0.7 collective-permute-start.7
  32.9 0.0 collective-permute-start.4
  32.9 0.5 collective-permute-start.6
  33.4 0.0 collective-permute-done.9.rest_6_
  33.4 0.0 collective-permute-start.10
  33.4 16.6 %collective-permute-done.7.rest_4_ = bf16[8,144,512]{2,1,0:T(8,128)(2,1)} collective-permute-done((bf16[8,144,512]{2,1,0:T(8,128)(2,1)}, bf16[8,144,512]{2,1,0:T(8,128)(2,1)}, u32[]{:S(2)}, u32[]{:S(2)}) %collective-permute-start.7) | collective-permute-done | bytes 1179680 | tf_op jit(solution)/shard_map/ppermute | solution.py:418
  50.0 0.0 collective-permute-start.8
  50.0 0.0 copy-done
  50.0 0.8 tiles.1
  50.9 9.7 %all-to-all-start = ((bf16[32,48,128]{2,1,0:T(8,128)(2,1)}), bf16[32,48,128]{2,1,0:T(8,128)(2,1)S(1)}, u32[]{:S(2)}, u32[]{:S(2)}) async-start(bf16[32,48,128]{2,1,0:T(8,128)(2,1)} %tiles.1), calls=%async_computation | async-start | bytes 786432 | tf_op jit(solution)/shard_map/all_to_all | solution.py:44
  60.6 0.0 copy-start.3
  60.6 0.0 copy-start.1
  60.7 0.0 copy-start.2
  60.7 3.1 %united.1 = bf16[16,264]{1,0:T(8,128)(2,1)S(1)} custom-call(bf16[16,5120]{1,0:T(8,128)(2,1)} %hid_hbm.1, bf16[264,5120]{1,0:T(8,128)(2,1)} %bitcast.10), custom_call_target="tpu_custom_call" | custom-call | tf_op jit(solution)/shard_map/united/pallas_call | solution.py:74
  63.8 0.3 collective-permute-start
  64.1 1.0 collective-permute-done
  65.1 1.7 %collective-permute-start.1 = (bf16[2,16,264]{2,1,0:T(8,128)(2,1)S(1)}, bf16[2,16,264]{2,1,0:T(8,128)(2,1)S(1)}, u32[]{:S(2)}, u32[]{:S(2)}) collective-permute-start(bf16[2,16,264]{2,1,0:T(8,128)(2,1)S(1)} %pad_maximum_fusion.refs_0_), channel_id=1, source_target_pairs={{2,0},{7,1},{4,2},{1,3},{6,4},{3,5},{0,6},{5,7},{10,8},{15,9},{12,... | collective-permute-start | bytes 50696 | tf_op jit(solution)/shard_map/ppermute | solution.py:423
  66.8 2.2 %collective-permute-done.1.refs_1_ = bf16[2,16,264]{2,1,0:T(8,128)(2,1)S(1)} collective-permute-done((bf16[2,16,264]{2,1,0:T(8,128)(2,1)S(1)}, bf16[2,16,264]{2,1,0:T(8,128)(2,1)S(1)}, u32[]{:S(2)}, u32[]{:S(2)}) %collective-permute-start.1) | collective-permute-done | bytes 16928 | tf_op jit(solution)/shard_map/ppermute | solution.py:423
  69.0 0.0 collective-permute-start.2
  69.0 0.0 copy-done.3
  69.0 1.2 collective-permute-done.2.refs_2_
  70.2 1.8 %collective-permute-start.3 = (bf16[2,16,264]{2,1,0:T(8,128)(2,1)S(1)}, bf16[2,16,264]{2,1,0:T(8,128)(2,1)S(1)}, u32[]{:S(2)}, u32[]{:S(2)}) collective-permute-start(bf16[2,16,264]{2,1,0:T(8,128)(2,1)S(1)} %collective-permute-done.1.refs_1_), channel_id=1, source_target_pairs={{2,0},{7,1},{4,2},{1,3},{6,4},{3,5},{0,6},{5,7},{10,8},{15,9},{12,... | collective-permute-start | bytes 50696 | tf_op jit(solution)/shard_map/ppermute | solution.py:424
  72.0 0.1 multiply_sine_fusion
  72.2 1.9 %collective-permute-done.3.refs_3_ = bf16[2,16,264]{2,1,0:T(8,128)(2,1)S(1)} collective-permute-done((bf16[2,16,264]{2,1,0:T(8,128)(2,1)S(1)}, bf16[2,16,264]{2,1,0:T(8,128)(2,1)S(1)}, u32[]{:S(2)}, u32[]{:S(2)}) %collective-permute-start.3) | collective-permute-done | bytes 16928 | tf_op jit(solution)/shard_map/ppermute | solution.py:424
  74.0 2.6 %all-to-all-done.refs_8_ = bf16[32,48,128]{2,1,0:T(8,128)(2,1)S(1)} async-done(((bf16[32,48,128]{2,1,0:T(8,128)(2,1)}), bf16[32,48,128]{2,1,0:T(8,128)(2,1)S(1)}, u32[]{:S(2)}, u32[]{:S(2)}) %all-to-all-start) | async-done | bytes 393248 | tf_op jit(solution)/shard_map/all_to_all | solution.py:44
  76.7 0.0 copy-done.1
  76.7 0.0 copy-done.2
  76.7 1.1 query.1
  77.8 7.1 %all-to-all-start.1 = ((bf16[32,16,128]{2,1,0:T(8,128)(2,1)}), bf16[32,16,128]{2,1,0:T(8,128)(2,1)S(1)}, u32[]{:S(2)}, u32[]{:S(2)}) async-start(bf16[32,16,128]{2,1,0:T(8,128)(2,1)} %get-tuple-element.5), calls=%async_computation.1 | async-start | bytes 262144 | tf_op jit(solution)/shard_map/all_to_all | solution.py:44
  84.9 1.6 %keys.1 = bf16[512,2048]{1,0:T(8,128)(2,1)S(1)} custom-call(bf16[512,2048]{1,0:T(8,128)(2,1)} %src.1), custom_call_target="tpu_custom_call" | custom-call | tf_op jit(solution)/shard_map/keys/pallas_call | solution.py:225
  86.5 1.4 %slots.1 = s32[128]{0:T(128)} custom-call(s32[4,16]{1,0:T(4,128)} %bitcast.13, s32[16]{0:T(128)} %lengths.1), custom_call_target="tpu_custom_call" | custom-call | tf_op jit(solution)/shard_map/slots/pallas_call | solution.py:209
  88.0 7.5 %all-to-all-done.1.q = bf16[32,16,128]{2,1,0:T(8,128)(2,1)S(1)} async-done(((bf16[32,16,128]{2,1,0:T(8,128)(2,1)}), bf16[32,16,128]{2,1,0:T(8,128)(2,1)S(1)}, u32[]{:S(2)}, u32[]{:S(2)}) %all-to-all-start.1) | async-done | bytes 131104 | tf_op jit(solution)/shard_map/all_to_all | solution.py:44
  95.5 0.7 absorb.1.q_s
  96.2 0.0 collective-permute-done.4.rest_1_
  96.2 0.0 collective-permute-done.6.rest_3_
  96.2 0.0 collective-permute-done.10.rest_7_
  96.2 0.0 collective-permute-done.8.rest_5_
  96.2 6.7 %attend.1 = bf16[32,8,640]{2,1,0:T(8,128)(2,1)S(1)} custom-call(s32[128]{0:T(128)} %slots.1, f32[16,16,640]{2,1,0:T(8,128)S(1)} %absorb.1.q_s, f32[16,640]{1,0:T(8,128)S(1)} %get-tuple-element.6.wide, bf16[8,144,512]{2,1,0:T(8,128)(2,1)} %pack.1.rest_0_, bf16[8,144,512]{2,1,0:T(8,128)(2,1)} %collective-permute-done.4.rest_1_, ...), custom_call_target="tpu_custom_call" | custom-call | tf_op jit(solution)/shard_map/attend/pallas_call | solution.py:352
  102.9 16.0 %all_to_all.20.parts = bf16[32,8,640]{2,1,0:T(8,128)(2,1)S(1)} all-to-all(bf16[32,8,640]{2,1,0:T(8,128)(2,1)S(1)} %attend.1), channel_id=1, replica_groups=mesh['z'=8,'x'=4,'y'=4,'c'=2] {'z','x'}, dimensions={0} | all-to-all | bytes 655360 | tf_op jit(solution)/shard_map/all_to_all | solution.py:44
  118.9 1.2 value.1
  120.1 13.5 %all_to_all.21 = bf16[32,8,128]{2,1,0:T(8,128)(2,1)S(1)} all-to-all(bf16[32,8,128]{2,1,0:T(8,128)(2,1)S(1)} %value.1), channel_id=1, replica_groups=mesh['z'=8,'x'=4,'y'=4,'c'=2] {'z','x'}, dimensions={0} | all-to-all | bytes 131072 | tf_op jit(solution)/shard_map/all_to_all | solution.py:44
  133.6 0.6 copy.14
  (3 shorter events, 0.0 us)
Async XLA Ops:
  0.6 49.4 %copy-start = (bf16[48,3072]{1,0:T(8,128)(2,1)S(1)}, bf16[48,3072]{1,0:T(8,128)(2,1)}, u32[]{:S(2)}) copy-start(bf16[48,3072]{1,0:T(8,128)(2,1)} %q_up.1) | copy-start | bytes 884740
  3.0 29.2 %collective-permute-start.5 = (bf16[8,144,512]{2,1,0:T(8,128)(2,1)}, bf16[8,144,512]{2,1,0:T(8,128)(2,1)}, u32[]{:S(2)}, u32[]{:S(2)}) collective-permute-start(bf16[8,144,512]{2,1,0:T(8,128)(2,1)} %pack.1.rest_0_), channel_id=1, source_target_pairs={{0,2},{1,7},{2,4},{3,1},{4,6},{5,3},{6,0},{7,5},{8,10},{9,15},{10,... | collective-permute-start | bytes 3538952 | tf_op jit(solution)/shard_map/ppermute | solution.py:417
  4.7 28.7 %collective-permute-start.9 = (bf16[8,144,512]{2,1,0:T(8,128)(2,1)}, bf16[8,144,512]{2,1,0:T(8,128)(2,1)}, u32[]{:S(2)}, u32[]{:S(2)}) collective-permute-start(bf16[8,144,512]{2,1,0:T(8,128)(2,1)} %pack.1.rest_0_), channel_id=1, source_target_pairs={{2,0},{7,1},{4,2},{1,3},{6,4},{3,5},{0,6},{5,7},{10,8},{15,9},{12,... | collective-permute-start | bytes 3538952 | tf_op jit(solution)/shard_map/ppermute | solution.py:419
  32.2 17.8 %collective-permute-start.7 = (bf16[8,144,512]{2,1,0:T(8,128)(2,1)}, bf16[8,144,512]{2,1,0:T(8,128)(2,1)}, u32[]{:S(2)}, u32[]{:S(2)}) collective-permute-start(bf16[8,144,512]{2,1,0:T(8,128)(2,1)} %collective-permute-done.5.rest_2_), channel_id=1, source_target_pairs={{0,2},{1,7},{2,4},{3,1},{4,6},{5,3},{6,0},{7,5},{8,10},{9,15},{10,... | collective-permute-start | bytes 3538952 | tf_op jit(solution)/shard_map/ppermute | solution.py:418
  32.9 63.3 %collective-permute-start.4 = (bf16[8,144,512]{2,1,0:T(8,128)(2,1)}, bf16[8,144,512]{2,1,0:T(8,128)(2,1)}, u32[]{:S(2)}, u32[]{:S(2)}) collective-permute-start(bf16[8,144,512]{2,1,0:T(8,128)(2,1)} %pack.1.rest_0_), channel_id=1, source_target_pairs={{0,1},{1,0},{2,3},{3,2},{4,5},{5,4},{6,7},{7,6},{8,9},{9,8},{10,11... | collective-permute-start | bytes 3538952 | tf_op jit(solution)/shard_map/ppermute | solution.py:427
  32.9 63.3 %collective-permute-start.6 = (bf16[8,144,512]{2,1,0:T(8,128)(2,1)}, bf16[8,144,512]{2,1,0:T(8,128)(2,1)}, u32[]{:S(2)}, u32[]{:S(2)}) collective-permute-start(bf16[8,144,512]{2,1,0:T(8,128)(2,1)} %collective-permute-done.5.rest_2_), channel_id=1, source_target_pairs={{0,1},{1,0},{2,3},{3,2},{4,5},{5,4},{6,7},{7,6},{8,9},{9,8},{10,11... | collective-permute-start | bytes 3538952 | tf_op jit(solution)/shard_map/ppermute | solution.py:427
  33.4 62.8 %collective-permute-start.10 = (bf16[8,144,512]{2,1,0:T(8,128)(2,1)}, bf16[8,144,512]{2,1,0:T(8,128)(2,1)}, u32[]{:S(2)}, u32[]{:S(2)}) collective-permute-start(bf16[8,144,512]{2,1,0:T(8,128)(2,1)} %collective-permute-done.9.rest_6_), channel_id=1, source_target_pairs={{0,1},{1,0},{2,3},{3,2},{4,5},{5,4},{6,7},{7,6},{8,9},{9,8},{10,11... | collective-permute-start | bytes 3538952 | tf_op jit(solution)/shard_map/ppermute | solution.py:427
  50.0 46.2 %collective-permute-start.8 = (bf16[8,144,512]{2,1,0:T(8,128)(2,1)}, bf16[8,144,512]{2,1,0:T(8,128)(2,1)}, u32[]{:S(2)}, u32[]{:S(2)}) collective-permute-start(bf16[8,144,512]{2,1,0:T(8,128)(2,1)} %collective-permute-done.7.rest_4_), channel_id=1, source_target_pairs={{0,1},{1,0},{2,3},{3,2},{4,5},{5,4},{6,7},{7,6},{8,9},{9,8},{10,11... | collective-permute-start | bytes 3538952 | tf_op jit(solution)/shard_map/ppermute | solution.py:427
  50.9 25.8 %all-to-all-start = ((bf16[32,48,128]{2,1,0:T(8,128)(2,1)}), bf16[32,48,128]{2,1,0:T(8,128)(2,1)S(1)}, u32[]{:S(2)}, u32[]{:S(2)}) async-start(bf16[32,48,128]{2,1,0:T(8,128)(2,1)} %tiles.1), calls=%async_computation | async-start | bytes 786432 | tf_op jit(solution)/shard_map/all_to_all | solution.py:44
  60.6 8.4 %copy-start.3 = (s32[16]{0:T(128)S(1)}, s32[16]{0:T(128)}, u32[]{:S(2)}) copy-start(s32[16]{0:T(128)} %lengths.1) | copy-start | bytes 196
  60.6 16.0 %copy-start.1 = (f32[1536]{0:T(1024)S(1)}, f32[1536]{0:T(1024)}, u32[]{:S(2)}) copy-start(f32[1536]{0:T(1024)} %refs_4_.1) | copy-start | bytes 18436
  60.7 16.0 %copy-start.2 = (f32[512]{0:T(512)S(1)}, f32[512]{0:T(512)}, u32[]{:S(2)}) copy-start(f32[512]{0:T(512)} %refs_5_.1) | copy-start | bytes 6148
  63.8 1.3 collective-permute-start
  65.1 3.9 %collective-permute-start.1 = (bf16[2,16,264]{2,1,0:T(8,128)(2,1)S(1)}, bf16[2,16,264]{2,1,0:T(8,128)(2,1)S(1)}, u32[]{:S(2)}, u32[]{:S(2)}) collective-permute-start(bf16[2,16,264]{2,1,0:T(8,128)(2,1)S(1)} %pad_maximum_fusion.refs_0_), channel_id=1, source_target_pairs={{2,0},{7,1},{4,2},{1,3},{6,4},{3,5},{0,6},{5,7},{10,8},{15,9},{12,... | collective-permute-start | bytes 50696 | tf_op jit(solution)/shard_map/ppermute | solution.py:423
  69.0 1.2 collective-permute-start.2
  70.2 3.8 %collective-permute-start.3 = (bf16[2,16,264]{2,1,0:T(8,128)(2,1)S(1)}, bf16[2,16,264]{2,1,0:T(8,128)(2,1)S(1)}, u32[]{:S(2)}, u32[]{:S(2)}) collective-permute-start(bf16[2,16,264]{2,1,0:T(8,128)(2,1)S(1)} %collective-permute-done.1.refs_1_), channel_id=1, source_target_pairs={{2,0},{7,1},{4,2},{1,3},{6,4},{3,5},{0,6},{5,7},{10,8},{15,9},{12,... | collective-permute-start | bytes 50696 | tf_op jit(solution)/shard_map/ppermute | solution.py:424
  77.8 17.7 %all-to-all-start.1 = ((bf16[32,16,128]{2,1,0:T(8,128)(2,1)}), bf16[32,16,128]{2,1,0:T(8,128)(2,1)S(1)}, u32[]{:S(2)}, u32[]{:S(2)}) async-start(bf16[32,16,128]{2,1,0:T(8,128)(2,1)} %get-tuple-element.5), calls=%async_computation.1 | async-start | bytes 262144 | tf_op jit(solution)/shard_map/all_to_all | solution.py:44

commit v9 on v8

--- a/solution.py
+++ b/solution.py
@@ -26,6 +26,10 @@
 VM = pltpu.MemorySpace.VMEM
 SM = pltpu.MemorySpace.SMEM
 HB = pltpu.MemorySpace.HBM
+
+
+def grant(mib):
+    return pltpu.CompilerParams(vmem_limit_bytes=mib << 20)
 
 
 def spec(space):
@@ -229,6 +233,7 @@
         out_specs=spec(VM),
         scratch_shapes=[pltpu.SemaphoreType.DMA],
         name="keys",
+        compiler_params=grant(58),
     )(*there(key_up))
 
 
@@ -260,6 +265,7 @@
         in_specs=[spec(VM)] * 2,
         out_specs=spec(VM),
         name="absorb",
+        compiler_params=grant(58),
     )(*here(q, keys))
 
 
@@ -366,6 +372,7 @@
             pltpu.SemaphoreType.DMA((4,)),
         ],
         name="attend",
+        compiler_params=grant(58),
     )(*there(slots), *here(q, wide), *there(*bufs))
 
 

time: 136 us -> 135 us (level)
  no operation moved by 1% of the time
where the time goes in v9:
time: 135 us; the launch traced here: 133 us
  waiting for transfers between devices  59.7 us (44%)
  blocking collectives  29.4 us (22%)
  starting transfers between devices  24.2 us (18%)
  Pallas kernels  18 us (13%)
    all_to_all x2, blocking collectives, exchange(): return lax.all_to_all(pieces, axes, split_axis=0, concat_axis=0, tiled=True)  29.4 us
    ppermute x1, waiting for transfers between devices, body(): alpha = lax.ppermute(mine, T, ALPHA)  26.7 us
    all_to_all x2, starting transfers between devices, exchange(): return lax.all_to_all(pieces, axes, split_axis=0, concat_axis=0, tiled=True)  16.9 us
    ppermute x1, waiting for transfers between devices, body(): far = lax.ppermute(alpha, T, ALPHA)  16.6 us
    all_to_all x2, waiting for transfers between devices, exchange(): return lax.all_to_all(pieces, axes, split_axis=0, concat_axis=0, tiled=True)  10.1 us
    pallas_call x1, Pallas kernels, attend_call(): pl.pallas_call(attend_kernel, out_shape=pltpu.VMEM((32, 8, LR + 128), bf1...  6.69 us
    pallas_call x1, Pallas kernels, united_call(): pl.pallas_call(united_kernel, out_shape=pltpu.VMEM((B, cols), bf16), in_s...  3.14 us
  transfers between devices with their start and end apart: 13, of which 8 were waited for; matrix products, arithmetic and copies ran while one was open for 0% of the time, Pallas kernels for 7%

profile of v9, /device:TPU:8, one launch (start us, length us, event | category | flops | bytes accessed | tf_op | source)
XLA Modules:
  0.0 132.9 jit_solution(163216854723631205)
XLA Ops:
  0.6 0.0 copy-start.1
  0.6 1.4 %pack.1.rest_0_ = bf16[8,144,512]{2,1,0:T(8,128)(2,1)S(1)} custom-call(bf16[8,128,512]{2,1,0:T(8,128)(2,1)} %lat.1, bf16[8,64,128]{2,1,0:T(8,128)(2,1)} %rope.1), custom_call_target="tpu_custom_call" | custom-call | tf_op jit(solution)/shard_map/pack/pallas_call | solution.py:122
  2.0 0.0 copy-start
  2.0 1.7 %collective-permute-start.5 = (bf16[8,144,512]{2,1,0:T(8,128)(2,1)S(1)}, bf16[8,144,512]{2,1,0:T(8,128)(2,1)}, u32[]{:S(2)}, u32[]{:S(2)}) collective-permute-start(bf16[8,144,512]{2,1,0:T(8,128)(2,1)S(1)} %pack.1.rest_0_), channel_id=1, source_target_pairs={{0,2},{1,7},{2,4},{3,1},{4,6},{5,3},{6,0},{7,5},{8,10},{9,15},{10,... | collective-permute-start | bytes 3538952 | tf_op jit(solution)/shard_map/ppermute | solution.py:424
  3.7 0.7 collective-permute-start.9
  4.3 26.7 %collective-permute-done.5.rest_2_ = bf16[8,144,512]{2,1,0:T(8,128)(2,1)} collective-permute-done((bf16[8,144,512]{2,1,0:T(8,128)(2,1)S(1)}, bf16[8,144,512]{2,1,0:T(8,128)(2,1)}, u32[]{:S(2)}, u32[]{:S(2)}) %collective-permute-start.5) | collective-permute-done | bytes 1179680 | tf_op jit(solution)/shard_map/ppermute | solution.py:424
  31.0 0.6 collective-permute-start.7
  31.7 0.0 collective-permute-start.4
  31.7 0.5 collective-permute-start.6
  32.2 0.0 collective-permute-done.9.rest_6_
  32.2 0.0 collective-permute-start.10
  32.2 16.6 %collective-permute-done.7.rest_4_ = bf16[8,144,512]{2,1,0:T(8,128)(2,1)} collective-permute-done((bf16[8,144,512]{2,1,0:T(8,128)(2,1)}, bf16[8,144,512]{2,1,0:T(8,128)(2,1)}, u32[]{:S(2)}, u32[]{:S(2)}) %collective-permute-start.7) | collective-permute-done | bytes 1179680 | tf_op jit(solution)/shard_map/ppermute | solution.py:425
  48.8 0.0 collective-permute-start.8
  48.8 0.0 copy-done.1
  48.8 0.8 tiles.1
  49.6 9.8 %all-to-all-start = ((bf16[32,48,128]{2,1,0:T(8,128)(2,1)}), bf16[32,48,128]{2,1,0:T(8,128)(2,1)S(1)}, u32[]{:S(2)}, u32[]{:S(2)}) async-start(bf16[32,48,128]{2,1,0:T(8,128)(2,1)} %tiles.1), calls=%async_computation | async-start | bytes 786432 | tf_op jit(solution)/shard_map/all_to_all | solution.py:48
  59.4 0.0 copy-start.4
  59.4 0.0 copy-start.2
  59.4 0.0 copy-start.3
  59.4 3.1 %united.1 = bf16[16,264]{1,0:T(8,128)(2,1)S(1)} custom-call(bf16[16,5120]{1,0:T(8,128)(2,1)} %hid_hbm.1, bf16[264,5120]{1,0:T(8,128)(2,1)} %bitcast.10), custom_call_target="tpu_custom_call" | custom-call | tf_op jit(solution)/shard_map/united/pallas_call | solution.py:78
  62.6 0.0 copy-done
  62.6 0.3 collective-permute-start
  62.9 1.0 collective-permute-done
  63.9 1.7 %collective-permute-start.1 = (bf16[2,16,264]{2,1,0:T(8,128)(2,1)S(1)}, bf16[2,16,264]{2,1,0:T(8,128)(2,1)S(1)}, u32[]{:S(2)}, u32[]{:S(2)}) collective-permute-start(bf16[2,16,264]{2,1,0:T(8,128)(2,1)S(1)} %pad_maximum_fusion.refs_0_), channel_id=1, source_target_pairs={{2,0},{7,1},{4,2},{1,3},{6,4},{3,5},{0,6},{5,7},{10,8},{15,9},{12,... | collective-permute-start | bytes 50696 | tf_op jit(solution)/shard_map/ppermute | solution.py:430
  65.5 2.3 %collective-permute-done.1.refs_1_ = bf16[2,16,264]{2,1,0:T(8,128)(2,1)S(1)} collective-permute-done((bf16[2,16,264]{2,1,0:T(8,128)(2,1)S(1)}, bf16[2,16,264]{2,1,0:T(8,128)(2,1)S(1)}, u32[]{:S(2)}, u32[]{:S(2)}) %collective-permute-start.1) | collective-permute-done | bytes 16928 | tf_op jit(solution)/shard_map/ppermute | solution.py:430
  67.8 0.0 collective-permute-start.2
  67.8 0.0 copy-done.4
  67.8 1.2 collective-permute-done.2.refs_2_
  69.0 1.8 %collective-permute-start.3 = (bf16[2,16,264]{2,1,0:T(8,128)(2,1)S(1)}, bf16[2,16,264]{2,1,0:T(8,128)(2,1)S(1)}, u32[]{:S(2)}, u32[]{:S(2)}) collective-permute-start(bf16[2,16,264]{2,1,0:T(8,128)(2,1)S(1)} %collective-permute-done.1.refs_1_), channel_id=1, source_target_pairs={{2,0},{7,1},{4,2},{1,3},{6,4},{3,5},{0,6},{5,7},{10,8},{15,9},{12,... | collective-permute-start | bytes 50696 | tf_op jit(solution)/shard_map/ppermute | solution.py:431
  70.8 0.1 multiply_sine_fusion
  70.9 1.9 %collective-permute-done.3.refs_3_ = bf16[2,16,264]{2,1,0:T(8,128)(2,1)S(1)} collective-permute-done((bf16[2,16,264]{2,1,0:T(8,128)(2,1)S(1)}, bf16[2,16,264]{2,1,0:T(8,128)(2,1)S(1)}, u32[]{:S(2)}, u32[]{:S(2)}) %collective-permute-start.3) | collective-permute-done | bytes 16928 | tf_op jit(solution)/shard_map/ppermute | solution.py:431
  72.8 2.6 %all-to-all-done.refs_8_ = bf16[32,48,128]{2,1,0:T(8,128)(2,1)S(1)} async-done(((bf16[32,48,128]{2,1,0:T(8,128)(2,1)}), bf16[32,48,128]{2,1,0:T(8,128)(2,1)S(1)}, u32[]{:S(2)}, u32[]{:S(2)}) %all-to-all-start) | async-done | bytes 393248 | tf_op jit(solution)/shard_map/all_to_all | solution.py:48
  75.4 0.0 copy-done.2
  75.4 0.0 copy-done.3
  75.4 1.1 query.1
  76.5 7.2 %all-to-all-start.1 = ((bf16[32,16,128]{2,1,0:T(8,128)(2,1)}), bf16[32,16,128]{2,1,0:T(8,128)(2,1)S(1)}, u32[]{:S(2)}, u32[]{:S(2)}) async-start(bf16[32,16,128]{2,1,0:T(8,128)(2,1)} %get-tuple-element.5), calls=%async_computation.1 | async-start | bytes 262144 | tf_op jit(solution)/shard_map/all_to_all | solution.py:48
  83.7 1.6 %keys.1 = bf16[512,2048]{1,0:T(8,128)(2,1)S(1)} custom-call(bf16[512,2048]{1,0:T(8,128)(2,1)} %src.1), custom_call_target="tpu_custom_call" | custom-call | tf_op jit(solution)/shard_map/keys/pallas_call | solution.py:229
  85.3 1.4 %slots.1 = s32[128]{0:T(128)} custom-call(s32[4,16]{1,0:T(4,128)} %bitcast.13, s32[16]{0:T(128)} %lengths.1), custom_call_target="tpu_custom_call" | custom-call | tf_op jit(solution)/shard_map/slots/pallas_call | solution.py:213
  86.7 7.5 %all-to-all-done.1.q = bf16[32,16,128]{2,1,0:T(8,128)(2,1)S(1)} async-done(((bf16[32,16,128]{2,1,0:T(8,128)(2,1)}), bf16[32,16,128]{2,1,0:T(8,128)(2,1)S(1)}, u32[]{:S(2)}, u32[]{:S(2)}) %all-to-all-start.1) | async-done | bytes 131104 | tf_op jit(solution)/shard_map/all_to_all | solution.py:48
  94.2 0.7 absorb.1.q_s
  95.0 0.0 collective-permute-done.4.rest_1_
  95.0 0.0 collective-permute-done.6.rest_3_
  95.0 0.0 collective-permute-done.10.rest_7_
  95.0 0.0 collective-permute-done.8.rest_5_
  95.0 6.7 %attend.1 = bf16[32,8,640]{2,1,0:T(8,128)(2,1)S(1)} custom-call(s32[128]{0:T(128)} %slots.1, f32[16,16,640]{2,1,0:T(8,128)S(1)} %absorb.1.q_s, f32[16,640]{1,0:T(8,128)S(1)} %get-tuple-element.6.wide, bf16[8,144,512]{2,1,0:T(8,128)(2,1)} %copy-done, bf16[8,144,512]{2,1,0:T(8,128)(2,1)} %collective-permute-done.4.rest_1_, ...), custom_call_target="tpu_custom_call" | custom-call | tf_op jit(solution)/shard_map/attend/pallas_call | solution.py:358
  101.7 16.0 %all_to_all.20.parts = bf16[32,8,640]{2,1,0:T(8,128)(2,1)S(1)} all-to-all(bf16[32,8,640]{2,1,0:T(8,128)(2,1)S(1)} %attend.1), channel_id=1, replica_groups=mesh['z'=8,'x'=4,'y'=4,'c'=2] {'z','x'}, dimensions={0} | all-to-all | bytes 655360 | tf_op jit(solution)/shard_map/all_to_all | solution.py:48
  117.7 1.2 value.1
  118.9 13.5 %all_to_all.21 = bf16[32,8,128]{2,1,0:T(8,128)(2,1)S(1)} all-to-all(bf16[32,8,128]{2,1,0:T(8,128)(2,1)S(1)} %value.1), channel_id=1, replica_groups=mesh['z'=8,'x'=4,'y'=4,'c'=2] {'z','x'}, dimensions={0} | all-to-all | bytes 131072 | tf_op jit(solution)/shard_map/all_to_all | solution.py:48
  132.3 0.6 copy.14
  (3 shorter events, 0.0 us)
Async XLA Ops:
  0.6 48.2 %copy-start.1 = (bf16[48,3072]{1,0:T(8,128)(2,1)S(1)}, bf16[48,3072]{1,0:T(8,128)(2,1)}, u32[]{:S(2)}) copy-start(bf16[48,3072]{1,0:T(8,128)(2,1)} %q_up.1) | copy-start | bytes 884740
  2.0 60.6 %copy-start = (bf16[8,144,512]{2,1,0:T(8,128)(2,1)}, bf16[8,144,512]{2,1,0:T(8,128)(2,1)S(1)}, u32[]{:S(2)}) copy-start(bf16[8,144,512]{2,1,0:T(8,128)(2,1)S(1)} %pack.1.rest_0_) | copy-start | bytes 3538948
  2.0 29.0 %collective-permute-start.5 = (bf16[8,144,512]{2,1,0:T(8,128)(2,1)S(1)}, bf16[8,144,512]{2,1,0:T(8,128)(2,1)}, u32[]{:S(2)}, u32[]{:S(2)}) collective-permute-start(bf16[8,144,512]{2,1,0:T(8,128)(2,1)S(1)} %pack.1.rest_0_), channel_id=1, source_target_pairs={{0,2},{1,7},{2,4},{3,1},{4,6},{5,3},{6,0},{7,5},{8,10},{9,15},{10,... | collective-permute-start | bytes 3538952 | tf_op jit(solution)/shard_map/ppermute | solution.py:424
  3.7 28.5 %collective-permute-start.9 = (bf16[8,144,512]{2,1,0:T(8,128)(2,1)S(1)}, bf16[8,144,512]{2,1,0:T(8,128)(2,1)}, u32[]{:S(2)}, u32[]{:S(2)}) collective-permute-start(bf16[8,144,512]{2,1,0:T(8,128)(2,1)S(1)} %pack.1.rest_0_), channel_id=1, source_target_pairs={{2,0},{7,1},{4,2},{1,3},{6,4},{3,5},{0,6},{5,7},{10,8},{15,9},{12,... | collective-permute-start | bytes 3538952 | tf_op jit(solution)/shard_map/ppermute | solution.py:426
  31.0 17.8 %collective-permute-start.7 = (bf16[8,144,512]{2,1,0:T(8,128)(2,1)}, bf16[8,144,512]{2,1,0:T(8,128)(2,1)}, u32[]{:S(2)}, u32[]{:S(2)}) collective-permute-start(bf16[8,144,512]{2,1,0:T(8,128)(2,1)} %collective-permute-done.5.rest_2_), channel_id=1, source_target_pairs={{0,2},{1,7},{2,4},{3,1},{4,6},{5,3},{6,0},{7,5},{8,10},{9,15},{10,... | collective-permute-start | bytes 3538952 | tf_op jit(solution)/shard_map/ppermute | solution.py:425
  31.7 63.3 %collective-permute-start.4 = (bf16[8,144,512]{2,1,0:T(8,128)(2,1)S(1)}, bf16[8,144,512]{2,1,0:T(8,128)(2,1)}, u32[]{:S(2)}, u32[]{:S(2)}) collective-permute-start(bf16[8,144,512]{2,1,0:T(8,128)(2,1)S(1)} %pack.1.rest_0_), channel_id=1, source_target_pairs={{0,1},{1,0},{2,3},{3,2},{4,5},{5,4},{6,7},{7,6},{8,9},{9,8},{10,11... | collective-permute-start | bytes 3538952 | tf_op jit(solution)/shard_map/ppermute | solution.py:434
  31.7 63.3 %collective-permute-start.6 = (bf16[8,144,512]{2,1,0:T(8,128)(2,1)}, bf16[8,144,512]{2,1,0:T(8,128)(2,1)}, u32[]{:S(2)}, u32[]{:S(2)}) collective-permute-start(bf16[8,144,512]{2,1,0:T(8,128)(2,1)} %collective-permute-done.5.rest_2_), channel_id=1, source_target_pairs={{0,1},{1,0},{2,3},{3,2},{4,5},{5,4},{6,7},{7,6},{8,9},{9,8},{10,11... | collective-permute-start | bytes 3538952 | tf_op jit(solution)/shard_map/ppermute | solution.py:434
  32.2 62.8 %collective-permute-start.10 = (bf16[8,144,512]{2,1,0:T(8,128)(2,1)}, bf16[8,144,512]{2,1,0:T(8,128)(2,1)}, u32[]{:S(2)}, u32[]{:S(2)}) collective-permute-start(bf16[8,144,512]{2,1,0:T(8,128)(2,1)} %collective-permute-done.9.rest_6_), channel_id=1, source_target_pairs={{0,1},{1,0},{2,3},{3,2},{4,5},{5,4},{6,7},{7,6},{8,9},{9,8},{10,11... | collective-permute-start | bytes 3538952 | tf_op jit(solution)/shard_map/ppermute | solution.py:434
  48.8 46.2 %collective-permute-start.8 = (bf16[8,144,512]{2,1,0:T(8,128)(2,1)}, bf16[8,144,512]{2,1,0:T(8,128)(2,1)}, u32[]{:S(2)}, u32[]{:S(2)}) collective-permute-start(bf16[8,144,512]{2,1,0:T(8,128)(2,1)} %collective-permute-done.7.rest_4_), channel_id=1, source_target_pairs={{0,1},{1,0},{2,3},{3,2},{4,5},{5,4},{6,7},{7,6},{8,9},{9,8},{10,11... | collective-permute-start | bytes 3538952 | tf_op jit(solution)/shard_map/ppermute | solution.py:434
  49.6 25.8 %all-to-all-start = ((bf16[32,48,128]{2,1,0:T(8,128)(2,1)}), bf16[32,48,128]{2,1,0:T(8,128)(2,1)S(1)}, u32[]{:S(2)}, u32[]{:S(2)}) async-start(bf16[32,48,128]{2,1,0:T(8,128)(2,1)} %tiles.1), calls=%async_computation | async-start | bytes 786432 | tf_op jit(solution)/shard_map/all_to_all | solution.py:48
  59.4 8.4 %copy-start.4 = (s32[16]{0:T(128)S(1)}, s32[16]{0:T(128)}, u32[]{:S(2)}) copy-start(s32[16]{0:T(128)} %lengths.1) | copy-start | bytes 196
  59.4 16.0 %copy-start.2 = (f32[1536]{0:T(1024)S(1)}, f32[1536]{0:T(1024)}, u32[]{:S(2)}) copy-start(f32[1536]{0:T(1024)} %refs_4_.1) | copy-start | bytes 18436
  59.4 16.0 %copy-start.3 = (f32[512]{0:T(512)S(1)}, f32[512]{0:T(512)}, u32[]{:S(2)}) copy-start(f32[512]{0:T(512)} %refs_5_.1) | copy-start | bytes 6148
  62.6 1.3 collective-permute-start
  63.9 3.9 %collective-permute-start.1 = (bf16[2,16,264]{2,1,0:T(8,128)(2,1)S(1)}, bf16[2,16,264]{2,1,0:T(8,128)(2,1)S(1)}, u32[]{:S(2)}, u32[]{:S(2)}) collective-permute-start(bf16[2,16,264]{2,1,0:T(8,128)(2,1)S(1)} %pad_maximum_fusion.refs_0_), channel_id=1, source_target_pairs={{2,0},{7,1},{4,2},{1,3},{6,4},{3,5},{0,6},{5,7},{10,8},{15,9},{12,... | collective-permute-start | bytes 50696 | tf_op jit(solution)/shard_map/ppermute | solution.py:430
  67.8 1.2 collective-permute-start.2
  69.0 3.8 %collective-permute-start.3 = (bf16[2,16,264]{2,1,0:T(8,128)(2,1)S(1)}, bf16[2,16,264]{2,1,0:T(8,128)(2,1)S(1)}, u32[]{:S(2)}, u32[]{:S(2)}) collective-permute-start(bf16[2,16,264]{2,1,0:T(8,128)(2,1)S(1)} %collective-permute-done.1.refs_1_), channel_id=1, source_target_pairs={{2,0},{7,1},{4,2},{1,3},{6,4},{3,5},{0,6},{5,7},{10,8},{15,9},{12,... | collective-permute-start | bytes 50696 | tf_op jit(solution)/shard_map/ppermute | solution.py:431
  76.5 17.7 %all-to-all-start.1 = ((bf16[32,16,128]{2,1,0:T(8,128)(2,1)}), bf16[32,16,128]{2,1,0:T(8,128)(2,1)S(1)}, u32[]{:S(2)}, u32[]{:S(2)}) async-start(bf16[32,16,128]{2,1,0:T(8,128)(2,1)} %get-tuple-element.5), calls=%async_computation.1 | async-start | bytes 262144 | tf_op jit(solution)/shard_map/all_to_all | solution.py:48
